TPU v7x, 512 devices: a whole 4x4x16 slice. The times are simulated.
512 devices in a mesh: group: 32 (over x, y, core), tp: 16 (over z).
Axes of the slice: x: 4, y: 4, z: 16, core: 2. Of those that a mesh axis runs over, the one named last changes fastest.
Arguments:
- hidden: bfloat16 [8192, 8192], P('group', 'tp'), may hold values from -6 to 6
- w_kv: bfloat16 [8192, 2048], P('tp'), may hold values from -0.0625 to 0.0625
- prompt_lengths: int32 [8, 16], replicated, may hold values from 1 to 128, 256 in all within a row
- owner_step: int32 [8, 16], replicated, may hold values from 1 to 3
- cache: bfloat16 [1024, 128, 2048], P(('group', 'tp')), may hold values from -8 to 8
- cache_len: int32 [1024], P(('group', 'tp')), may hold values from 1 to 128
- queries: bfloat16 [1024, 8192], P('group', 'tp'), may hold values from -200 to 200
- fresh: bfloat16 [1024, 2048], P('group', 'tp'), may hold values from -10 to 10
- logits: bfloat16 [1024, 122880], P('group', 'tp'), may hold values from -300 to 300
- states: int32 [1024], P('group'), may hold values from 0 to 23
- masks: int32 [24, 4096], P(None, 'tp'), may hold values from 0 to 1073741823, as said below
Outputs:
- attended: bfloat16 [1024, 8192], P('group', 'tp')
- logprob: float32 [1024, 122880], P('group', 'tp')
Inputs may be any that keep to these rules, and one draw needn't show every extreme that they name: `prompt_lengths`: each row sums to 256; the longest prompt of every row has exactly 128 tokens. Prompt k of prefill group p goes to group p + owner_step[p, k] * 8. `masks`: every state allows at least one token in each aligned block of 7680 vocabulary entries.
All inputs are finite; a program needn't handle non-finite values.
Results may differ from a plain program's by a relative error of at most 0.02.
Values may be sent and summed in bfloat16 or wider, within the bound.
No kernel may reach another device: no remote copies, remote signals or barrier semaphores. Data moves between devices by JAX's collectives and lax.ppermute only.
A program may use at most 64 MiB of HBM per device.

v0:
```python
import math

import jax
import jax.numpy as jnp
from jax import lax
from jax.sharding import PartitionSpec as P

HEADS = 64
KVH = 8
HD = 128
MAXLEN = 128
CACHE = 128
STATES = 24


def split_up(value, dim, peers):
    shape = value.shape
    pieces = value.reshape(*shape[:dim], peers, shape[dim] // peers, *shape[dim + 1 :])
    return jnp.moveaxis(pieces, dim, 0)


def summed_on_arrival(value, axis, dim):
    peers = lax.axis_size(axis)
    pieces = lax.all_to_all(split_up(value, dim, peers), axis, 0, 0, tiled=True)
    return jnp.sum(pieces.astype(jnp.float32), axis=0)


def from_behind(block, axis, distance):
    devices = range(lax.axis_size(axis))
    route = [(i - distance, i) for i in devices if i - distance in devices]
    return lax.ppermute(block, axis, route)


def from_everyone(value, axis):
    peers = lax.axis_size(axis)
    return lax.all_to_all(
        jnp.broadcast_to(value[None], (peers, *value.shape)), axis, 0, 0, tiled=True
    )


def collected_together(value, axis):
    leaves = jax.tree.leaves(value)
    turns = sorted(range(len(leaves)), key=lambda k: -leaves[k].size)
    width = (1, *leaves[turns[0]].shape)[-1]
    lines = [
        jnp.pad(leaves[k].reshape(-1), (0, -leaves[k].size % width)).reshape(-1, width)
        for k in turns
    ]
    both, at, found = (from_everyone(jnp.concatenate(lines), axis), 0, {})
    for k, line in zip(turns, lines):
        section = both[:, at : at + len(line)].reshape(len(both), -1)
        found[k] = section[:, : leaves[k].size].reshape(-1, *leaves[k].shape)
        at += len(line)
    numbers = iter(range(len(leaves)))
    return jax.tree.map(lambda _: found[next(numbers)], value)


def combined_pairwise(pieces, combine):
    while len(jax.tree.leaves(pieces)[0]) > 1:
        pieces = jax.vmap(combine)(
            *(jax.tree.map(lambda part: part[side::2], pieces) for side in (0, 1))
        )
    return jax.tree.map(lambda part: part[0], pieces)


def joined_all(value, axis, combine):
    pieces = collected_together(value, axis)
    return combined_pairwise(pieces, combine)


def landing(slot_ids, source, turn_index, prompt_lengths, owner_step):
    chosen = owner_step[source] == turn_index
    ranking = jnp.cumsum(chosen.astype(jnp.int32)) - 1
    arrivals = jnp.sum(chosen.astype(jnp.int32))
    matched = chosen[None, :] & (ranking[None, :] == slot_ids[:, None])
    lengths = prompt_lengths[source]
    starts = jnp.cumsum(lengths) - lengths
    first_row = jnp.sum(jnp.where(matched, starts[None, :], 0), axis=1)
    prompt_len = jnp.sum(jnp.where(matched, lengths[None, :], 0), axis=1)
    landed = (slot_ids < arrivals) & (turn_index >= 1)
    return (landed, first_row, prompt_len)


def attend(query_rows, merged, alive_len, fresh_rows):
    row_count = merged.shape[0]
    group_size = HEADS // KVH
    key_rows = merged[:, :, : KVH * HD].reshape(row_count, CACHE, KVH, HD)
    value_rows = merged[:, :, KVH * HD :].reshape(row_count, CACHE, KVH, HD)
    queries = query_rows.reshape(row_count, KVH, group_size, HD)
    own_key = fresh_rows[:, : KVH * HD].reshape(row_count, KVH, HD)
    own_value = fresh_rows[:, KVH * HD :].reshape(row_count, KVH, HD)
    scaling = 1.0 / math.sqrt(HD)
    scores = (
        jnp.einsum("rkgd,rtkd->rkgt", queries, key_rows, preferred_element_type=jnp.float32)
        * scaling
    )
    own_score = (
        jnp.einsum("rkgd,rkd->rkg", queries, own_key, preferred_element_type=jnp.float32) * scaling
    )
    positions = jnp.arange(CACHE, dtype=jnp.int32)
    alive_mask = (positions[None, :] < alive_len[:, None])[:, None, None, :]
    highest = jnp.maximum(jnp.max(jnp.where(alive_mask, scores, -jnp.inf), axis=3), own_score)
    exponent = jnp.where(alive_mask, jnp.exp(scores - highest[..., None]), 0.0)
    own_exponent = jnp.exp(own_score - highest)
    denominator = jnp.sum(exponent, axis=3) + own_exponent
    weights = (exponent / denominator[..., None]).astype(jnp.bfloat16)
    own_weight = (own_exponent / denominator).astype(jnp.bfloat16)
    attended = jnp.einsum(
        "rkgt,rtkd->rkgd", weights, value_rows, preferred_element_type=jnp.float32
    )
    attended = (
        attended
        + own_weight.astype(jnp.float32)[..., None] * own_value.astype(jnp.float32)[:, :, None, :]
    )
    return attended.reshape(row_count, HEADS * HD).astype(jnp.bfloat16)


def merge_terms(first, second):
    highest = jnp.maximum(first[0], second[0])
    summed = first[1] * jnp.exp(first[0] - highest) + second[1] * jnp.exp(second[0] - highest)
    return (highest, summed)


def per_device(
    hidden,
    w_kv,
    prompt_lengths,
    owner_step,
    cache,
    cache_len,
    queries,
    fresh,
    logits,
    states,
    masks,
):
    tensor_size = lax.axis_size("tp")
    groups = lax.axis_size("group")
    prefill = groups // 4
    group_index = lax.axis_index("group")
    column = lax.axis_index("tp")
    is_prefill = group_index < prefill
    source = group_index % prefill
    turn_index = group_index // prefill
    token_count = hidden.shape[0]
    kv_width = w_kv.shape[1]
    own_count = cache.shape[0]
    prompt_count = prompt_lengths.shape[1]
    own_slots = jnp.arange(own_count, dtype=jnp.int32) * tensor_size + column
    landed, first_row, prompt_len = landing(
        own_slots, source, turn_index, prompt_lengths, owner_step
    )

    def compute():
        return lax.dot_general(
            w_kv, hidden, (((0,), (1,)), ((), ())), preferred_element_type=jnp.float32
        )

    kv_piece = summed_on_arrival(
        lax.cond(
            is_prefill,
            compute,
            lambda: jnp.zeros(
                (kv_width // tensor_size * lax.axis_size("tp"), token_count), jnp.float32
            ),
        ).astype(jnp.bfloat16),
        "tp",
        0,
    ).astype(jnp.bfloat16)
    arrived = [from_behind(kv_piece, "group", prefill * step_index) for step_index in (1, 2, 3)]
    incoming = jnp.where(
        turn_index == 1, arrived[0], jnp.where(turn_index == 2, arrived[1], arrived[2])
    )
    padded = jnp.pad(incoming, ((0, 0), (0, MAXLEN)))
    owned = min(own_count, -(-prompt_count // tensor_size))
    owner_ids = jnp.arange(tensor_size, dtype=jnp.int32)
    place_ids = jnp.arange(owned, dtype=jnp.int32)
    all_slots = (place_ids[None, :] * tensor_size + owner_ids[:, None]).reshape(-1)
    all_first = landing(all_slots, source, turn_index, prompt_lengths, owner_step)[1]
    take_index = (all_first[:, None] + jnp.arange(MAXLEN, dtype=jnp.int32)[None, :]).reshape(-1)
    outgoing = jnp.take(padded, take_index, axis=1)
    received = lax.all_to_all(outgoing, "tp", split_axis=1, concat_axis=0, tiled=True)
    handed = jnp.transpose(received.reshape(kv_width, owned, MAXLEN), (1, 2, 0))
    handed = jnp.pad(handed, ((0, own_count - owned), (0, 0), (0, 0)))
    front = jnp.where(landed[:, None, None], handed, cache)
    merged = jnp.concatenate([front, cache[:, MAXLEN:]], axis=1)
    alive_len = jnp.where(landed, prompt_len, cache_len)
    mine_queries, mine_fresh = (
        lax.all_to_all(queries, "tp", split_axis=0, concat_axis=1, tiled=True),
        lax.all_to_all(fresh, "tp", split_axis=0, concat_axis=1, tiled=True),
    )
    attended = attend(mine_queries, merged, alive_len, mine_fresh)
    attended = lax.all_to_all(attended, "tp", split_axis=1, concat_axis=0, tiled=True)
    onehot = states[:, None] == jnp.arange(STATES, dtype=jnp.int32)[None, :]
    packed = jnp.sum(jnp.where(onehot[:, :, None], masks[None, :, :], 0), axis=1)
    shifts = jnp.arange(30, dtype=jnp.int32)
    bit_flags = jnp.bitwise_and(jnp.right_shift(packed[:, :, None], shifts[None, None, :]), 1)
    permitted = bit_flags.reshape(packed.shape[0], logits.shape[1]) == 1
    values = logits.astype(jnp.float32)
    local_peak = jnp.max(jnp.where(permitted, values, -jnp.inf), axis=1)
    local_terms = jnp.sum(jnp.where(permitted, jnp.exp(values - local_peak[:, None]), 0.0), axis=1)
    highest, denominator = joined_all((local_peak, local_terms), "tp", merge_terms)
    normalizer = highest + jnp.log(denominator)
    logprob = jnp.where(permitted, values - normalizer[:, None], 0.0)
    return (attended, logprob)


def solution(mesh):
    in_specs = (
        P("group", "tp"),
        P("tp", None),
        P(),
        P(),
        P(("group", "tp"), None, None),
        P(("group", "tp")),
        P("group", "tp"),
        P("group", "tp"),
        P("group", "tp"),
        P("group"),
        P(None, "tp"),
    )
    out_specs = (P("group", "tp"), P("group", "tp"))
    return jax.shard_map(
        per_device, mesh=mesh, in_specs=in_specs, out_specs=out_specs, check_vma=False
    )
```

profile of v0, /device:TPU:24, one launch (start us, length us, event | category | flops | bytes accessed | tf_op | source)
XLA Modules:
  0.0 181.3 jit_solution(15258341795473198941)
XLA Ops:
  0.6 3.4 %conditional.1 = (bf16[2048,256]{1,0:T(8,128)(2,1)}) conditional(s32[]{:T(128)} %convert_element_type.52, () %tuple.14, (bf16[512,2048]{1,0:T(8,128)(2,1)}, bf16[256,512]{1,0:T(8,128)(2,1)}) %tuple.15), branch_computations={%region_5.6_spmd, %region_6.7_spmd} | conditional | flops 536870912 | bytes 3407880 | solution.py:160
  0.7 3.3 %fusion.25 = bf16[2048,256]{1,0:T(8,128)(2,1)} fusion(bf16[512,2048]{1,0:T(8,128)(2,1)} %get-tuple-element.13, bf16[256,512]{1,0:T(8,128)(2,1)} %get-tuple-element.14), kind=kOutput, calls=%fused_computation.68 | convolution fusion | flops 536870912 | bytes 3407872 | tf_op jit(solution)/shard_map/cond/branch_1_fun/dot_general | solution.py:155
  4.0 15.3 %all-to-all-start = ((bf16[16,128,256]{2,1,0:T(8,128)(2,1)}), bf16[16,128,256]{2,1,0:T(8,128)(2,1)S(1)}, u32[]{:S(2)}, u32[]{:S(2)}) async-start(bf16[16,128,256]{2,1,0:T(8,128)(2,1)} %bitcast.4), calls=%async_computation | async-start | bytes 2097152 | tf_op jit(solution)/shard_map/all_to_all | solution.py:24
  19.4 0.2 select_reduce_fusion
  19.7 3.0 %shift_right_arithmetic.20 = s32[32,256,30]{2,1,0:T(8,128)} broadcast(s32[32,256]{1,0:T(8,128)S(1)} %select_reduce_fusion), dimensions={0,1} | broadcast | bytes 1015808 | tf_op jit(solution)/shard_map/shift_right_arithmetic | solution.py:197
  22.7 3.9 %shift_right_arithmetic.21 = s32[32,7680]{1,0:T(8,128)S(1)} reshape(s32[32,256,30]{2,1,0:T(8,128)} %shift_right_arithmetic.20) | data formatting | bytes 1966080 | tf_op jit(solution)/shard_map/shift_right_arithmetic | solution.py:197
  26.7 0.1 shift_right_arithmetic.23
  26.8 1.4 constant_dynamic-slice_fusion
  28.2 0.2 reduce-window_1_clone.1
  28.4 0.7 compare_bitcast_fusion
  29.1 0.1 copy.37
  29.3 0.4 fusion.1
  29.7 0.4 fusion.4
  30.1 0.1 add_reduce_fusion
  30.2 0.1 select_reduce_fusion.2
  30.4 0.1 compare_and_fusion
  30.6 38.7 %all-to-all-done = bf16[16,128,256]{2,1,0:T(8,128)(2,1)S(1)} async-done(((bf16[16,128,256]{2,1,0:T(8,128)(2,1)}), bf16[16,128,256]{2,1,0:T(8,128)(2,1)S(1)}, u32[]{:S(2)}, u32[]{:S(2)}) %all-to-all-start) | async-done | bytes 1048608 | tf_op jit(solution)/shard_map/all_to_all | solution.py:24
  69.3 0.6 broadcast_in_dim.140
  69.9 7.9 %all-to-all-start.5 = ((f32[16,2,32]{2,1,0:T(2,128)}), f32[16,2,32]{2,1,0:T(2,128)S(1)}, u32[]{:S(2)}, u32[]{:S(2)}) async-start(f32[16,2,32]{2,1,0:T(2,128)} %broadcast_in_dim.140), calls=%async_computation.5 | async-start | bytes 32768 | tf_op jit(solution)/shard_map/all_to_all | solution.py:36
  77.8 0.1 reduce_sum.69
  78.0 0.1 copy.38
  78.1 1.3 collective-permute-start
  79.4 4.4 %collective-permute-start.1 = (bf16[128,256]{0,1:T(8,128)(2,1)S(1)}, bf16[128,256]{0,1:T(8,128)(2,1)S(1)}, u32[]{:S(2)}, u32[]{:S(2)}) collective-permute-start(bf16[128,256]{0,1:T(8,128)(2,1)S(1)} %copy.38), channel_id=1, source_target_pairs={{0,256},{16,272},{32,288},{48,304},{64,320},{80,336},{96,352},{112... | collective-permute-start | bytes 196616 | tf_op jit(solution)/shard_map/ppermute | solution.py:31
  83.8 1.3 collective-permute-start.2
  85.1 0.2 fusion.15
  85.3 0.7 copy.42
  86.0 0.6 all_to_all.57
  86.6 3.7 %all-to-all-done.5 = f32[16,2,32]{2,1,0:T(2,128)S(1)} async-done(((f32[16,2,32]{2,1,0:T(2,128)}), f32[16,2,32]{2,1,0:T(2,128)S(1)}, u32[]{:S(2)}, u32[]{:S(2)}) %all-to-all-start.5) | async-done | bytes 4128 | tf_op jit(solution)/shard_map/all_to_all | solution.py:36
  90.3 8.3 %all-to-all-start.3 = ((bf16[16,2,128]{2,1,0:T(2,128)(2,1)}), bf16[16,2,128]{2,1,0:T(2,128)(2,1)S(1)}, u32[]{:S(2)}, u32[]{:S(2)}) async-start(bf16[16,2,128]{2,1,0:T(2,128)(2,1)} %bitcast.14), calls=%async_computation.3 | async-start | bytes 16384 | tf_op jit(solution)/shard_map/all_to_all | solution.py:190
  98.7 6.2 %gather_fusion = bf16[2048,128]{1,0:T(8,128)(2,1)S(1)} fusion(bf16[128,384]{0,1:T(8,128)(2,1)S(1)} %pad.8, s32[2048]{0:T(1024)S(1)} %broadcast_clamp_fusion), kind=kCustom, calls=%fused_computation | custom fusion | bytes 1056768 | tf_op jit(solution)/shard_map/jit(_take)/gather | solution.py:181
  104.9 6.1 %all-to-all-done.3 = bf16[16,2,128]{2,1,0:T(2,128)(2,1)S(1)} async-done(((bf16[16,2,128]{2,1,0:T(2,128)(2,1)}), bf16[16,2,128]{2,1,0:T(2,128)(2,1)S(1)}, u32[]{:S(2)}, u32[]{:S(2)}) %all-to-all-start.3) | async-done | bytes 8224 | tf_op jit(solution)/shard_map/all_to_all | solution.py:190
  111.1 5.9 %all-to-all-start.2 = ((bf16[16,2,512]{2,1,0:T(2,128)(2,1)}), bf16[16,2,512]{2,1,0:T(2,128)(2,1)S(1)}, u32[]{:S(2)}, u32[]{:S(2)}) async-start(bf16[16,2,512]{2,1,0:T(2,128)(2,1)} %all_to_all.57), calls=%async_computation.2 | async-start | bytes 65536 | tf_op jit(solution)/shard_map/all_to_all | solution.py:189
  117.0 1.1 broadcast_select_fusion
  118.1 11.5 %all-to-all-done.2 = bf16[16,2,512]{2,1,0:T(2,128)(2,1)S(1)} async-done(((bf16[16,2,512]{2,1,0:T(2,128)(2,1)}), bf16[16,2,512]{2,1,0:T(2,128)(2,1)S(1)}, u32[]{:S(2)}, u32[]{:S(2)}) %all-to-all-start.2) | async-done | bytes 32800 | tf_op jit(solution)/shard_map/all_to_all | solution.py:189
  129.6 3.6 %all-to-all-start.1 = ((bf16[128,16,128]{0,2,1:T(8,128)(2,1)}), bf16[128,16,128]{0,2,1:T(8,128)(2,1)S(1)}, u32[]{:S(2)}, u32[]{:S(2)}) async-start(bf16[128,16,128]{0,2,1:T(8,128)(2,1)} %broadcast_select_fusion), calls=%async_computation.1 | async-start | bytes 1048576 | tf_op jit(solution)/shard_map/all_to_all | solution.py:182
  133.2 0.7 fusion.21
  134.4 0.1 fusion.26
  134.5 24.0 %all-to-all-done.1 = bf16[128,16,128]{0,2,1:T(8,128)(2,1)S(1)} async-done(((bf16[128,16,128]{0,2,1:T(8,128)(2,1)}), bf16[128,16,128]{0,2,1:T(8,128)(2,1)S(1)}, u32[]{:S(2)}, u32[]{:S(2)}) %all-to-all-start.1) | async-done | bytes 524320 | tf_op jit(solution)/shard_map/all_to_all | solution.py:182
  158.6 0.3 copy.41
  158.8 0.2 pad_select_fusion
  159.1 0.3 select_reduce_fusion.1
  159.4 0.2 bitcast_reduce_fusion
  159.6 0.4 fusion
  160.1 0.6 copy.46
  160.7 7.3 %all-to-all-start.4 = ((bf16[2,16,512]{2,0,1:T(2,128)(2,1)}), bf16[2,16,512]{2,0,1:T(2,128)(2,1)S(1)}, u32[]{:S(2)}, u32[]{:S(2)}) async-start(bf16[2,16,512]{2,0,1:T(2,128)(2,1)} %copy.46), calls=%async_computation.4 | async-start | bytes 65536 | tf_op jit(solution)/shard_map/all_to_all | solution.py:193
  168.1 1.2 fusion.5
  169.2 11.4 %all-to-all-done.4 = bf16[2,16,512]{2,0,1:T(2,128)(2,1)S(1)} async-done(((bf16[2,16,512]{2,0,1:T(2,128)(2,1)}), bf16[2,16,512]{2,0,1:T(2,128)(2,1)S(1)}, u32[]{:S(2)}, u32[]{:S(2)}) %all-to-all-start.4) | async-done | bytes 32800 | tf_op jit(solution)/shard_map/all_to_all | solution.py:193
  180.7 0.6 all_to_all.66
  (53 shorter events, 0.9 us)
Async XLA Ops:
  4.0 15.4 %copy-start.4 = (s32[32]{0:T(128)S(1)}, s32[32]{0:T(128)}, u32[]{:S(2)}) copy-start(s32[32]{0:T(128)} %param.22) | copy-start | bytes 388
  4.0 15.4 %copy-start.3 = (s32[24,256]{1,0:T(8,128)S(1)}, s32[24,256]{1,0:T(8,128)}, u32[]{:S(2)}) copy-start(s32[24,256]{1,0:T(8,128)} %param.23) | copy-start | bytes 73732
  4.0 65.3 %all-to-all-start = ((bf16[16,128,256]{2,1,0:T(8,128)(2,1)}), bf16[16,128,256]{2,1,0:T(8,128)(2,1)S(1)}, u32[]{:S(2)}, u32[]{:S(2)}) async-start(bf16[16,128,256]{2,1,0:T(8,128)(2,1)} %bitcast.4), calls=%async_computation | async-start | bytes 2097152 | tf_op jit(solution)/shard_map/all_to_all | solution.py:24
  22.7 6.5 %copy-start = (bf16[32,7680]{1,0:T(8,128)(2,1)S(1)}, bf16[32,7680]{1,0:T(8,128)(2,1)}, u32[]{:S(2)}) copy-start(bf16[32,7680]{1,0:T(8,128)(2,1)} %param.21) | copy-start | bytes 1474564
  29.7 55.7 %copy-start.1 = (bf16[2,128,2048]{2,1,0:T(8,128)(2,1)S(1)}, bf16[2,128,2048]{2,1,0:T(8,128)(2,1)}, u32[]{:S(2)}) copy-start(bf16[2,128,2048]{2,1,0:T(8,128)(2,1)} %param.17) | copy-start | bytes 3145732
  29.7 56.3 %copy-start.2 = (bf16[32,512]{1,0:T(8,128)(2,1)S(1)}, bf16[32,512]{1,0:T(8,128)(2,1)}, u32[]{:S(2)}) copy-start(bf16[32,512]{1,0:T(8,128)(2,1)} %param.19) | copy-start | bytes 98308
  69.9 20.4 %all-to-all-start.5 = ((f32[16,2,32]{2,1,0:T(2,128)}), f32[16,2,32]{2,1,0:T(2,128)S(1)}, u32[]{:S(2)}, u32[]{:S(2)}) async-start(f32[16,2,32]{2,1,0:T(2,128)} %broadcast_in_dim.140), calls=%async_computation.5 | async-start | bytes 32768 | tf_op jit(solution)/shard_map/all_to_all | solution.py:36
  78.1 20.6 %collective-permute-start = (bf16[128,256]{0,1:T(8,128)(2,1)S(1)}, bf16[128,256]{0,1:T(8,128)(2,1)S(1)}, u32[]{:S(2)}, u32[]{:S(2)}) collective-permute-start(bf16[128,256]{0,1:T(8,128)(2,1)S(1)} %copy.38), channel_id=1, source_target_pairs={{0,128},{16,144},{32,160},{48,176},{64,192},{80,208},{96,224},{112... | collective-permute-start | bytes 196616 | tf_op jit(solution)/shard_map/ppermute | solution.py:31
  79.4 19.3 %collective-permute-start.1 = (bf16[128,256]{0,1:T(8,128)(2,1)S(1)}, bf16[128,256]{0,1:T(8,128)(2,1)S(1)}, u32[]{:S(2)}, u32[]{:S(2)}) collective-permute-start(bf16[128,256]{0,1:T(8,128)(2,1)S(1)} %copy.38), channel_id=1, source_target_pairs={{0,256},{16,272},{32,288},{48,304},{64,320},{80,336},{96,352},{112... | collective-permute-start | bytes 196616 | tf_op jit(solution)/shard_map/ppermute | solution.py:31
  83.8 14.9 %collective-permute-start.2 = (bf16[128,256]{0,1:T(8,128)(2,1)S(1)}, bf16[128,256]{0,1:T(8,128)(2,1)S(1)}, u32[]{:S(2)}, u32[]{:S(2)}) collective-permute-start(bf16[128,256]{0,1:T(8,128)(2,1)S(1)} %copy.38), channel_id=1, source_target_pairs={{0,384},{16,400},{32,416},{48,432},{64,448},{80,464},{96,480},{112... | collective-permute-start | bytes 196616 | tf_op jit(solution)/shard_map/ppermute | solution.py:31
  90.3 20.8 %all-to-all-start.3 = ((bf16[16,2,128]{2,1,0:T(2,128)(2,1)}), bf16[16,2,128]{2,1,0:T(2,128)(2,1)S(1)}, u32[]{:S(2)}, u32[]{:S(2)}) async-start(bf16[16,2,128]{2,1,0:T(2,128)(2,1)} %bitcast.14), calls=%async_computation.3 | async-start | bytes 16384 | tf_op jit(solution)/shard_map/all_to_all | solution.py:190
  104.9 28.3 %copy-start.5 = (s32[2]{0:T(128)S(1)}, s32[2]{0:T(128)}, u32[]{:S(2)}) copy-start(s32[2]{0:T(128)} %param.18) | copy-start | bytes 28
  111.1 18.5 %all-to-all-start.2 = ((bf16[16,2,512]{2,1,0:T(2,128)(2,1)}), bf16[16,2,512]{2,1,0:T(2,128)(2,1)S(1)}, u32[]{:S(2)}, u32[]{:S(2)}) async-start(bf16[16,2,512]{2,1,0:T(2,128)(2,1)} %all_to_all.57), calls=%async_computation.2 | async-start | bytes 65536 | tf_op jit(solution)/shard_map/all_to_all | solution.py:189
  129.6 28.9 %all-to-all-start.1 = ((bf16[128,16,128]{0,2,1:T(8,128)(2,1)}), bf16[128,16,128]{0,2,1:T(8,128)(2,1)S(1)}, u32[]{:S(2)}, u32[]{:S(2)}) async-start(bf16[128,16,128]{0,2,1:T(8,128)(2,1)} %broadcast_select_fusion), calls=%async_computation.1 | async-start | bytes 1048576 | tf_op jit(solution)/shard_map/all_to_all | solution.py:182
  160.7 19.9 %all-to-all-start.4 = ((bf16[2,16,512]{2,0,1:T(2,128)(2,1)}), bf16[2,16,512]{2,0,1:T(2,128)(2,1)S(1)}, u32[]{:S(2)}, u32[]{:S(2)}) async-start(bf16[2,16,512]{2,0,1:T(2,128)(2,1)} %copy.46), calls=%async_computation.4 | async-start | bytes 65536 | tf_op jit(solution)/shard_map/all_to_all | solution.py:193
where the time goes:
time: 182 us; the launch traced here: 181 us
  waiting for transfers between devices  95.5 us (52%)
  starting transfers between devices  55.4 us (30%)
  local copies, waits for them, and re-layouts  17.4 us (10%)
  other arithmetic  7.76 us (4%)
  matrix products  4.2 us (2%)
    all_to_all x1, waiting for transfers between devices, summed_on_arrival(): pieces = lax.all_to_all(split_up(value, dim, peers), axis, 0, 0, tiled=True)  38.7 us
    all_to_all x1, waiting for transfers between devices, per_device(): lax.all_to_all(outgoing, 'tp', split_axis=1, concat_axis=0, tiled=True)  24 us
    all_to_all x1, starting transfers between devices, summed_on_arrival(): pieces = lax.all_to_all(split_up(value, dim, peers), axis, 0, 0, tiled=True)  15.3 us
    all_to_all x1, waiting for transfers between devices, per_device(): lax.all_to_all(queries, 'tp', split_axis=0, concat_axis=1, tiled=True)  11.5 us
    all_to_all x1, waiting for transfers between devices, per_device(): lax.all_to_all(attended, 'tp', split_axis=1, concat_axis=0, tiled=True)  11.4 us
    all_to_all x1, starting transfers between devices, per_device(): lax.all_to_all(fresh, 'tp', split_axis=0, concat_axis=1, tiled=True)  8.34 us
    all_to_all x1, starting transfers between devices, from_everyone(): lax.all_to_all(jnp.broadcast_to(value[None], (peers, *value.shape)), axis...  7.92 us
    all_to_all x1, starting transfers between devices, per_device(): lax.all_to_all(attended, 'tp', split_axis=1, concat_axis=0, tiled=True)  7.31 us
  transfers between devices with their start and end apart: 9, of which 6 were waited for; matrix products, arithmetic and copies ran while one was open for 12% of the time, Pallas kernels for 0%

commit v1 on v0

v1 whole, which is shorter than its diff:
```python
import math

import jax
import jax.numpy as jnp
from jax import lax
from jax.experimental import pallas as pl
from jax.experimental.pallas import tpu as pltpu
from jax.sharding import Mesh, PartitionSpec as P

HEADS = 64
KVH = 8
HD = 128
STATES = 24
BITS = 30
BLK = 1920
SCALE = 1.0 / math.sqrt(HD)
F32 = jnp.float32
BF16 = jnp.bfloat16
I32 = jnp.int32
TP = ("zh", "zl")


def iota(shape, dim):
    return lax.broadcasted_iota(I32, shape, dim)


def one_hot(target, width):
    rows = target.shape[0]
    return (iota((rows, width), 1) == target).astype(F32).astype(BF16)


def pick(target, table):
    return jnp.dot(one_hot(target, table.shape[0]), table, preferred_element_type=F32)


def call(kernel, out, name, memory=None):
    return pl.pallas_call(kernel, out_shape=out, name=name)


def prompts_of(lengths, owners, source, turn):
    count = lengths.shape[1]
    here = iota(lengths.shape, 0) == source
    length = jnp.sum(jnp.where(here, lengths, 0).astype(F32), axis=0, keepdims=True)
    owner = jnp.sum(jnp.where(here, owners, 0).astype(F32), axis=0, keepdims=True)
    chosen = ((owner == turn.astype(F32)) & (turn >= 1)).astype(F32)
    row, lane = iota((count, count), 0), iota((count, count), 1)

    def before(values):
        column = jnp.sum(jnp.where(row == lane, values, 0.0), axis=1, keepdims=True)
        return jnp.sum(jnp.where(row < lane, column, 0.0), axis=0, keepdims=True)

    return chosen, before(chosen), before(length), length


def landing(slot, prompts):
    chosen, rank, start, length = prompts
    matched = jnp.where(rank == slot.astype(F32), chosen, 0.0)
    total = lambda values: jnp.sum(matched * values, axis=1, keepdims=True)
    return jnp.sum(matched, axis=1, keepdims=True), total(start), total(length)


def pack_queries(queries, fresh, out):
    table = jnp.concatenate(
        [queries[:, HD * i : HD * (i + 1)] for i in range(4)] + [fresh[...]], axis=0
    )
    row = iota((256, 1), 0)
    dest, k = row // 16, row % 16
    target = jnp.where(
        k < 8,
        (k % 4) * 32 + 2 * dest + k // 4,
        jnp.where(k < 10, 128 + 2 * dest + k - 8, 160),
    )
    out[...] = pick(target, table).astype(BF16).reshape(16, 16, HD)


def project(own, first, second, third, weight, out):
    turn = lax.axis_index("x")
    tokens = jnp.where(turn == 0, own[0:64, :], first[...] + second[...] + third[...])
    full = jnp.dot(tokens, weight[...], preferred_element_type=F32).astype(BF16)
    for c in range(16):
        block = c // 2 + (c % 2) * KVH
        out[c] = full[:, HD * block : HD * (block + 1)]


def reduce_blocks(pieces, out):
    total = pieces[0].astype(F32)
    for c in range(1, 16):
        total = total + pieces[c].astype(F32)
    total = total.astype(BF16)
    for d in range(8):
        out[d] = total


def grammar(logits, key, masks, masked, terms):
    lane = iota((STATES, HD), 1)
    blocks = []
    for half in range(2):
        words = masks[:, HD * half : HD * (half + 1)]
        turned = pltpu.roll(words, 64, 1)
        for x, y in ((words, turned), (turned, words)):
            byte = lambda v, j: jnp.bitwise_and(jnp.right_shift(v, 8 * j), 255)
            blocks.append(
                jnp.concatenate(
                    [
                        jnp.where(lane < 64, byte(x, 0), byte(y, 1)),
                        jnp.where(lane < 64, byte(x, 2), byte(y, 3)),
                    ],
                    axis=1,
                )
            )
    table = jnp.concatenate(blocks, axis=0).astype(F32).astype(BF16)
    chosen = pick(key[...], table).astype(BF16)
    column = iota((1, BLK), 1)
    word = jnp.right_shift(column * 34953, 20)
    bit = column - word * BITS
    wanted = jnp.right_shift(bit, 3) * 64 + word
    flag = jnp.left_shift(jnp.ones_like(bit), jnp.bitwise_and(bit, 7))
    spread = (iota((256, BLK), 0) == wanted).astype(F32).astype(BF16)
    peak = None
    kept = []
    for b in range(4):
        value = jnp.dot(
            chosen[32 * b : 32 * (b + 1)], spread, preferred_element_type=F32
        ).astype(I32)
        section = logits[:, BLK * b : BLK * (b + 1)].astype(F32)
        section = jnp.where(jnp.bitwise_and(value, flag) != 0, section, -jnp.inf)
        kept.append(section)
        masked[:, BLK * b : BLK * (b + 1)] = section.astype(BF16)
        top = jnp.max(section, axis=1, keepdims=True)
        peak = top if peak is None else jnp.maximum(peak, top)
    total = sum(jnp.sum(jnp.exp(section - peak), axis=1, keepdims=True) for section in kept)
    high = total.astype(BF16).astype(F32)
    middle = (total - high).astype(BF16).astype(F32)
    low = total - high - middle
    row, lane = iota((32, HD), 0), iota((32, HD), 1)
    spot = lane - row
    line = jnp.where(
        spot == 0, peak, jnp.where(spot == 32, high, jnp.where(spot == 64, middle, low))
    )
    line = jnp.where(jnp.bitwise_and(spot, 31) == 0, line, 0.0)
    terms[...] = jnp.broadcast_to(jnp.sum(line, axis=0, keepdims=True), (16, HD)).astype(BF16)


def softmax(score, own, alive):
    highest = jnp.maximum(
        jnp.max(jnp.where(alive, score, -jnp.inf), axis=1, keepdims=True), own
    )
    exponent = jnp.where(alive, jnp.exp(score - highest), 0.0)
    own_exponent = jnp.exp(own - highest)
    total = jnp.sum(exponent, axis=1, keepdims=True) + own_exponent
    own_weight = (own_exponent / total).astype(BF16).astype(F32)
    return (exponent / total).astype(BF16), own_weight


def transposed(a, b):
    return lax.dot_general(a, b, (((1,), (1,)), ((), ())), preferred_element_type=F32)


def attend_cached(cache_len, received, cache, terms, lengths, owners, out):
    column = lax.axis_index("zh") * 2 + lax.axis_index("zl")
    prompts = prompts_of(
        lengths[...], owners[...], lax.axis_index("c8"), lax.axis_index("x")
    )
    landed = landing(jnp.full((1, 1), column, I32), prompts)[0]
    table = received[...].reshape(256, HD)
    row = iota((256, 1), 0)
    device, k = row // 16, row % 16
    second = (k >= 4) & (k < 8)
    fresh_row = (device // 2) * 16 + jnp.where(second, 9, 8)
    own_key = pick(fresh_row, table)
    own_value = pick(fresh_row + KVH * 16, table)
    own = jnp.sum(table.astype(F32) * own_key, axis=1, keepdims=True) * SCALE
    second32 = second[0:32]
    scores = []
    for h in range(KVH):
        rows = table[32 * h : 32 * (h + 1)]
        both = [transposed(rows, cache[r, :, HD * h : HD * (h + 1)]) for r in range(2)]
        scores.append(jnp.where(second32, both[1], both[0]))
    score = jnp.concatenate(scores, axis=0) * SCALE
    alive = iota((256, HD), 1) < jnp.where(second, cache_len[1], cache_len[0])
    weight, own_weight = softmax(score, own, alive)
    values = []
    for h in range(KVH):
        rows = weight[32 * h : 32 * (h + 1)]
        at = HD * (KVH + h)
        both = [
            jnp.dot(rows, cache[r, :, at : at + HD], preferred_element_type=F32)
            for r in range(2)
        ]
        values.append(jnp.where(second32, both[1], both[0]))
    result = jnp.concatenate(values, axis=0) + own_weight * own_value
    arrived = jnp.broadcast_to(landed > 0.5, (256, 1))
    result = jnp.where(arrived & (k == 0), own_key, result)
    result = jnp.where(arrived & (k == 1), own_value, result)
    result = jnp.where(k == 8, terms[0:1, :].astype(F32), result)
    out[...] = result.astype(BF16).reshape(16, 16, HD)


def finish_logprob(masked, received, out):
    lines = received[:, 8, :].astype(F32)
    take = lambda k: lines[:, 32 * k : 32 * (k + 1)]
    peak, total = take(0), take(1) + take(2) + take(3)
    highest = jnp.max(peak, axis=0, keepdims=True)
    total = jnp.sum(total * jnp.exp(peak - highest), axis=0, keepdims=True)
    normalizer = highest + jnp.log(total)
    row, lane = iota((32, 32), 0), iota((32, 32), 1)
    normalizer = jnp.sum(jnp.where(row == lane, normalizer, 0.0), axis=1, keepdims=True)
    values = masked[...].astype(F32)
    out[...] = jnp.where(values == -jnp.inf, 0.0, values - normalizer)


def attend_landed(blocks, queries, received, lengths, owners, out):
    prompts = prompts_of(
        lengths[...], owners[...], lax.axis_index("c8"), lax.axis_index("x")
    )
    row = iota((128, 1), 0)
    head, request = row // 32, row % 32
    landed, start, length = landing((request % 2) * 16 + request // 2, prompts)
    keys = jnp.concatenate([blocks[2 * x] for x in range(4)], axis=0)
    values = jnp.concatenate([blocks[2 * x + 1] for x in range(4)], axis=0)
    query = jnp.concatenate([queries[:, HD * i : HD * (i + 1)] for i in range(4)], axis=0)
    table = received[...].reshape(256, HD)
    slot = (request // 2) * 16
    own_key = pick(slot, table)
    own_value = pick(slot + 1, table)
    cached = pick(slot + (request % 2) * 4 + head, table)
    own = jnp.sum(query.astype(F32) * own_key, axis=1, keepdims=True) * SCALE
    score = transposed(query, keys) * SCALE
    position = iota((128, 256), 1).astype(F32)
    alive = (position >= start) & (position < start + length)
    weight, own_weight = softmax(score, own, alive)
    result = jnp.dot(weight, values, preferred_element_type=F32) + own_weight * own_value
    result = jnp.where(landed > 0.5, result, cached).astype(BF16)
    for i in range(4):
        out[:, HD * i : HD * (i + 1)] = result[32 * i : 32 * (i + 1)]


def exchanged(slots, axis):
    return lax.all_to_all(slots, axis, 0, 0, tiled=True)


def per_device(
    hidden,
    w_kv,
    prompt_lengths,
    owner_step,
    cache,
    cache_len,
    queries,
    fresh,
    logits,
    states,
    masks,
):
    shape = jax.ShapeDtypeStruct
    smem = pl.BlockSpec(memory_space=pltpu.SMEM)
    vmem = pl.BlockSpec(memory_space=pltpu.VMEM)
    shares = [
        lax.ppermute(hidden[64 * k : 64 * (k + 1)], "x", [(0, k)]) for k in (1, 2, 3)
    ]
    asked = pl.pallas_call(pack_queries, out_shape=shape((16, 16, HD), BF16), name="pack")(
        queries, fresh
    )
    asked = exchanged(asked, TP)
    projected = pl.pallas_call(
        project, out_shape=shape((16, 64, HD), BF16), name="project"
    )(hidden[0:64], *shares, w_kv)
    pieces = exchanged(projected, TP)
    key = (states[None, :] + STATES * jnp.arange(4, dtype=I32)[:, None]).reshape(128, 1)
    masked, terms = pl.pallas_call(
        grammar,
        out_shape=(shape(logits.shape, BF16), shape((16, HD), BF16)),
        name="grammar",
    )(logits, key, masks)
    answers = pl.pallas_call(
        attend_cached,
        out_shape=shape((16, 16, HD), BF16),
        in_specs=[smem] + [vmem] * 5,
        name="cached",
    )(cache_len, asked, cache, terms, prompt_lengths, owner_step)
    answers = exchanged(answers, TP)
    blocks = pl.pallas_call(
        reduce_blocks, out_shape=shape((8, 64, HD), BF16), name="reduce"
    )(pieces)
    blocks = exchanged(blocks, ("x", "zl"))
    logprob = pl.pallas_call(
        finish_logprob, out_shape=shape(logits.shape, F32), name="logprob"
    )(masked, answers)
    attended = pl.pallas_call(
        attend_landed, out_shape=shape(queries.shape, BF16), name="landed"
    )(blocks, queries, answers, prompt_lengths, owner_step)
    return attended, logprob


def solution(mesh):
    groups, columns = mesh.shape["group"], mesh.shape["tp"]
    finer = Mesh(
        mesh.devices.reshape(4, groups // 4, columns // 2, 2), ("x", "c8", "zh", "zl")
    )
    group = ("x", "c8")
    in_specs = (
        P(group, TP),
        P(TP, None),
        P(),
        P(),
        P(group + TP, None, None),
        P(group + TP),
        P(group, TP),
        P(group, TP),
        P(group, TP),
        P(group),
        P(None, TP),
    )
    return jax.shard_map(
        per_device,
        mesh=finer,
        in_specs=in_specs,
        out_specs=(P(group, TP), P(group, TP)),
        check_vma=False,
    )
```

time: 182 us -> 95 us (0.52)
  waiting for transfers between devices: 95.5 us -> 28.4 us
  Pallas kernels: 0 us -> 16.2 us
  local copies, waits for them, and re-layouts: 17.4 us -> 3.61 us
  starting transfers between devices: 55.4 us -> 45.2 us
  other arithmetic: 7.76 us -> 0.08 us
  matrix products: 4.2 us -> 0 us
    all_to_all x6 -> x4, waiting for transfers between devices: 95.5 us -> 26.5 us  [exchanged(): return lax.all_to_all(slots, axis, 0, 0, tiled=True)]
    pallas_call x0 -> x7, Pallas kernels: none -> 16.2 us  [the longest x1 2.93 us: per_device(): pl.pallas_call(project, out_shape=shape((16, 64, HD), BF16), name='project')]
    all_to_all x6 -> x4, starting transfers between devices: 48.4 us -> 38 us  [exchanged(): return lax.all_to_all(slots, axis, 0, 0, tiled=True)]
    shift_right_arithmetic x4 -> x0, local copies, waits for them, and re-layouts: 7.1 us -> none  [per_device(): jnp.right_shift(packed[:, :, None], shifts[None, None, :])]
    gather x1 -> x0, local copies, waits for them, and re-layouts: 6.18 us -> none  [per_device(): outgoing = jnp.take(padded, take_index, axis=1)]
    dot_general x4 -> x0, matrix products: 4.2 us -> none  [the longest x1 3.33 us: compute(): lax.dot_general(w_kv, hidden, (((0,), (1,)), ((), ())), preferred_element...]
    select_n x6 -> x0, other arithmetic: 3.2 us -> none  [the longest x1 1.19 us: per_device(): logprob = jnp.where(permitted, values - normalizer[:, None], 0.0)]
    ppermute x3, waiting for transfers between devices: 0.01 us -> 1.86 us  [per_device(): lax.ppermute(hidden[64 * k:64 * (k + 1)], 'x', [(0, k)])]
  transfers between devices with their start and end apart: 9 -> 7, of which waited for: 6 -> 5; matrix products, arithmetic and copies ran while one was open for 12% -> 3% of each run, Pallas kernels for 0% -> 13%
where the time goes in v1:
time: 95 us; the launch traced here: 94.3 us
  starting transfers between devices  45.2 us (48%)
  waiting for transfers between devices  28.4 us (30%)
  Pallas kernels  16.2 us (17%)
  local copies, waits for them, and re-layouts  3.61 us (4%)
    all_to_all x4, starting transfers between devices, exchanged(): return lax.all_to_all(slots, axis, 0, 0, tiled=True)  38 us
    all_to_all x4, waiting for transfers between devices, exchanged(): return lax.all_to_all(slots, axis, 0, 0, tiled=True)  26.5 us
    ppermute x3, starting transfers between devices, per_device(): lax.ppermute(hidden[64 * k:64 * (k + 1)], 'x', [(0, k)])  7.24 us
    pallas_call x1, Pallas kernels, per_device(): pl.pallas_call(project, out_shape=shape((16, 64, HD), BF16), name='project')  2.93 us
    pallas_call x1, Pallas kernels, per_device(): pl.pallas_call(grammar, out_shape=(shape(logits.shape, BF16), shape((16,...  2.9 us
    pallas_call x1, Pallas kernels, per_device(): pl.pallas_call(attend_cached, out_shape=shape((16, 16, HD), BF16), in_spe...  2.63 us
    pallas_call x1, Pallas kernels, per_device(): pl.pallas_call(finish_logprob, out_shape=shape(logits.shape, F32), name='...  2.46 us
    pallas_call x1, Pallas kernels, per_device(): pl.pallas_call(attend_landed, out_shape=shape(queries.shape, BF16), name=...  2.09 us
  transfers between devices with their start and end apart: 7, of which 5 were waited for; matrix products, arithmetic and copies ran while one was open for 3% of the time, Pallas kernels for 13%

profile of v1, /device:TPU:24, one launch (start us, length us, event | category | flops | bytes accessed | tf_op | source)
XLA Modules:
  0.0 94.3 jit_solution(5490960504344446426)
XLA Ops:
  0.6 0.0 copy-start.7
  0.6 1.6 %pack.1 = bf16[16,16,128]{2,1,0:T(8,128)(2,1)} custom-call(bf16[32,512]{1,0:T(8,128)(2,1)} %queries.3, bf16[32,128]{1,0:T(8,128)(2,1)} %fresh.1), custom_call_target="tpu_custom_call" | custom-call | tf_op jit(solution)/shard_map/pack/pallas_call | solution.py:261
  2.2 15.2 %all-to-all-start.2 = ((bf16[16,16,128]{2,1,0:T(8,128)(2,1)}), bf16[16,16,128]{2,1,0:T(8,128)(2,1)S(1)}, u32[]{:S(2)}, u32[]{:S(2)}) async-start(bf16[16,16,128]{2,1,0:T(8,128)(2,1)} %pack.1), calls=%async_computation.2 | async-start | bytes 131072 | tf_op jit(solution)/shard_map/all_to_all | solution.py:239
  17.4 1.6 %fusion = (bf16[64,512]{1,0:T(8,128)(2,1)S(1)}, bf16[64,512]{1,0:T(8,128)(2,1)S(1)}, bf16[64,512]{1,0:T(8,128)(2,1)}, bf16[64,512]{1,0:T(8,128)(2,1)S(1)}) fusion(bf16[256,512]{1,0:T(8,128)(2,1)} %param.11), kind=kLoop, calls=%fused_computation.2 | loop fusion | bytes 524288 | tf_op jit(solution)/shard_map/slice | solution.py:259
  19.0 4.7 %collective-permute-start.2 = (bf16[64,512]{1,0:T(8,128)(2,1)S(1)}, bf16[64,512]{1,0:T(8,128)(2,1)S(1)}, u32[]{:S(2)}, u32[]{:S(2)}) collective-permute-start(bf16[64,512]{1,0:T(8,128)(2,1)S(1)} %get-tuple-element.6), channel_id=1, source_target_pairs={{0,384},{1,385},{2,386},{3,387},{4,388},{5,389},{6,390},{7,391},{8... | collective-permute-start | bytes 196616 | tf_op jit(solution)/shard_map/ppermute | solution.py:259
  23.7 1.3 %collective-permute-start = (bf16[64,512]{1,0:T(8,128)(2,1)S(1)}, bf16[64,512]{1,0:T(8,128)(2,1)S(1)}, u32[]{:S(2)}, u32[]{:S(2)}) collective-permute-start(bf16[64,512]{1,0:T(8,128)(2,1)S(1)} %get-tuple-element.7), channel_id=1, source_target_pairs={{0,128},{1,129},{2,130},{3,131},{4,132},{5,133},{6,134},{7,135},{8... | collective-permute-start | bytes 196616 | tf_op jit(solution)/shard_map/ppermute | solution.py:259
  25.0 1.3 %collective-permute-start.1 = (bf16[64,512]{1,0:T(8,128)(2,1)S(1)}, bf16[64,512]{1,0:T(8,128)(2,1)S(1)}, u32[]{:S(2)}, u32[]{:S(2)}) collective-permute-start(bf16[64,512]{1,0:T(8,128)(2,1)S(1)} %get-tuple-element.9), channel_id=1, source_target_pairs={{0,256},{1,257},{2,258},{3,259},{4,260},{5,261},{6,262},{7,263},{8... | collective-permute-start | bytes 196616 | tf_op jit(solution)/shard_map/ppermute | solution.py:259
  26.3 0.0 collective-permute-done.2.third
  26.3 0.0 copy-start.4
  26.3 1.0 %collective-permute-done.first = bf16[64,512]{1,0:T(8,128)(2,1)S(1)} collective-permute-done((bf16[64,512]{1,0:T(8,128)(2,1)S(1)}, bf16[64,512]{1,0:T(8,128)(2,1)S(1)}, u32[]{:S(2)}, u32[]{:S(2)}) %collective-permute-start) | collective-permute-done | bytes 65568 | tf_op jit(solution)/shard_map/ppermute | solution.py:259
  27.3 0.0 copy-start.5
  27.3 0.8 collective-permute-done.1.second
  28.1 0.0 copy-start.6
  28.1 0.0 copy-done.4
  28.1 0.0 copy-done.5
  28.2 0.6 copy-done.6
  28.8 2.9 %project.1 = bf16[16,64,128]{2,1,0:T(8,128)(2,1)} custom-call(bf16[64,512]{1,0:T(8,128)(2,1)} %get-tuple-element.8.own, bf16[64,512]{1,0:T(8,128)(2,1)} %copy-done.5, bf16[64,512]{1,0:T(8,128)(2,1)} %copy-done.6, bf16[64,512]{1,0:T(8,128)(2,1)} %copy-done.4, bf16[512,2048]{1,0:T(8,128)(2,1)} %weight.1), custom_call_target="tpu_custom_call" | custom-call | tf_op jit(solution)/shard_map/project/pallas_call | solution.py:265
  31.7 0.0 all-to-all-done.2.received
  31.7 0.0 copy-start.3
  31.7 12.0 %all-to-all-start = ((bf16[16,64,128]{2,1,0:T(8,128)(2,1)}), bf16[16,64,128]{2,1,0:T(8,128)(2,1)S(1)}, u32[]{:S(2)}, u32[]{:S(2)}) async-start(bf16[16,64,128]{2,1,0:T(8,128)(2,1)} %project.1), calls=%async_computation | async-start | bytes 524288 | tf_op jit(solution)/shard_map/all_to_all | solution.py:239
  43.8 0.0 copy-done.7
  43.8 0.1 broadcast_add_fusion
  43.8 0.7 add.27.key
  44.6 2.9 %grammar.1 = (bf16[32,7680]{1,0:T(8,128)(2,1)}, bf16[16,128]{1,0:T(8,128)(2,1)}) custom-call(bf16[32,7680]{1,0:T(8,128)(2,1)} %logits.1, s32[128,1]{1,0:T(8,128)} %add.27.key, s32[24,256]{1,0:T(8,128)} %masks.1), custom_call_target="tpu_custom_call" | custom-call | tf_op jit(solution)/shard_map/grammar/pallas_call | solution.py:270
  47.5 0.0 copy-done.3
  47.5 2.6 %cached.1 = bf16[16,16,128]{2,1,0:T(8,128)(2,1)} custom-call(s32[2]{0:T(128)} %cache_len.1, bf16[16,16,128]{2,1,0:T(8,128)(2,1)} %copy-done.3, bf16[2,128,2048]{2,1,0:T(8,128)(2,1)} %cache.1, bf16[16,128]{1,0:T(8,128)(2,1)} %get-tuple-element.4.terms, s32[8,16]{1,0:T(8,128)} %lengths.3, s32[8,16]{1,0:T(8,128)} %owners.3), custom_call_target="tpu_custom_call" | custom-call | tf_op jit(solution)/shard_map/cached/pallas_call | solution.py:275
  50.1 11.1 %all-to-all-done.pieces = bf16[16,64,128]{2,1,0:T(8,128)(2,1)S(1)} async-done(((bf16[16,64,128]{2,1,0:T(8,128)(2,1)}), bf16[16,64,128]{2,1,0:T(8,128)(2,1)S(1)}, u32[]{:S(2)}, u32[]{:S(2)}) %all-to-all-start) | async-done | bytes 262176 | tf_op jit(solution)/shard_map/all_to_all | solution.py:239
  61.2 0.0 copy-start
  61.2 5.4 %all-to-all-start.3 = ((bf16[16,16,128]{2,1,0:T(8,128)(2,1)}), bf16[16,16,128]{2,1,0:T(8,128)(2,1)S(1)}, u32[]{:S(2)}, u32[]{:S(2)}) async-start(bf16[16,16,128]{2,1,0:T(8,128)(2,1)} %cached.1), calls=%async_computation.3 | async-start | bytes 131072 | tf_op jit(solution)/shard_map/all_to_all | solution.py:239
  66.7 0.0 copy-done
  66.7 1.6 %reduce.1 = bf16[8,64,128]{2,1,0:T(8,128)(2,1)} custom-call(bf16[16,64,128]{2,1,0:T(8,128)(2,1)} %copy-done), custom_call_target="tpu_custom_call" | custom-call | tf_op jit(solution)/shard_map/reduce/pallas_call | solution.py:282
  68.3 11.2 %all-to-all-done.3.received = bf16[16,16,128]{2,1,0:T(8,128)(2,1)S(1)} async-done(((bf16[16,16,128]{2,1,0:T(8,128)(2,1)}), bf16[16,16,128]{2,1,0:T(8,128)(2,1)S(1)}, u32[]{:S(2)}, u32[]{:S(2)}) %all-to-all-start.3) | async-done | bytes 65568 | tf_op jit(solution)/shard_map/all_to_all | solution.py:239
  79.5 0.0 copy-start.1
  79.5 5.3 %all-to-all-start.1 = ((bf16[8,64,128]{2,1,0:T(8,128)(2,1)}), bf16[8,64,128]{2,1,0:T(8,128)(2,1)S(1)}, u32[]{:S(2)}, u32[]{:S(2)}) async-start(bf16[8,64,128]{2,1,0:T(8,128)(2,1)} %reduce.1), calls=%async_computation.1 | async-start | bytes 262144 | tf_op jit(solution)/shard_map/all_to_all | solution.py:239
  84.8 0.0 copy-done.1
  84.8 2.5 %logprob.1 = f32[32,7680]{1,0:T(8,128)} custom-call(bf16[32,7680]{1,0:T(8,128)(2,1)} %get-tuple-element.5.masked, bf16[16,16,128]{2,1,0:T(8,128)(2,1)} %copy-done.1), custom_call_target="tpu_custom_call" | custom-call | tf_op jit(solution)/shard_map/logprob/pallas_call | solution.py:286
  87.3 4.2 %all-to-all-done.1.blocks = bf16[8,64,128]{2,1,0:T(8,128)(2,1)S(1)} async-done(((bf16[8,64,128]{2,1,0:T(8,128)(2,1)}), bf16[8,64,128]{2,1,0:T(8,128)(2,1)S(1)}, u32[]{:S(2)}, u32[]{:S(2)}) %all-to-all-start.1) | async-done | bytes 131104 | tf_op jit(solution)/shard_map/all_to_all | solution.py:239
  91.5 0.0 copy-start.2
  91.5 0.6 copy-done.2
  92.2 2.1 %landed.1 = bf16[32,512]{1,0:T(8,128)(2,1)} custom-call(bf16[8,64,128]{2,1,0:T(8,128)(2,1)} %copy-done.2, bf16[32,512]{1,0:T(8,128)(2,1)} %queries.3, bf16[16,16,128]{2,1,0:T(8,128)(2,1)} %copy-done.1, s32[8,16]{1,0:T(8,128)} %lengths.3, s32[8,16]{1,0:T(8,128)} %owners.3), custom_call_target="tpu_custom_call" | custom-call | tf_op jit(solution)/shard_map/landed/pallas_call | solution.py:289
  (1 shorter events, 0.0 us)
Async XLA Ops:
  0.6 43.1 %copy-start.7 = (s32[32]{0:T(128)S(1)}, s32[32]{0:T(128)}, u32[]{:S(2)}) copy-start(s32[32]{0:T(128)} %param.20) | copy-start | bytes 388
  2.2 29.5 %all-to-all-start.2 = ((bf16[16,16,128]{2,1,0:T(8,128)(2,1)}), bf16[16,16,128]{2,1,0:T(8,128)(2,1)S(1)}, u32[]{:S(2)}, u32[]{:S(2)}) async-start(bf16[16,16,128]{2,1,0:T(8,128)(2,1)} %pack.1), calls=%async_computation.2 | async-start | bytes 131072 | tf_op jit(solution)/shard_map/all_to_all | solution.py:239
  19.0 7.3 %collective-permute-start.2 = (bf16[64,512]{1,0:T(8,128)(2,1)S(1)}, bf16[64,512]{1,0:T(8,128)(2,1)S(1)}, u32[]{:S(2)}, u32[]{:S(2)}) collective-permute-start(bf16[64,512]{1,0:T(8,128)(2,1)S(1)} %get-tuple-element.6), channel_id=1, source_target_pairs={{0,384},{1,385},{2,386},{3,387},{4,388},{5,389},{6,390},{7,391},{8... | collective-permute-start | bytes 196616 | tf_op jit(solution)/shard_map/ppermute | solution.py:259
  23.7 3.7 %collective-permute-start = (bf16[64,512]{1,0:T(8,128)(2,1)S(1)}, bf16[64,512]{1,0:T(8,128)(2,1)S(1)}, u32[]{:S(2)}, u32[]{:S(2)}) collective-permute-start(bf16[64,512]{1,0:T(8,128)(2,1)S(1)} %get-tuple-element.7), channel_id=1, source_target_pairs={{0,128},{1,129},{2,130},{3,131},{4,132},{5,133},{6,134},{7,135},{8... | collective-permute-start | bytes 196616 | tf_op jit(solution)/shard_map/ppermute | solution.py:259
  25.0 3.2 %collective-permute-start.1 = (bf16[64,512]{1,0:T(8,128)(2,1)S(1)}, bf16[64,512]{1,0:T(8,128)(2,1)S(1)}, u32[]{:S(2)}, u32[]{:S(2)}) collective-permute-start(bf16[64,512]{1,0:T(8,128)(2,1)S(1)} %get-tuple-element.9), channel_id=1, source_target_pairs={{0,256},{1,257},{2,258},{3,259},{4,260},{5,261},{6,262},{7,263},{8... | collective-permute-start | bytes 196616 | tf_op jit(solution)/shard_map/ppermute | solution.py:259
  26.3 1.9 %copy-start.4 = (bf16[64,512]{1,0:T(8,128)(2,1)}, bf16[64,512]{1,0:T(8,128)(2,1)S(1)}, u32[]{:S(2)}) copy-start(bf16[64,512]{1,0:T(8,128)(2,1)S(1)} %collective-permute-done.2.third) | copy-start | bytes 196612
  27.3 0.8 copy-start.5
  28.1 0.6 copy-start.6
  31.7 15.8 %copy-start.3 = (bf16[16,16,128]{2,1,0:T(8,128)(2,1)}, bf16[16,16,128]{2,1,0:T(8,128)(2,1)S(1)}, u32[]{:S(2)}) copy-start(bf16[16,16,128]{2,1,0:T(8,128)(2,1)S(1)} %all-to-all-done.2.received) | copy-start | bytes 196612
  31.7 29.5 %all-to-all-start = ((bf16[16,64,128]{2,1,0:T(8,128)(2,1)}), bf16[16,64,128]{2,1,0:T(8,128)(2,1)S(1)}, u32[]{:S(2)}, u32[]{:S(2)}) async-start(bf16[16,64,128]{2,1,0:T(8,128)(2,1)} %project.1), calls=%async_computation | async-start | bytes 524288 | tf_op jit(solution)/shard_map/all_to_all | solution.py:239
  61.2 5.5 %copy-start = (bf16[16,64,128]{2,1,0:T(8,128)(2,1)}, bf16[16,64,128]{2,1,0:T(8,128)(2,1)S(1)}, u32[]{:S(2)}) copy-start(bf16[16,64,128]{2,1,0:T(8,128)(2,1)S(1)} %all-to-all-done.pieces) | copy-start | bytes 786436
  61.2 18.3 %all-to-all-start.3 = ((bf16[16,16,128]{2,1,0:T(8,128)(2,1)}), bf16[16,16,128]{2,1,0:T(8,128)(2,1)S(1)}, u32[]{:S(2)}, u32[]{:S(2)}) async-start(bf16[16,16,128]{2,1,0:T(8,128)(2,1)} %cached.1), calls=%async_computation.3 | async-start | bytes 131072 | tf_op jit(solution)/shard_map/all_to_all | solution.py:239
  79.5 5.3 %copy-start.1 = (bf16[16,16,128]{2,1,0:T(8,128)(2,1)}, bf16[16,16,128]{2,1,0:T(8,128)(2,1)S(1)}, u32[]{:S(2)}) copy-start(bf16[16,16,128]{2,1,0:T(8,128)(2,1)S(1)} %all-to-all-done.3.received) | copy-start | bytes 196612
  79.5 12.0 %all-to-all-start.1 = ((bf16[8,64,128]{2,1,0:T(8,128)(2,1)}), bf16[8,64,128]{2,1,0:T(8,128)(2,1)S(1)}, u32[]{:S(2)}, u32[]{:S(2)}) async-start(bf16[8,64,128]{2,1,0:T(8,128)(2,1)} %reduce.1), calls=%async_computation.1 | async-start | bytes 262144 | tf_op jit(solution)/shard_map/all_to_all | solution.py:239
  91.5 0.6 copy-start.2

commit v2 on v1

--- a/solution.py
+++ b/solution.py
@@ -7,11 +7,11 @@
 from jax.experimental.pallas import tpu as pltpu
 from jax.sharding import Mesh, PartitionSpec as P
 
-HEADS = 64
 KVH = 8
 HD = 128
 STATES = 24
 BITS = 30
+LOWEST = -1e30
 BLK = 1920
 SCALE = 1.0 / math.sqrt(HD)
 F32 = jnp.float32
@@ -31,10 +31,6 @@
 
 def pick(target, table):
     return jnp.dot(one_hot(target, table.shape[0]), table, preferred_element_type=F32)
-
-
-def call(kernel, out, name, memory=None):
-    return pl.pallas_call(kernel, out_shape=out, name=name)
 
 
 def prompts_of(lengths, owners, source, turn):
@@ -59,9 +55,21 @@
     return jnp.sum(matched, axis=1, keepdims=True), total(start), total(length)
 
 
-def pack_queries(queries, fresh, out):
+def prepare(hidden, queries, fresh, own, first, second, third, asked, query, new, sems):
+    shares = [
+        pltpu.make_async_copy(hidden.at[pl.ds(64 * k, 64)], out, sems.at[k])
+        for k, out in enumerate((own, first, second, third))
+    ]
+    loads = [
+        pltpu.make_async_copy(queries, query, sems.at[4]),
+        pltpu.make_async_copy(fresh, new, sems.at[5]),
+    ]
+    for copy in loads + shares:
+        copy.start()
+    for copy in loads:
+        copy.wait()
     table = jnp.concatenate(
-        [queries[:, HD * i : HD * (i + 1)] for i in range(4)] + [fresh[...]], axis=0
+        [query[:, HD * i : HD * (i + 1)] for i in range(4)] + [new[...]], axis=0
     )
     row = iota((256, 1), 0)
     dest, k = row // 16, row % 16
@@ -70,28 +78,37 @@
         (k % 4) * 32 + 2 * dest + k // 4,
         jnp.where(k < 10, 128 + 2 * dest + k - 8, 160),
     )
-    out[...] = pick(target, table).astype(BF16).reshape(16, 16, HD)
-
-
-def project(own, first, second, third, weight, out):
+    asked[...] = pick(target, table).astype(BF16).reshape(16, 16, HD)
+    for copy in shares:
+        copy.wait()
+
+
+def fetch(weight, out, sem):
+    copy = pltpu.make_async_copy(weight, out, sem)
+    copy.start()
+    copy.wait()
+
+
+def project(own, first, second, third, weight, asked, out):
     turn = lax.axis_index("x")
-    tokens = jnp.where(turn == 0, own[0:64, :], first[...] + second[...] + third[...])
+    tokens = jnp.where(turn == 0, own[...], first[...] + second[...] + third[...])
     full = jnp.dot(tokens, weight[...], preferred_element_type=F32).astype(BF16)
     for c in range(16):
         block = c // 2 + (c % 2) * KVH
-        out[c] = full[:, HD * block : HD * (block + 1)]
+        out[c, 0:64] = full[:, HD * block : HD * (block + 1)]
+        out[c, 64:80] = asked[c]
 
 
 def reduce_blocks(pieces, out):
-    total = pieces[0].astype(F32)
+    total = pieces[0, 0:64].astype(F32)
     for c in range(1, 16):
-        total = total + pieces[c].astype(F32)
+        total = total + pieces[c, 0:64].astype(F32)
     total = total.astype(BF16)
     for d in range(8):
         out[d] = total
 
 
-def grammar(logits, key, masks, masked, terms):
+def grammar(logits, states, masks, masked, terms):
     lane = iota((STATES, HD), 1)
     blocks = []
     for half in range(2):
@@ -109,7 +126,11 @@
                 )
             )
     table = jnp.concatenate(blocks, axis=0).astype(F32).astype(BF16)
-    chosen = pick(key[...], table).astype(BF16)
+    row, lane = iota((32, 32), 0), iota((32, 32), 1)
+    state = jnp.where(row == lane, states[...], 0).astype(F32)
+    state = jnp.sum(state, axis=1, keepdims=True).astype(I32)
+    key = jnp.concatenate([state + STATES * b for b in range(4)], axis=0)
+    chosen = pick(key, table).astype(BF16)
     column = iota((1, BLK), 1)
     word = jnp.right_shift(column * 34953, 20)
     bit = column - word * BITS
@@ -162,7 +183,7 @@
         lengths[...], owners[...], lax.axis_index("c8"), lax.axis_index("x")
     )
     landed = landing(jnp.full((1, 1), column, I32), prompts)[0]
-    table = received[...].reshape(256, HD)
+    table = received[:, 64:80, :].reshape(256, HD)
     row = iota((256, 1), 0)
     device, k = row // 16, row % 16
     second = (k >= 4) & (k < 8)
@@ -196,7 +217,32 @@
     out[...] = result.astype(BF16).reshape(16, 16, HD)
 
 
-def finish_logprob(masked, received, out):
+def own_prompts(row, lengths, owners):
+    request = row % 32
+    prompts = prompts_of(
+        lengths[...], owners[...], lax.axis_index("c8"), lax.axis_index("x")
+    )
+    return landing((request % 2) * 16 + request // 2, prompts)
+
+
+def attend_prompts(blocks, queries, lengths, owners, result, stats):
+    row = iota((128, 1), 0)
+    landed, start, length = own_prompts(row, lengths, owners)
+    keys = jnp.concatenate([blocks[2 * x] for x in range(4)], axis=0)
+    values = jnp.concatenate([blocks[2 * x + 1] for x in range(4)], axis=0)
+    query = jnp.concatenate([queries[:, HD * i : HD * (i + 1)] for i in range(4)], axis=0)
+    score = transposed(query, keys) * SCALE
+    position = iota((128, 256), 1).astype(F32)
+    alive = (position >= start) & (position < start + length)
+    highest = jnp.max(jnp.where(alive, score, LOWEST), axis=1, keepdims=True)
+    exponent = jnp.where(alive, jnp.exp(score - highest), 0.0)
+    result[...] = jnp.dot(exponent.astype(BF16), values, preferred_element_type=F32)
+    total = jnp.sum(exponent, axis=1, keepdims=True)
+    lane = iota((128, HD), 1)
+    stats[...] = jnp.where(lane == 0, highest, jnp.where(lane == 1, total, landed))
+
+
+def finish(masked, received, queries, result, stats, logprob, attended, values, sems):
     lines = received[:, 8, :].astype(F32)
     take = lambda k: lines[:, 32 * k : 32 * (k + 1)]
     peak, total = take(0), take(1) + take(2) + take(3)
@@ -205,19 +251,19 @@
     normalizer = highest + jnp.log(total)
     row, lane = iota((32, 32), 0), iota((32, 32), 1)
     normalizer = jnp.sum(jnp.where(row == lane, normalizer, 0.0), axis=1, keepdims=True)
-    values = masked[...].astype(F32)
-    out[...] = jnp.where(values == -jnp.inf, 0.0, values - normalizer)
-
-
-def attend_landed(blocks, queries, received, lengths, owners, out):
-    prompts = prompts_of(
-        lengths[...], owners[...], lax.axis_index("c8"), lax.axis_index("x")
-    )
+    copies = []
+    for b in range(4):
+        at = slice(BLK * b, BLK * (b + 1))
+        section = masked[:, at].astype(F32)
+        values[:, at] = jnp.where(section == -jnp.inf, 0.0, section - normalizer)
+        copies.append(
+            pltpu.make_async_copy(
+                values.at[:, pl.ds(BLK * b, BLK)], logprob.at[:, pl.ds(BLK * b, BLK)], sems.at[b]
+            )
+        )
+        copies[-1].start()
     row = iota((128, 1), 0)
     head, request = row // 32, row % 32
-    landed, start, length = landing((request % 2) * 16 + request // 2, prompts)
-    keys = jnp.concatenate([blocks[2 * x] for x in range(4)], axis=0)
-    values = jnp.concatenate([blocks[2 * x + 1] for x in range(4)], axis=0)
     query = jnp.concatenate([queries[:, HD * i : HD * (i + 1)] for i in range(4)], axis=0)
     table = received[...].reshape(256, HD)
     slot = (request // 2) * 16
@@ -225,14 +271,16 @@
     own_value = pick(slot + 1, table)
     cached = pick(slot + (request % 2) * 4 + head, table)
     own = jnp.sum(query.astype(F32) * own_key, axis=1, keepdims=True) * SCALE
-    score = transposed(query, keys) * SCALE
-    position = iota((128, 256), 1).astype(F32)
-    alive = (position >= start) & (position < start + length)
-    weight, own_weight = softmax(score, own, alive)
-    result = jnp.dot(weight, values, preferred_element_type=F32) + own_weight * own_value
-    result = jnp.where(landed > 0.5, result, cached).astype(BF16)
+    top, total, landed = stats[:, 0:1], stats[:, 1:2], stats[:, 2:3]
+    highest = jnp.maximum(top, own)
+    share, own_share = jnp.exp(top - highest), jnp.exp(own - highest)
+    scale = 1.0 / (total * share + own_share)
+    merged = (result[...] * share + own_value * own_share) * scale
+    merged = jnp.where(landed > 0.5, merged, cached).astype(BF16)
     for i in range(4):
-        out[:, HD * i : HD * (i + 1)] = result[32 * i : 32 * (i + 1)]
+        attended[:, HD * i : HD * (i + 1)] = merged[32 * i : 32 * (i + 1)]
+    for copy in copies:
+        copy.wait()
 
 
 def exchanged(slots, axis):
@@ -252,43 +300,79 @@
     states,
     masks,
 ):
-    shape = jax.ShapeDtypeStruct
     smem = pl.BlockSpec(memory_space=pltpu.SMEM)
     vmem = pl.BlockSpec(memory_space=pltpu.VMEM)
-    shares = [
-        lax.ppermute(hidden[64 * k : 64 * (k + 1)], "x", [(0, k)]) for k in (1, 2, 3)
+    hbm = pl.BlockSpec(memory_space=pl.ANY)
+    sent = jax.ShapeDtypeStruct
+    kept = pltpu.VMEM
+    held = lambda *values: [
+        pltpu.with_memory_space_constraint(value, pltpu.VMEM) for value in values
     ]
-    asked = pl.pallas_call(pack_queries, out_shape=shape((16, 16, HD), BF16), name="pack")(
-        queries, fresh
-    )
-    asked = exchanged(asked, TP)
+    tokens, wide = hidden.shape[0] // 4, hidden.shape[1]
+    *shares, asked = pl.pallas_call(
+        prepare,
+        out_shape=[kept((tokens, wide), BF16)] * 4 + [kept((16, 16, HD), BF16)],
+        in_specs=[hbm] * 3,
+        out_specs=[vmem] * 5,
+        scratch_shapes=[
+            pltpu.VMEM(queries.shape, BF16),
+            pltpu.VMEM(fresh.shape, BF16),
+            pltpu.SemaphoreType.DMA((6,)),
+        ],
+        name="prepare",
+    )(hidden, queries, fresh)
+    shares[1:] = [lax.ppermute(shares[k], "x", [(0, k)]) for k in (1, 2, 3)]
+    weight = pl.pallas_call(
+        fetch,
+        out_shape=kept(w_kv.shape, BF16),
+        in_specs=[hbm],
+        out_specs=vmem,
+        scratch_shapes=[pltpu.SemaphoreType.DMA],
+        name="fetch",
+    )(w_kv)
     projected = pl.pallas_call(
-        project, out_shape=shape((16, 64, HD), BF16), name="project"
-    )(hidden[0:64], *shares, w_kv)
+        project,
+        out_shape=sent((16, 80, HD), BF16),
+        in_specs=[vmem] * 6,
+        name="project",
+    )(*held(*shares, weight, asked))
     pieces = exchanged(projected, TP)
-    key = (states[None, :] + STATES * jnp.arange(4, dtype=I32)[:, None]).reshape(128, 1)
     masked, terms = pl.pallas_call(
         grammar,
-        out_shape=(shape(logits.shape, BF16), shape((16, HD), BF16)),
+        out_shape=[kept(logits.shape, BF16), kept((16, HD), BF16)],
+        in_specs=[vmem] * 3,
+        out_specs=[vmem] * 2,
         name="grammar",
-    )(logits, key, masks)
+    )(*held(logits, states.reshape(1, -1), masks))
+    blocks = pl.pallas_call(
+        reduce_blocks,
+        out_shape=sent((8, tokens, HD), BF16),
+        in_specs=[vmem],
+        name="reduce",
+    )(*held(pieces))
+    blocks = exchanged(blocks, ("x", "zl"))
     answers = pl.pallas_call(
         attend_cached,
-        out_shape=shape((16, 16, HD), BF16),
+        out_shape=sent((16, 16, HD), BF16),
         in_specs=[smem] + [vmem] * 5,
         name="cached",
-    )(cache_len, asked, cache, terms, prompt_lengths, owner_step)
+    )(cache_len, *held(pieces, cache, terms, prompt_lengths, owner_step))
     answers = exchanged(answers, TP)
-    blocks = pl.pallas_call(
-        reduce_blocks, out_shape=shape((8, 64, HD), BF16), name="reduce"
-    )(pieces)
-    blocks = exchanged(blocks, ("x", "zl"))
-    logprob = pl.pallas_call(
-        finish_logprob, out_shape=shape(logits.shape, F32), name="logprob"
-    )(masked, answers)
-    attended = pl.pallas_call(
-        attend_landed, out_shape=shape(queries.shape, BF16), name="landed"
-    )(blocks, queries, answers, prompt_lengths, owner_step)
+    result, stats = pl.pallas_call(
+        attend_prompts,
+        out_shape=[kept((128, HD), F32), kept((128, HD), F32)],
+        in_specs=[vmem] * 4,
+        out_specs=[vmem] * 2,
+        name="prompts",
+    )(*held(blocks, queries, prompt_lengths, owner_step))
+    logprob, attended = pl.pallas_call(
+        finish,
+        out_shape=[sent(logits.shape, F32), sent(queries.shape, BF16)],
+        in_specs=[vmem] * 5,
+        out_specs=[hbm, vmem],
+        scratch_shapes=[pltpu.VMEM(logits.shape, F32), pltpu.SemaphoreType.DMA((4,))],
+        name="finish",
+    )(*held(masked, answers, queries, result, stats))
     return attended, logprob
 
 

time: 95 us -> 81.4 us (0.86)
  blocking collectives: 0 us -> 35.7 us
  starting transfers between devices: 45.2 us -> 18 us
  waiting for transfers between devices: 28.4 us -> 15 us
  Pallas kernels: 16.2 us -> 10.3 us
  local copies, waits for them, and re-layouts: 3.61 us -> 1.05 us
    all_to_all x0 -> x1, blocking collectives: none -> 35.7 us  [exchanged(): return lax.all_to_all(slots, axis, 0, 0, tiled=True)]
    all_to_all x4 -> x2, starting transfers between devices: 38 us -> 11.1 us  [exchanged(): return lax.all_to_all(slots, axis, 0, 0, tiled=True)]
    all_to_all x4 -> x2, waiting for transfers between devices: 26.5 us -> 14.7 us  [exchanged(): return lax.all_to_all(slots, axis, 0, 0, tiled=True)]
    pallas_call x7 -> x8, Pallas kernels: 16.2 us -> 10.3 us  [the longest x1 2.05 us: per_device(): pl.pallas_call(attend_cached, out_shape=sent((16, 16, HD), BF16), in_spec...]
    ppermute x3, waiting for transfers between devices: 1.86 us -> 0.23 us  [per_device(): shares[1:] = [lax.ppermute(shares[k], 'x', [(0, k)]) for k in (1, 2, 3)]]
    slice x1 -> x0, local copies, waits for them, and re-layouts: 1.58 us -> none  [per_device(): hidden[64 * k:64 * (k + 1)]]
  transfers between devices with their start and end apart: 7 -> 5, of which waited for: 5 -> 3; matrix products, arithmetic and copies ran while one was open for 3% -> 0% of each run, Pallas kernels for 13% -> 7%
where the time goes in v2:
time: 81.4 us; the launch traced here: 80.8 us
  blocking collectives  35.7 us (44%)
  starting transfers between devices  18 us (22%)
  waiting for transfers between devices  15 us (18%)
  Pallas kernels  10.3 us (13%)
  local copies, waits for them, and re-layouts  1.05 us (1%)
    all_to_all x1, blocking collectives, exchanged(): return lax.all_to_all(slots, axis, 0, 0, tiled=True)  35.7 us
    all_to_all x2, waiting for transfers between devices, exchanged(): return lax.all_to_all(slots, axis, 0, 0, tiled=True)  14.7 us
    all_to_all x2, starting transfers between devices, exchanged(): return lax.all_to_all(slots, axis, 0, 0, tiled=True)  11.1 us
    ppermute x3, starting transfers between devices, per_device(): shares[1:] = [lax.ppermute(shares[k], 'x', [(0, k)]) for k in (1, 2, 3)]  6.89 us
    pallas_call x1, Pallas kernels, per_device(): pl.pallas_call(attend_cached, out_shape=sent((16, 16, HD), BF16), in_spec...  2.05 us
    pallas_call x1, Pallas kernels, per_device(): pl.pallas_call(finish, out_shape=[sent(logits.shape, F32), sent(queries.s...  2.01 us
  transfers between devices with their start and end apart: 5, of which 3 were waited for; matrix products, arithmetic and copies ran while one was open for 0% of the time, Pallas kernels for 7%

profile of v2, /device:TPU:24, one launch (start us, length us, event | category | flops | bytes accessed | tf_op | source)
XLA Modules:
  0.0 80.8 jit_solution(16048402949951247220)
XLA Ops:
  0.6 1.0 %prepare.1 = (bf16[64,512]{1,0:T(8,128)(2,1)S(1)}, bf16[64,512]{1,0:T(8,128)(2,1)S(1)}, bf16[64,512]{1,0:T(8,128)(2,1)S(1)}, bf16[64,512]{1,0:T(8,128)(2,1)S(1)}, bf16[16,16,128]{2,1,0:T(8,128)(2,1)S(1)}) custom-call(bf16[256,512]{1,0:T(8,128)(2,1)} %hidden.1, bf16[32,512]{1,0:T(8,128)(2,1)} %queries.5, bf16[32,128]{1,0:T(8,128)(2,1)} %fresh.1), custom_call_target="tpu_custom_call" | custom-call | tf_op jit(solution)/shard_map/prepare/pallas_call | solution.py:312
  1.7 3.4 %collective-permute-start = (bf16[64,512]{1,0:T(8,128)(2,1)S(1)}, bf16[64,512]{1,0:T(8,128)(2,1)S(1)}, u32[]{:S(2)}, u32[]{:S(2)}) collective-permute-start(bf16[64,512]{1,0:T(8,128)(2,1)S(1)} %get-tuple-element.15), channel_id=1, source_target_pairs={{0,128},{1,129},{2,130},{3,131},{4,132},{5,133},{6,134},{7,135},{8... | collective-permute-start | bytes 196616 | tf_op jit(solution)/shard_map/ppermute | solution.py:324
  5.1 2.2 %collective-permute-start.1 = (bf16[64,512]{1,0:T(8,128)(2,1)S(1)}, bf16[64,512]{1,0:T(8,128)(2,1)S(1)}, u32[]{:S(2)}, u32[]{:S(2)}) collective-permute-start(bf16[64,512]{1,0:T(8,128)(2,1)S(1)} %get-tuple-element.16), channel_id=1, source_target_pairs={{0,256},{1,257},{2,258},{3,259},{4,260},{5,261},{6,262},{7,263},{8... | collective-permute-start | bytes 196616 | tf_op jit(solution)/shard_map/ppermute | solution.py:324
  7.3 1.3 %collective-permute-start.2 = (bf16[64,512]{1,0:T(8,128)(2,1)S(1)}, bf16[64,512]{1,0:T(8,128)(2,1)S(1)}, u32[]{:S(2)}, u32[]{:S(2)}) collective-permute-start(bf16[64,512]{1,0:T(8,128)(2,1)S(1)} %get-tuple-element.17), channel_id=1, source_target_pairs={{0,384},{1,385},{2,386},{3,387},{4,388},{5,389},{6,390},{7,391},{8... | collective-permute-start | bytes 196616 | tf_op jit(solution)/shard_map/ppermute | solution.py:324
  8.6 1.6 %fetch.1.weight = bf16[512,2048]{1,0:T(8,128)(2,1)S(1)} custom-call(bf16[512,2048]{1,0:T(8,128)(2,1)} %weight.1), custom_call_target="tpu_custom_call" | custom-call | tf_op jit(solution)/shard_map/fetch/pallas_call | solution.py:325
  10.2 0.0 copy-start.3
  10.2 0.0 copy-start.6
  10.2 0.0 collective-permute-done.first
  10.2 0.0 collective-permute-done.1.second
  10.2 0.2 collective-permute-done.2.third
  10.5 0.0 copy-start
  10.5 0.0 copy-start.4
  10.5 0.0 copy-start.5
  10.5 1.2 %project.1 = bf16[16,80,128]{2,1,0:T(8,128)(2,1)} custom-call(bf16[64,512]{1,0:T(8,128)(2,1)S(1)} %get-tuple-element.14.own, bf16[64,512]{1,0:T(8,128)(2,1)S(1)} %collective-permute-done.first, bf16[64,512]{1,0:T(8,128)(2,1)S(1)} %collective-permute-done.1.second, bf16[64,512]{1,0:T(8,128)(2,1)S(1)} %collective-permute-done.2.third, ...), custom_call_target="tpu_custom_call" | custom-call | tf_op jit(solution)/shard_map/project/pallas_call | solution.py:333
  11.7 0.0 copy-start.2
  11.7 35.7 %all_to_all.15.received.pieces = bf16[16,80,128]{2,1,0:T(8,128)(2,1)S(1)} all-to-all(bf16[16,80,128]{2,1,0:T(8,128)(2,1)} %project.1), channel_id=1, replica_groups=mesh['x'=4,'c8'=8,'zh'=8,'zl'=2] {'zh','zl'}, dimensions={0} | all-to-all | bytes 655360 | tf_op jit(solution)/shard_map/all_to_all | solution.py:287
  47.4 0.7 reduce.1
  48.1 4.9 %all-to-all-start.2 = ((bf16[8,64,128]{2,1,0:T(8,128)(2,1)}), bf16[8,64,128]{2,1,0:T(8,128)(2,1)S(1)}, u32[]{:S(2)}, u32[]{:S(2)}) async-start(bf16[8,64,128]{2,1,0:T(8,128)(2,1)} %reduce.1), calls=%async_computation.2 | async-start | bytes 262144 | tf_op jit(solution)/shard_map/all_to_all | solution.py:287
  53.0 0.0 copy-done.3
  53.0 0.0 copy-done.6
  53.0 0.0 copy-start.1
  53.0 1.0 %copy-done.1 = bf16[32,7680]{1,0:T(8,128)(2,1)S(1)} copy-done((bf16[32,7680]{1,0:T(8,128)(2,1)S(1)}, bf16[32,7680]{1,0:T(8,128)(2,1)}, u32[]{:S(2)}) %copy-start.1) | copy-done | bytes 491544
  54.1 1.3 %grammar.1 = (bf16[32,7680]{1,0:T(8,128)(2,1)S(1)}, bf16[16,128]{1,0:T(8,128)(2,1)S(1)}) custom-call(bf16[32,7680]{1,0:T(8,128)(2,1)S(1)} %copy-done.1, s32[1,32]{1,0:T(1,128)S(1)} %bitcast.1, s32[24,256]{1,0:T(8,128)S(1)} %copy-done.3), custom_call_target="tpu_custom_call" | custom-call | tf_op jit(solution)/shard_map/grammar/pallas_call | solution.py:340
  55.4 0.0 copy-done
  55.4 0.0 copy-done.4
  55.4 0.0 copy-done.5
  55.4 2.1 %cached.1 = bf16[16,16,128]{2,1,0:T(8,128)(2,1)} custom-call(s32[2]{0:T(128)} %cache_len.1, bf16[16,80,128]{2,1,0:T(8,128)(2,1)S(1)} %all_to_all.15.received.pieces, bf16[2,128,2048]{2,1,0:T(8,128)(2,1)S(1)} %copy-done, bf16[16,128]{1,0:T(8,128)(2,1)S(1)} %get-tuple-element.19.terms, s32[8,16]{1,0:T(8,128)S(1)} %copy-done.4, s32[8,16]{1,0:T(8,128)S(1)} %copy-done.5), custom_call_target="tpu_custom_call" | custom-call | tf_op jit(solution)/shard_map/cached/pallas_call | solution.py:354
  57.4 2.3 %all-to-all-done.2.blocks = bf16[8,64,128]{2,1,0:T(8,128)(2,1)S(1)} async-done(((bf16[8,64,128]{2,1,0:T(8,128)(2,1)}), bf16[8,64,128]{2,1,0:T(8,128)(2,1)S(1)}, u32[]{:S(2)}, u32[]{:S(2)}) %all-to-all-start.2) | async-done | bytes 131104 | tf_op jit(solution)/shard_map/all_to_all | solution.py:287
  59.7 6.2 %all-to-all-start.1 = ((bf16[16,16,128]{2,1,0:T(8,128)(2,1)}), bf16[16,16,128]{2,1,0:T(8,128)(2,1)S(1)}, u32[]{:S(2)}, u32[]{:S(2)}) async-start(bf16[16,16,128]{2,1,0:T(8,128)(2,1)} %cached.1), calls=%async_computation.1 | async-start | bytes 131072 | tf_op jit(solution)/shard_map/all_to_all | solution.py:287
  65.9 0.0 copy-done.2
  65.9 0.4 prompts.1
  66.3 12.5 %all-to-all-done.1.received = bf16[16,16,128]{2,1,0:T(8,128)(2,1)S(1)} async-done(((bf16[16,16,128]{2,1,0:T(8,128)(2,1)}), bf16[16,16,128]{2,1,0:T(8,128)(2,1)S(1)}, u32[]{:S(2)}, u32[]{:S(2)}) %all-to-all-start.1) | async-done | bytes 65568 | tf_op jit(solution)/shard_map/all_to_all | solution.py:287
  78.8 2.0 %finish.1 = (f32[32,7680]{1,0:T(8,128)}, bf16[32,512]{1,0:T(8,128)(2,1)}) custom-call(bf16[32,7680]{1,0:T(8,128)(2,1)S(1)} %get-tuple-element.13.masked, bf16[16,16,128]{2,1,0:T(8,128)(2,1)S(1)} %all-to-all-done.1.received, bf16[32,512]{1,0:T(8,128)(2,1)S(1)} %copy-done.2, f32[128,128]{1,0:T(8,128)S(1)} %get-tuple-element.20.result, ...), custom_call_target="tpu_custom_call" | custom-call | tf_op jit(solution)/shard_map/finish/pallas_call | solution.py:368
Async XLA Ops:
  1.7 8.5 %collective-permute-start = (bf16[64,512]{1,0:T(8,128)(2,1)S(1)}, bf16[64,512]{1,0:T(8,128)(2,1)S(1)}, u32[]{:S(2)}, u32[]{:S(2)}) collective-permute-start(bf16[64,512]{1,0:T(8,128)(2,1)S(1)} %get-tuple-element.15), channel_id=1, source_target_pairs={{0,128},{1,129},{2,130},{3,131},{4,132},{5,133},{6,134},{7,135},{8... | collective-permute-start | bytes 196616 | tf_op jit(solution)/shard_map/ppermute | solution.py:324
  5.1 5.2 %collective-permute-start.1 = (bf16[64,512]{1,0:T(8,128)(2,1)S(1)}, bf16[64,512]{1,0:T(8,128)(2,1)S(1)}, u32[]{:S(2)}, u32[]{:S(2)}) collective-permute-start(bf16[64,512]{1,0:T(8,128)(2,1)S(1)} %get-tuple-element.16), channel_id=1, source_target_pairs={{0,256},{1,257},{2,258},{3,259},{4,260},{5,261},{6,262},{7,263},{8... | collective-permute-start | bytes 196616 | tf_op jit(solution)/shard_map/ppermute | solution.py:324
  7.3 3.2 %collective-permute-start.2 = (bf16[64,512]{1,0:T(8,128)(2,1)S(1)}, bf16[64,512]{1,0:T(8,128)(2,1)S(1)}, u32[]{:S(2)}, u32[]{:S(2)}) collective-permute-start(bf16[64,512]{1,0:T(8,128)(2,1)S(1)} %get-tuple-element.17), channel_id=1, source_target_pairs={{0,384},{1,385},{2,386},{3,387},{4,388},{5,389},{6,390},{7,391},{8... | collective-permute-start | bytes 196616 | tf_op jit(solution)/shard_map/ppermute | solution.py:324
  10.2 42.8 %copy-start.3 = (s32[24,256]{1,0:T(8,128)S(1)}, s32[24,256]{1,0:T(8,128)}, u32[]{:S(2)}) copy-start(s32[24,256]{1,0:T(8,128)} %masks.1) | copy-start | bytes 73732
  10.2 42.8 %copy-start.6 = (s32[32]{0:T(128)S(1)}, s32[32]{0:T(128)}, u32[]{:S(2)}) copy-start(s32[32]{0:T(128)} %param.20) | copy-start | bytes 388
  10.5 44.9 %copy-start = (bf16[2,128,2048]{2,1,0:T(8,128)(2,1)S(1)}, bf16[2,128,2048]{2,1,0:T(8,128)(2,1)}, u32[]{:S(2)}) copy-start(bf16[2,128,2048]{2,1,0:T(8,128)(2,1)} %cache.1) | copy-start | bytes 3145732
  10.5 44.9 %copy-start.4 = (s32[8,16]{1,0:T(8,128)S(1)}, s32[8,16]{1,0:T(8,128)}, u32[]{:S(2)}) copy-start(s32[8,16]{1,0:T(8,128)} %lengths.3) | copy-start | bytes 1540
  10.5 44.9 %copy-start.5 = (s32[8,16]{1,0:T(8,128)S(1)}, s32[8,16]{1,0:T(8,128)}, u32[]{:S(2)}) copy-start(s32[8,16]{1,0:T(8,128)} %owners.3) | copy-start | bytes 1540
  11.7 54.2 %copy-start.2 = (bf16[32,512]{1,0:T(8,128)(2,1)S(1)}, bf16[32,512]{1,0:T(8,128)(2,1)}, u32[]{:S(2)}) copy-start(bf16[32,512]{1,0:T(8,128)(2,1)} %queries.5) | copy-start | bytes 98308
  48.1 11.6 %all-to-all-start.2 = ((bf16[8,64,128]{2,1,0:T(8,128)(2,1)}), bf16[8,64,128]{2,1,0:T(8,128)(2,1)S(1)}, u32[]{:S(2)}, u32[]{:S(2)}) async-start(bf16[8,64,128]{2,1,0:T(8,128)(2,1)} %reduce.1), calls=%async_computation.2 | async-start | bytes 262144 | tf_op jit(solution)/shard_map/all_to_all | solution.py:287
  53.0 1.0 %copy-start.1 = (bf16[32,7680]{1,0:T(8,128)(2,1)S(1)}, bf16[32,7680]{1,0:T(8,128)(2,1)}, u32[]{:S(2)}) copy-start(bf16[32,7680]{1,0:T(8,128)(2,1)} %logits.1) | copy-start | bytes 1474564
  59.7 19.1 %all-to-all-start.1 = ((bf16[16,16,128]{2,1,0:T(8,128)(2,1)}), bf16[16,16,128]{2,1,0:T(8,128)(2,1)S(1)}, u32[]{:S(2)}, u32[]{:S(2)}) async-start(bf16[16,16,128]{2,1,0:T(8,128)(2,1)} %cached.1), calls=%async_computation.1 | async-start | bytes 131072 | tf_op jit(solution)/shard_map/all_to_all | solution.py:287

commit v3 on v2

--- a/solution.py
+++ b/solution.py
@@ -11,7 +11,6 @@
 HD = 128
 STATES = 24
 BITS = 30
-LOWEST = -1e30
 BLK = 1920
 SCALE = 1.0 / math.sqrt(HD)
 F32 = jnp.float32
@@ -83,29 +82,34 @@
         copy.wait()
 
 
-def fetch(weight, out, sem):
-    copy = pltpu.make_async_copy(weight, out, sem)
-    copy.start()
-    copy.wait()
-
-
-def project(own, first, second, third, weight, asked, out):
+def project(own, first, second, third, asked, weight, out, held, sems):
+    width = weight.shape[1] // 4
+    loads = [
+        pltpu.make_async_copy(
+            weight.at[:, pl.ds(width * k, width)], held.at[:, pl.ds(width * k, width)], sems.at[k]
+        )
+        for k in range(4)
+    ]
+    for load in loads:
+        load.start()
     turn = lax.axis_index("x")
     tokens = jnp.where(turn == 0, own[...], first[...] + second[...] + third[...])
-    full = jnp.dot(tokens, weight[...], preferred_element_type=F32).astype(BF16)
-    for c in range(16):
-        block = c // 2 + (c % 2) * KVH
-        out[c, 0:64] = full[:, HD * block : HD * (block + 1)]
-        out[c, 64:80] = asked[c]
+    out[:, 64:80] = asked[...]
+    for k in range(4):
+        loads[k].wait()
+        part = held[:, width * k : width * (k + 1)]
+        part = jnp.dot(tokens, part, preferred_element_type=F32).astype(BF16)
+        for i in range(4):
+            block = 4 * k + i
+            c = 2 * (block % KVH) + block // KVH
+            out[c, 0:64] = part[:, HD * i : HD * (i + 1)]
 
 
 def reduce_blocks(pieces, out):
     total = pieces[0, 0:64].astype(F32)
     for c in range(1, 16):
         total = total + pieces[c, 0:64].astype(F32)
-    total = total.astype(BF16)
-    for d in range(8):
-        out[d] = total
+    out[...] = total.astype(BF16)
 
 
 def grammar(logits, states, masks, masked, terms):
@@ -217,32 +221,7 @@
     out[...] = result.astype(BF16).reshape(16, 16, HD)
 
 
-def own_prompts(row, lengths, owners):
-    request = row % 32
-    prompts = prompts_of(
-        lengths[...], owners[...], lax.axis_index("c8"), lax.axis_index("x")
-    )
-    return landing((request % 2) * 16 + request // 2, prompts)
-
-
-def attend_prompts(blocks, queries, lengths, owners, result, stats):
-    row = iota((128, 1), 0)
-    landed, start, length = own_prompts(row, lengths, owners)
-    keys = jnp.concatenate([blocks[2 * x] for x in range(4)], axis=0)
-    values = jnp.concatenate([blocks[2 * x + 1] for x in range(4)], axis=0)
-    query = jnp.concatenate([queries[:, HD * i : HD * (i + 1)] for i in range(4)], axis=0)
-    score = transposed(query, keys) * SCALE
-    position = iota((128, 256), 1).astype(F32)
-    alive = (position >= start) & (position < start + length)
-    highest = jnp.max(jnp.where(alive, score, LOWEST), axis=1, keepdims=True)
-    exponent = jnp.where(alive, jnp.exp(score - highest), 0.0)
-    result[...] = jnp.dot(exponent.astype(BF16), values, preferred_element_type=F32)
-    total = jnp.sum(exponent, axis=1, keepdims=True)
-    lane = iota((128, HD), 1)
-    stats[...] = jnp.where(lane == 0, highest, jnp.where(lane == 1, total, landed))
-
-
-def finish(masked, received, queries, result, stats, logprob, attended, values, sems):
+def finish_logprob(masked, received, logprob, values, sems):
     lines = received[:, 8, :].astype(F32)
     take = lambda k: lines[:, 32 * k : 32 * (k + 1)]
     peak, total = take(0), take(1) + take(2) + take(3)
@@ -262,8 +241,19 @@
             )
         )
         copies[-1].start()
+    for copy in copies:
+        copy.wait()
+
+
+def attend_landed(mine, other, queries, received, lengths, owners, out):
+    turn = lax.axis_index("x")
+    prompts = prompts_of(lengths[...], owners[...], lax.axis_index("c8"), turn)
     row = iota((128, 1), 0)
     head, request = row // 32, row % 32
+    landed, start, length = landing((request % 2) * 16 + request // 2, prompts)
+    even = lax.axis_index("zl") == 0
+    keys = jnp.where(even, mine[...], other[...])
+    values = jnp.where(even, other[...], mine[...])
     query = jnp.concatenate([queries[:, HD * i : HD * (i + 1)] for i in range(4)], axis=0)
     table = received[...].reshape(256, HD)
     slot = (request // 2) * 16
@@ -271,16 +261,15 @@
     own_value = pick(slot + 1, table)
     cached = pick(slot + (request % 2) * 4 + head, table)
     own = jnp.sum(query.astype(F32) * own_key, axis=1, keepdims=True) * SCALE
-    top, total, landed = stats[:, 0:1], stats[:, 1:2], stats[:, 2:3]
-    highest = jnp.maximum(top, own)
-    share, own_share = jnp.exp(top - highest), jnp.exp(own - highest)
-    scale = 1.0 / (total * share + own_share)
-    merged = (result[...] * share + own_value * own_share) * scale
-    merged = jnp.where(landed > 0.5, merged, cached).astype(BF16)
+    score = transposed(query, keys) * SCALE
+    lane = iota((128, 256), 1)
+    position = ((turn + 4 - lane // 64) % 4 * 64 + lane % 64).astype(F32)
+    alive = (position >= start) & (position < start + length)
+    weight, own_weight = softmax(score, own, alive)
+    result = jnp.dot(weight, values, preferred_element_type=F32) + own_weight * own_value
+    result = jnp.where(landed > 0.5, result, cached).astype(BF16)
     for i in range(4):
-        attended[:, HD * i : HD * (i + 1)] = merged[32 * i : 32 * (i + 1)]
-    for copy in copies:
-        copy.wait()
+        out[:, HD * i : HD * (i + 1)] = result[32 * i : 32 * (i + 1)]
 
 
 def exchanged(slots, axis):
@@ -322,20 +311,13 @@
         name="prepare",
     )(hidden, queries, fresh)
     shares[1:] = [lax.ppermute(shares[k], "x", [(0, k)]) for k in (1, 2, 3)]
-    weight = pl.pallas_call(
-        fetch,
-        out_shape=kept(w_kv.shape, BF16),
-        in_specs=[hbm],
-        out_specs=vmem,
-        scratch_shapes=[pltpu.SemaphoreType.DMA],
-        name="fetch",
-    )(w_kv)
     projected = pl.pallas_call(
         project,
         out_shape=sent((16, 80, HD), BF16),
-        in_specs=[vmem] * 6,
+        in_specs=[vmem] * 5 + [hbm],
+        scratch_shapes=[pltpu.VMEM(w_kv.shape, BF16), pltpu.SemaphoreType.DMA((4,))],
         name="project",
-    )(*held(*shares, weight, asked))
+    )(*held(*shares, asked), w_kv)
     pieces = exchanged(projected, TP)
     masked, terms = pl.pallas_call(
         grammar,
@@ -344,13 +326,6 @@
         out_specs=[vmem] * 2,
         name="grammar",
     )(*held(logits, states.reshape(1, -1), masks))
-    blocks = pl.pallas_call(
-        reduce_blocks,
-        out_shape=sent((8, tokens, HD), BF16),
-        in_specs=[vmem],
-        name="reduce",
-    )(*held(pieces))
-    blocks = exchanged(blocks, ("x", "zl"))
     answers = pl.pallas_call(
         attend_cached,
         out_shape=sent((16, 16, HD), BF16),
@@ -358,21 +333,33 @@
         name="cached",
     )(cache_len, *held(pieces, cache, terms, prompt_lengths, owner_step))
     answers = exchanged(answers, TP)
-    result, stats = pl.pallas_call(
-        attend_prompts,
-        out_shape=[kept((128, HD), F32), kept((128, HD), F32)],
-        in_specs=[vmem] * 4,
-        out_specs=[vmem] * 2,
-        name="prompts",
-    )(*held(blocks, queries, prompt_lengths, owner_step))
-    logprob, attended = pl.pallas_call(
-        finish,
-        out_shape=[sent(logits.shape, F32), sent(queries.shape, BF16)],
-        in_specs=[vmem] * 5,
-        out_specs=[hbm, vmem],
+    block = pl.pallas_call(
+        reduce_blocks,
+        out_shape=kept((tokens, HD), BF16),
+        in_specs=[vmem],
+        out_specs=vmem,
+        name="reduce",
+    )(*held(pieces))
+    around = [
+        lax.ppermute(block, "x", [(i, (i + k) % 4) for i in range(4) if (i + k) % 4])
+        for k in (1, 2, 3)
+    ]
+    mine = jnp.concatenate([block] + around, axis=0)
+    other = lax.ppermute(mine, "zl", [(0, 1), (1, 0)])
+    logprob = pl.pallas_call(
+        finish_logprob,
+        out_shape=sent(logits.shape, F32),
+        in_specs=[vmem] * 2,
+        out_specs=hbm,
         scratch_shapes=[pltpu.VMEM(logits.shape, F32), pltpu.SemaphoreType.DMA((4,))],
-        name="finish",
-    )(*held(masked, answers, queries, result, stats))
+        name="logprob",
+    )(*held(masked, answers))
+    attended = pl.pallas_call(
+        attend_landed,
+        out_shape=sent(queries.shape, BF16),
+        in_specs=[vmem] * 6,
+        name="landed",
+    )(*held(mine, other, queries, answers, prompt_lengths, owner_step))
     return attended, logprob
 
 

time: 81.4 us -> 78.2 us (0.961)
  blocking collectives: 35.7 us -> 0 us
  starting transfers between devices: 18 us -> 41.6 us
  waiting for transfers between devices: 15 us -> 23.7 us
    all_to_all x1 -> x0, blocking collectives: 35.7 us -> none  [exchanged(): return lax.all_to_all(slots, axis, 0, 0, tiled=True)]
    ppermute x0 -> x4, starting transfers between devices: none -> 13.7 us  [the longest x3 9.87 us: per_device(): lax.ppermute(block, 'x', [(i, (i + k) % 4) for i in range(4) if (i + k) %...]
    all_to_all x2, starting transfers between devices: 11.1 us -> 21.1 us  [exchanged(): return lax.all_to_all(slots, axis, 0, 0, tiled=True)]
    ppermute x0 -> x4, waiting for transfers between devices: none -> 3.73 us  [the longest x1 2.32 us: per_device(): other = lax.ppermute(mine, 'zl', [(0, 1), (1, 0)])]
    all_to_all x2, waiting for transfers between devices: 14.7 us -> 18.1 us  [exchanged(): return lax.all_to_all(slots, axis, 0, 0, tiled=True)]
    pallas_call x4 -> x3, Pallas kernels: 4.73 us -> 2.57 us  [the longest x1 1.38 us: per_device(): pl.pallas_call(finish_logprob, out_shape=sent(logits.shape, F32), in_spec...]
    ppermute x3, waiting for transfers between devices: 0.23 us -> 1.88 us  [per_device(): shares[1:] = [lax.ppermute(shares[k], 'x', [(0, k)]) for k in (1, 2, 3)]]
    pallas_call x1, Pallas kernels: 1.2 us -> 2.65 us  [per_device(): pl.pallas_call(project, out_shape=sent((16, 80, HD), BF16), in_specs=[vme...]
  transfers between devices with their start and end apart: 5 -> 9, of which waited for: 3 -> 5; matrix products, arithmetic and copies ran while one was open for 0% -> 0% of each run, Pallas kernels for 7% -> 2%
where the time goes in v3:
time: 78.2 us; the launch traced here: 76.9 us
  starting transfers between devices  41.6 us (53%)
  waiting for transfers between devices  23.7 us (30%)
  Pallas kernels  9.82 us (13%)
  between operations  0.86 us (1%)
  local copies, waits for them, and re-layouts  0.81 us (1%)
    all_to_all x2, starting transfers between devices, exchanged(): return lax.all_to_all(slots, axis, 0, 0, tiled=True)  21.1 us
    all_to_all x2, waiting for transfers between devices, exchanged(): return lax.all_to_all(slots, axis, 0, 0, tiled=True)  18.1 us
    ppermute x3, starting transfers between devices, per_device(): lax.ppermute(block, 'x', [(i, (i + k) % 4) for i in range(4) if (i + k) %...  9.87 us
    ppermute x3, starting transfers between devices, per_device(): shares[1:] = [lax.ppermute(shares[k], 'x', [(0, k)]) for k in (1, 2, 3)]  6.89 us
    ppermute x1, starting transfers between devices, per_device(): other = lax.ppermute(mine, 'zl', [(0, 1), (1, 0)])  3.82 us
    pallas_call x1, Pallas kernels, per_device(): pl.pallas_call(project, out_shape=sent((16, 80, HD), BF16), in_specs=[vme...  2.65 us
    ppermute x1, waiting for transfers between devices, per_device(): other = lax.ppermute(mine, 'zl', [(0, 1), (1, 0)])  2.32 us
    pallas_call x1, Pallas kernels, per_device(): pl.pallas_call(attend_cached, out_shape=sent((16, 16, HD), BF16), in_spec...  2.18 us
  transfers between devices with their start and end apart: 9, of which 5 were waited for; matrix products, arithmetic and copies ran while one was open for 0% of the time, Pallas kernels for 2%

profile of v3, /device:TPU:24, one launch (start us, length us, event | category | flops | bytes accessed | tf_op | source)
XLA Modules:
  0.0 76.9 jit_solution(6250989926435767621)
XLA Ops:
  0.6 0.0 copy-start.5
  0.6 0.0 copy-start.8
  0.7 0.0 copy-start.1
  0.7 0.0 copy-start.7
  0.7 0.0 copy-start.6
  0.7 0.0 copy-start
  0.7 1.1 %prepare.1 = (bf16[64,512]{1,0:T(8,128)(2,1)S(1)}, bf16[64,512]{1,0:T(8,128)(2,1)S(1)}, bf16[64,512]{1,0:T(8,128)(2,1)S(1)}, bf16[64,512]{1,0:T(8,128)(2,1)S(1)}, bf16[16,16,128]{2,1,0:T(8,128)(2,1)S(1)}) custom-call(bf16[256,512]{1,0:T(8,128)(2,1)} %hidden.1, bf16[32,512]{1,0:T(8,128)(2,1)} %queries.3, bf16[32,128]{1,0:T(8,128)(2,1)} %fresh.1), custom_call_target="tpu_custom_call" | custom-call | tf_op jit(solution)/shard_map/prepare/pallas_call | solution.py:301
  1.8 3.4 %collective-permute-start = (bf16[64,512]{1,0:T(8,128)(2,1)S(1)}, bf16[64,512]{1,0:T(8,128)(2,1)S(1)}, u32[]{:S(2)}, u32[]{:S(2)}) collective-permute-start(bf16[64,512]{1,0:T(8,128)(2,1)S(1)} %get-tuple-element.10), channel_id=1, source_target_pairs={{0,128},{1,129},{2,130},{3,131},{4,132},{5,133},{6,134},{7,135},{8... | collective-permute-start | bytes 196616 | tf_op jit(solution)/shard_map/ppermute | solution.py:313
  5.2 2.2 %collective-permute-start.1 = (bf16[64,512]{1,0:T(8,128)(2,1)S(1)}, bf16[64,512]{1,0:T(8,128)(2,1)S(1)}, u32[]{:S(2)}, u32[]{:S(2)}) collective-permute-start(bf16[64,512]{1,0:T(8,128)(2,1)S(1)} %get-tuple-element.11), channel_id=1, source_target_pairs={{0,256},{1,257},{2,258},{3,259},{4,260},{5,261},{6,262},{7,263},{8... | collective-permute-start | bytes 196616 | tf_op jit(solution)/shard_map/ppermute | solution.py:313
  7.4 1.3 %collective-permute-start.2 = (bf16[64,512]{1,0:T(8,128)(2,1)S(1)}, bf16[64,512]{1,0:T(8,128)(2,1)S(1)}, u32[]{:S(2)}, u32[]{:S(2)}) collective-permute-start(bf16[64,512]{1,0:T(8,128)(2,1)S(1)} %get-tuple-element.12), channel_id=1, source_target_pairs={{0,384},{1,385},{2,386},{3,387},{4,388},{5,389},{6,390},{7,391},{8... | collective-permute-start | bytes 196616 | tf_op jit(solution)/shard_map/ppermute | solution.py:313
  8.7 0.0 collective-permute-done.first
  8.8 0.6 collective-permute-done.1.second
  9.3 1.3 %collective-permute-done.2.third = bf16[64,512]{1,0:T(8,128)(2,1)S(1)} collective-permute-done((bf16[64,512]{1,0:T(8,128)(2,1)S(1)}, bf16[64,512]{1,0:T(8,128)(2,1)S(1)}, u32[]{:S(2)}, u32[]{:S(2)}) %collective-permute-start.2) | collective-permute-done | bytes 65568 | tf_op jit(solution)/shard_map/ppermute | solution.py:313
  10.6 2.6 %project.1 = bf16[16,80,128]{2,1,0:T(8,128)(2,1)} custom-call(bf16[64,512]{1,0:T(8,128)(2,1)S(1)} %get-tuple-element.9.own, bf16[64,512]{1,0:T(8,128)(2,1)S(1)} %collective-permute-done.first, bf16[64,512]{1,0:T(8,128)(2,1)S(1)} %collective-permute-done.1.second, bf16[64,512]{1,0:T(8,128)(2,1)S(1)} %collective-permute-done.2.third, ...), custom_call_target="tpu_custom_call" | custom-call | tf_op jit(solution)/shard_map/project/pallas_call | solution.py:314
  13.3 0.0 copy-start.4
  13.3 15.2 %all-to-all-start = ((bf16[16,80,128]{2,1,0:T(8,128)(2,1)}), bf16[16,80,128]{2,1,0:T(8,128)(2,1)S(1)}, u32[]{:S(2)}, u32[]{:S(2)}) async-start(bf16[16,80,128]{2,1,0:T(8,128)(2,1)} %project.1), calls=%async_computation | async-start | bytes 655360 | tf_op jit(solution)/shard_map/all_to_all | solution.py:276
  28.5 0.0 copy-done.5
  28.5 0.0 copy-done.8
  28.5 0.0 copy-done.1
  28.5 1.3 %grammar.1 = (bf16[32,7680]{1,0:T(8,128)(2,1)S(1)}, bf16[16,128]{1,0:T(8,128)(2,1)S(1)}) custom-call(bf16[32,7680]{1,0:T(8,128)(2,1)S(1)} %copy-done.1, s32[1,32]{1,0:T(1,128)S(1)} %bitcast.1, s32[24,256]{1,0:T(8,128)S(1)} %copy-done.5), custom_call_target="tpu_custom_call" | custom-call | tf_op jit(solution)/shard_map/grammar/pallas_call | solution.py:322
  29.9 0.0 copy-start.2
  29.9 0.8 %copy-done.2 = bf16[32,7680]{1,0:T(8,128)(2,1)} copy-done((bf16[32,7680]{1,0:T(8,128)(2,1)}, bf16[32,7680]{1,0:T(8,128)(2,1)S(1)}, u32[]{:S(2)}) %copy-start.2) | copy-done | bytes 491544
  30.6 18.1 %all-to-all-done.pieces.received = bf16[16,80,128]{2,1,0:T(8,128)(2,1)S(1)} async-done(((bf16[16,80,128]{2,1,0:T(8,128)(2,1)}), bf16[16,80,128]{2,1,0:T(8,128)(2,1)S(1)}, u32[]{:S(2)}, u32[]{:S(2)}) %all-to-all-start) | async-done | bytes 327712 | tf_op jit(solution)/shard_map/all_to_all | solution.py:276
  48.8 0.0 copy-start.3
  48.8 0.0 copy-done.7
  48.8 0.0 copy-done.6
  48.8 0.0 copy-done
  48.8 2.2 %cached.1 = bf16[16,16,128]{2,1,0:T(8,128)(2,1)} custom-call(s32[2]{0:T(128)} %cache_len.1, bf16[16,80,128]{2,1,0:T(8,128)(2,1)S(1)} %all-to-all-done.pieces.received, bf16[2,128,2048]{2,1,0:T(8,128)(2,1)S(1)} %copy-done, bf16[16,128]{1,0:T(8,128)(2,1)S(1)} %get-tuple-element.14.terms, s32[8,16]{1,0:T(8,128)S(1)} %copy-done.6, s32[8,16]{1,0:T(8,128)S(1)} %copy-done.7), custom_call_target="tpu_custom_call" | custom-call | tf_op jit(solution)/shard_map/cached/pallas_call | solution.py:329
  51.0 5.9 %all-to-all-start.1 = ((bf16[16,16,128]{2,1,0:T(8,128)(2,1)}), bf16[16,16,128]{2,1,0:T(8,128)(2,1)S(1)}, u32[]{:S(2)}, u32[]{:S(2)}) async-start(bf16[16,16,128]{2,1,0:T(8,128)(2,1)} %cached.1), calls=%async_computation.1 | async-start | bytes 131072 | tf_op jit(solution)/shard_map/all_to_all | solution.py:276
  56.9 5.2 %collective-permute-start.5 = (bf16[64,128]{1,0:T(8,128)(2,1)S(1)}, bf16[64,128]{1,0:T(8,128)(2,1)S(1)}, u32[]{:S(2)}, u32[]{:S(2)}) collective-permute-start(bf16[64,128]{1,0:T(8,128)(2,1)S(1)} %reduce.1), channel_id=1, source_target_pairs={{0,384},{256,128},{384,256},{1,385},{257,129},{385,257},{2,386},{2... | collective-permute-start | bytes 49160 | tf_op jit(solution)/shard_map/ppermute | solution.py:344
  62.1 1.3 %collective-permute-start.4 = (bf16[64,128]{1,0:T(8,128)(2,1)S(1)}, bf16[64,128]{1,0:T(8,128)(2,1)S(1)}, u32[]{:S(2)}, u32[]{:S(2)}) collective-permute-start(bf16[64,128]{1,0:T(8,128)(2,1)S(1)} %reduce.1), channel_id=1, source_target_pairs={{0,256},{128,384},{384,128},{1,257},{129,385},{385,129},{2,258},{1... | collective-permute-start | bytes 49160 | tf_op jit(solution)/shard_map/ppermute | solution.py:344
  63.4 3.4 %collective-permute-start.3 = (bf16[64,128]{1,0:T(8,128)(2,1)S(1)}, bf16[64,128]{1,0:T(8,128)(2,1)S(1)}, u32[]{:S(2)}, u32[]{:S(2)}) collective-permute-start(bf16[64,128]{1,0:T(8,128)(2,1)S(1)} %reduce.1), channel_id=1, source_target_pairs={{0,128},{128,256},{256,384},{1,129},{129,257},{257,385},{2,130},{1... | collective-permute-start | bytes 49160 | tf_op jit(solution)/shard_map/ppermute | solution.py:344
  66.8 0.0 collective-permute-done.5
  66.8 0.0 collective-permute-done.4
  66.8 1.4 %collective-permute-done.3 = bf16[64,128]{1,0:T(8,128)(2,1)S(1)} collective-permute-done((bf16[64,128]{1,0:T(8,128)(2,1)S(1)}, bf16[64,128]{1,0:T(8,128)(2,1)S(1)}, u32[]{:S(2)}, u32[]{:S(2)}) %collective-permute-start.3) | collective-permute-done | bytes 16416 | tf_op jit(solution)/shard_map/ppermute | solution.py:344
  68.2 3.8 %collective-permute-start.6 = (bf16[256,128]{1,0:T(8,128)(2,1)S(1)}, bf16[256,128]{1,0:T(8,128)(2,1)S(1)}, u32[]{:S(2)}, u32[]{:S(2)}) collective-permute-start(bf16[256,128]{1,0:T(8,128)(2,1)S(1)} %pad_maximum_fusion.mine), channel_id=1, source_target_pairs={{0,1},{1,0},{2,3},{3,2},{4,5},{5,4},{6,7},{7,6},{8,9},{9,8},{10,11... | collective-permute-start | bytes 196616 | tf_op jit(solution)/shard_map/ppermute | solution.py:348
  72.0 2.3 %collective-permute-done.6.other = bf16[256,128]{1,0:T(8,128)(2,1)S(1)} collective-permute-done((bf16[256,128]{1,0:T(8,128)(2,1)S(1)}, bf16[256,128]{1,0:T(8,128)(2,1)S(1)}, u32[]{:S(2)}, u32[]{:S(2)}) %collective-permute-start.6) | collective-permute-done | bytes 65568 | tf_op jit(solution)/shard_map/ppermute | solution.py:348
  74.3 0.0 all-to-all-done.1.received
  74.3 0.0 copy-done.4
  74.3 1.1 %landed.1 = bf16[32,512]{1,0:T(8,128)(2,1)} custom-call(bf16[256,128]{1,0:T(8,128)(2,1)S(1)} %pad_maximum_fusion.mine, bf16[256,128]{1,0:T(8,128)(2,1)S(1)} %collective-permute-done.6.other, bf16[32,512]{1,0:T(8,128)(2,1)S(1)} %copy-done.4, bf16[16,16,128]{2,1,0:T(8,128)(2,1)S(1)} %all-to-all-done.1.received, s32[8,16]{1,0:T(8,128)S(1)} %copy-done.6, ...), custom_call_target="tpu_custom_call" | custom-call | tf_op jit(solution)/shard_map/landed/pallas_call | solution.py:357
  75.5 0.0 copy-done.3
  75.5 1.4 %logprob.1 = f32[32,7680]{1,0:T(8,128)} custom-call(bf16[32,7680]{1,0:T(8,128)(2,1)S(1)} %copy-done.3, bf16[16,16,128]{2,1,0:T(8,128)(2,1)S(1)} %all-to-all-done.1.received), custom_call_target="tpu_custom_call" | custom-call | tf_op jit(solution)/shard_map/logprob/pallas_call | solution.py:349
  (2 shorter events, 0.0 us)
Async XLA Ops:
  0.6 27.9 %copy-start.5 = (s32[24,256]{1,0:T(8,128)S(1)}, s32[24,256]{1,0:T(8,128)}, u32[]{:S(2)}) copy-start(s32[24,256]{1,0:T(8,128)} %masks.1) | copy-start | bytes 73732
  0.6 27.9 %copy-start.8 = (s32[32]{0:T(128)S(1)}, s32[32]{0:T(128)}, u32[]{:S(2)}) copy-start(s32[32]{0:T(128)} %param.20) | copy-start | bytes 388
  0.7 27.9 %copy-start.1 = (bf16[32,7680]{1,0:T(8,128)(2,1)S(1)}, bf16[32,7680]{1,0:T(8,128)(2,1)}, u32[]{:S(2)}) copy-start(bf16[32,7680]{1,0:T(8,128)(2,1)} %logits.1) | copy-start | bytes 1474564
  0.7 48.1 %copy-start.7 = (s32[8,16]{1,0:T(8,128)S(1)}, s32[8,16]{1,0:T(8,128)}, u32[]{:S(2)}) copy-start(s32[8,16]{1,0:T(8,128)} %owners.3) | copy-start | bytes 1540
  0.7 48.1 %copy-start.6 = (s32[8,16]{1,0:T(8,128)S(1)}, s32[8,16]{1,0:T(8,128)}, u32[]{:S(2)}) copy-start(s32[8,16]{1,0:T(8,128)} %lengths.3) | copy-start | bytes 1540
  0.7 48.1 %copy-start = (bf16[2,128,2048]{2,1,0:T(8,128)(2,1)S(1)}, bf16[2,128,2048]{2,1,0:T(8,128)(2,1)}, u32[]{:S(2)}) copy-start(bf16[2,128,2048]{2,1,0:T(8,128)(2,1)} %cache.1) | copy-start | bytes 3145732
  1.8 6.9 %collective-permute-start = (bf16[64,512]{1,0:T(8,128)(2,1)S(1)}, bf16[64,512]{1,0:T(8,128)(2,1)S(1)}, u32[]{:S(2)}, u32[]{:S(2)}) collective-permute-start(bf16[64,512]{1,0:T(8,128)(2,1)S(1)} %get-tuple-element.10), channel_id=1, source_target_pairs={{0,128},{1,129},{2,130},{3,131},{4,132},{5,133},{6,134},{7,135},{8... | collective-permute-start | bytes 196616 | tf_op jit(solution)/shard_map/ppermute | solution.py:313
  5.2 4.1 %collective-permute-start.1 = (bf16[64,512]{1,0:T(8,128)(2,1)S(1)}, bf16[64,512]{1,0:T(8,128)(2,1)S(1)}, u32[]{:S(2)}, u32[]{:S(2)}) collective-permute-start(bf16[64,512]{1,0:T(8,128)(2,1)S(1)} %get-tuple-element.11), channel_id=1, source_target_pairs={{0,256},{1,257},{2,258},{3,259},{4,260},{5,261},{6,262},{7,263},{8... | collective-permute-start | bytes 196616 | tf_op jit(solution)/shard_map/ppermute | solution.py:313
  7.4 3.2 %collective-permute-start.2 = (bf16[64,512]{1,0:T(8,128)(2,1)S(1)}, bf16[64,512]{1,0:T(8,128)(2,1)S(1)}, u32[]{:S(2)}, u32[]{:S(2)}) collective-permute-start(bf16[64,512]{1,0:T(8,128)(2,1)S(1)} %get-tuple-element.12), channel_id=1, source_target_pairs={{0,384},{1,385},{2,386},{3,387},{4,388},{5,389},{6,390},{7,391},{8... | collective-permute-start | bytes 196616 | tf_op jit(solution)/shard_map/ppermute | solution.py:313
  13.3 61.1 %copy-start.4 = (bf16[32,512]{1,0:T(8,128)(2,1)S(1)}, bf16[32,512]{1,0:T(8,128)(2,1)}, u32[]{:S(2)}) copy-start(bf16[32,512]{1,0:T(8,128)(2,1)} %queries.3) | copy-start | bytes 98308
  13.3 35.5 %all-to-all-start = ((bf16[16,80,128]{2,1,0:T(8,128)(2,1)}), bf16[16,80,128]{2,1,0:T(8,128)(2,1)S(1)}, u32[]{:S(2)}, u32[]{:S(2)}) async-start(bf16[16,80,128]{2,1,0:T(8,128)(2,1)} %project.1), calls=%async_computation | async-start | bytes 655360 | tf_op jit(solution)/shard_map/all_to_all | solution.py:276
  29.9 0.8 %copy-start.2 = (bf16[32,7680]{1,0:T(8,128)(2,1)}, bf16[32,7680]{1,0:T(8,128)(2,1)S(1)}, u32[]{:S(2)}) copy-start(bf16[32,7680]{1,0:T(8,128)(2,1)S(1)} %get-tuple-element.15.masked) | copy-start | bytes 1474564
  48.8 26.7 %copy-start.3 = (bf16[32,7680]{1,0:T(8,128)(2,1)S(1)}, bf16[32,7680]{1,0:T(8,128)(2,1)}, u32[]{:S(2)}) copy-start(bf16[32,7680]{1,0:T(8,128)(2,1)} %copy-done.2) | copy-start | bytes 1474564
  51.0 23.4 %all-to-all-start.1 = ((bf16[16,16,128]{2,1,0:T(8,128)(2,1)}), bf16[16,16,128]{2,1,0:T(8,128)(2,1)S(1)}, u32[]{:S(2)}, u32[]{:S(2)}) async-start(bf16[16,16,128]{2,1,0:T(8,128)(2,1)} %cached.1), calls=%async_computation.1 | async-start | bytes 131072 | tf_op jit(solution)/shard_map/all_to_all | solution.py:276
  56.9 9.9 %collective-permute-start.5 = (bf16[64,128]{1,0:T(8,128)(2,1)S(1)}, bf16[64,128]{1,0:T(8,128)(2,1)S(1)}, u32[]{:S(2)}, u32[]{:S(2)}) collective-permute-start(bf16[64,128]{1,0:T(8,128)(2,1)S(1)} %reduce.1), channel_id=1, source_target_pairs={{0,384},{256,128},{384,256},{1,385},{257,129},{385,257},{2,386},{2... | collective-permute-start | bytes 49160 | tf_op jit(solution)/shard_map/ppermute | solution.py:344
  62.1 4.7 %collective-permute-start.4 = (bf16[64,128]{1,0:T(8,128)(2,1)S(1)}, bf16[64,128]{1,0:T(8,128)(2,1)S(1)}, u32[]{:S(2)}, u32[]{:S(2)}) collective-permute-start(bf16[64,128]{1,0:T(8,128)(2,1)S(1)} %reduce.1), channel_id=1, source_target_pairs={{0,256},{128,384},{384,128},{1,257},{129,385},{385,129},{2,258},{1... | collective-permute-start | bytes 49160 | tf_op jit(solution)/shard_map/ppermute | solution.py:344
  63.4 4.8 %collective-permute-start.3 = (bf16[64,128]{1,0:T(8,128)(2,1)S(1)}, bf16[64,128]{1,0:T(8,128)(2,1)S(1)}, u32[]{:S(2)}, u32[]{:S(2)}) collective-permute-start(bf16[64,128]{1,0:T(8,128)(2,1)S(1)} %reduce.1), channel_id=1, source_target_pairs={{0,128},{128,256},{256,384},{1,129},{129,257},{257,385},{2,130},{1... | collective-permute-start | bytes 49160 | tf_op jit(solution)/shard_map/ppermute | solution.py:344
  68.2 6.1 %collective-permute-start.6 = (bf16[256,128]{1,0:T(8,128)(2,1)S(1)}, bf16[256,128]{1,0:T(8,128)(2,1)S(1)}, u32[]{:S(2)}, u32[]{:S(2)}) collective-permute-start(bf16[256,128]{1,0:T(8,128)(2,1)S(1)} %pad_maximum_fusion.mine), channel_id=1, source_target_pairs={{0,1},{1,0},{2,3},{3,2},{4,5},{5,4},{6,7},{7,6},{8,9},{9,8},{10,11... | collective-permute-start | bytes 196616 | tf_op jit(solution)/shard_map/ppermute | solution.py:348

commit v4 on v3

--- a/solution.py
+++ b/solution.py
@@ -82,27 +82,20 @@
         copy.wait()
 
 
-def project(own, first, second, third, asked, weight, out, held, sems):
-    width = weight.shape[1] // 4
-    loads = [
-        pltpu.make_async_copy(
-            weight.at[:, pl.ds(width * k, width)], held.at[:, pl.ds(width * k, width)], sems.at[k]
-        )
-        for k in range(4)
-    ]
-    for load in loads:
-        load.start()
+def fetch(weight, out, sem):
+    copy = pltpu.make_async_copy(weight, out, sem)
+    copy.start()
+    copy.wait()
+
+
+def project(own, first, second, third, asked, weight, out):
     turn = lax.axis_index("x")
     tokens = jnp.where(turn == 0, own[...], first[...] + second[...] + third[...])
+    full = jnp.dot(tokens, weight[...], preferred_element_type=F32).astype(BF16)
     out[:, 64:80] = asked[...]
-    for k in range(4):
-        loads[k].wait()
-        part = held[:, width * k : width * (k + 1)]
-        part = jnp.dot(tokens, part, preferred_element_type=F32).astype(BF16)
-        for i in range(4):
-            block = 4 * k + i
-            c = 2 * (block % KVH) + block // KVH
-            out[c, 0:64] = part[:, HD * i : HD * (i + 1)]
+    for c in range(16):
+        block = c // 2 + (c % 2) * KVH
+        out[c, 0:64] = full[:, HD * block : HD * (block + 1)]
 
 
 def reduce_blocks(pieces, out):
@@ -245,15 +238,18 @@
         copy.wait()
 
 
-def attend_landed(mine, other, queries, received, lengths, owners, out):
+def attend_landed(here, second, first, third, queries, received, lengths, owners, out):
     turn = lax.axis_index("x")
     prompts = prompts_of(lengths[...], owners[...], lax.axis_index("c8"), turn)
     row = iota((128, 1), 0)
     head, request = row // 32, row % 32
     landed, start, length = landing((request % 2) * 16 + request // 2, prompts)
     even = lax.axis_index("zl") == 0
-    keys = jnp.where(even, mine[...], other[...])
-    values = jnp.where(even, other[...], mine[...])
+    parts = (here, first, second, third)
+    mine = jnp.concatenate([part[0:64] for part in parts], axis=0)
+    other = jnp.concatenate([part[64:128] for part in parts], axis=0)
+    keys = jnp.where(even, mine, other)
+    values = jnp.where(even, other, mine)
     query = jnp.concatenate([queries[:, HD * i : HD * (i + 1)] for i in range(4)], axis=0)
     table = received[...].reshape(256, HD)
     slot = (request // 2) * 16
@@ -310,14 +306,22 @@
         ],
         name="prepare",
     )(hidden, queries, fresh)
-    shares[1:] = [lax.ppermute(shares[k], "x", [(0, k)]) for k in (1, 2, 3)]
+    for k in (2, 1, 3):
+        shares[k] = lax.ppermute(shares[k], "x", [(0, k)])
+    weight = pl.pallas_call(
+        fetch,
+        out_shape=kept(w_kv.shape, BF16),
+        in_specs=[hbm],
+        out_specs=vmem,
+        scratch_shapes=[pltpu.SemaphoreType.DMA],
+        name="fetch",
+    )(w_kv)
     projected = pl.pallas_call(
         project,
         out_shape=sent((16, 80, HD), BF16),
-        in_specs=[vmem] * 5 + [hbm],
-        scratch_shapes=[pltpu.VMEM(w_kv.shape, BF16), pltpu.SemaphoreType.DMA((4,))],
+        in_specs=[vmem] * 6,
         name="project",
-    )(*held(*shares, asked), w_kv)
+    )(*held(*shares, asked, weight))
     pieces = exchanged(projected, TP)
     masked, terms = pl.pallas_call(
         grammar,
@@ -326,6 +330,14 @@
         out_specs=[vmem] * 2,
         name="grammar",
     )(*held(logits, states.reshape(1, -1), masks))
+    block = pl.pallas_call(
+        reduce_blocks,
+        out_shape=kept((tokens, HD), BF16),
+        in_specs=[vmem],
+        out_specs=vmem,
+        name="reduce",
+    )(*held(pieces))
+    other = lax.ppermute(block, "zl", [(0, 1), (1, 0)])
     answers = pl.pallas_call(
         attend_cached,
         out_shape=sent((16, 16, HD), BF16),
@@ -333,19 +345,11 @@
         name="cached",
     )(cache_len, *held(pieces, cache, terms, prompt_lengths, owner_step))
     answers = exchanged(answers, TP)
-    block = pl.pallas_call(
-        reduce_blocks,
-        out_shape=kept((tokens, HD), BF16),
-        in_specs=[vmem],
-        out_specs=vmem,
-        name="reduce",
-    )(*held(pieces))
-    around = [
-        lax.ppermute(block, "x", [(i, (i + k) % 4) for i in range(4) if (i + k) % 4])
-        for k in (1, 2, 3)
-    ]
-    mine = jnp.concatenate([block] + around, axis=0)
-    other = lax.ppermute(mine, "zl", [(0, 1), (1, 0)])
+    both = jnp.concatenate([block, other], axis=0)
+    around = [both]
+    for k in (2, 1, 3):
+        route = [(i, (i + k) % 4) for i in range(4) if (i + k) % 4]
+        around.append(lax.ppermute(both, "x", route))
     logprob = pl.pallas_call(
         finish_logprob,
         out_shape=sent(logits.shape, F32),
@@ -357,9 +361,9 @@
     attended = pl.pallas_call(
         attend_landed,
         out_shape=sent(queries.shape, BF16),
-        in_specs=[vmem] * 6,
+        in_specs=[vmem] * 8,
         name="landed",
-    )(*held(mine, other, queries, answers, prompt_lengths, owner_step))
+    )(*held(*around, queries, answers, prompt_lengths, owner_step))
     return attended, logprob
 
 

time: 78.2 us -> 75.8 us (0.969)
  the two profiles are of different devices: /device:TPU:24 before, /device:TPU:26 now
where the time goes in v4:
time: 75.8 us; the launch traced here: 75.3 us
  starting transfers between devices  38.4 us (51%)
  waiting for transfers between devices  24.6 us (32%)
  Pallas kernels  10.4 us (14%)
  local copies, waits for them, and re-layouts  1.06 us (1%)
  between operations  0.83 us (1%)
    all_to_all x2, starting transfers between devices, exchanged(): return lax.all_to_all(slots, axis, 0, 0, tiled=True)  21.2 us
    all_to_all x2, waiting for transfers between devices, exchanged(): return lax.all_to_all(slots, axis, 0, 0, tiled=True)  17.4 us
    ppermute x3, starting transfers between devices, per_device(): around.append(lax.ppermute(both, 'x', route))  10.7 us
    ppermute x1, starting transfers between devices, per_device(): other = lax.ppermute(block, 'zl', [(0, 1), (1, 0)])  3.83 us
    ppermute x3, waiting for transfers between devices, per_device(): around.append(lax.ppermute(both, 'x', route))  3.11 us
    ppermute x3, starting transfers between devices, per_device(): shares[k] = lax.ppermute(shares[k], 'x', [(0, k)])  2.62 us
    ppermute x1, waiting for transfers between devices, per_device(): other = lax.ppermute(block, 'zl', [(0, 1), (1, 0)])  2.06 us
    ppermute x3, waiting for transfers between devices, per_device(): shares[k] = lax.ppermute(shares[k], 'x', [(0, k)])  2.06 us
  transfers between devices with their start and end apart: 9, of which 5 were waited for; matrix products, arithmetic and copies ran while one was open for 0% of the time, Pallas kernels for 6%

profile of v4, /device:TPU:26, one launch (start us, length us, event | category | flops | bytes accessed | tf_op | source)
XLA Modules:
  0.0 75.3 jit_solution(11807096253050744634)
XLA Ops:
  0.6 1.7 %prepare.1 = (bf16[64,512]{1,0:T(8,128)(2,1)S(1)}, bf16[64,512]{1,0:T(8,128)(2,1)}, bf16[64,512]{1,0:T(8,128)(2,1)}, bf16[64,512]{1,0:T(8,128)(2,1)}, bf16[16,16,128]{2,1,0:T(8,128)(2,1)S(1)}) custom-call(bf16[256,512]{1,0:T(8,128)(2,1)} %hidden.1, bf16[32,512]{1,0:T(8,128)(2,1)} %queries.3, bf16[32,128]{1,0:T(8,128)(2,1)} %fresh.1), custom_call_target="tpu_custom_call" | custom-call | tf_op jit(solution)/shard_map/prepare/pallas_call | solution.py:297
  2.3 1.3 %collective-permute-start = (bf16[64,512]{1,0:T(8,128)(2,1)}, bf16[64,512]{1,0:T(8,128)(2,1)S(1)}, u32[]{:S(2)}, u32[]{:S(2)}) collective-permute-start(bf16[64,512]{1,0:T(8,128)(2,1)} %get-tuple-element.10), channel_id=1, source_target_pairs={{0,128},{1,129},{2,130},{3,131},{4,132},{5,133},{6,134},{7,135},{8... | collective-permute-start | bytes 196616 | tf_op jit(solution)/shard_map/ppermute | solution.py:310
  3.6 0.7 collective-permute-start.1
  4.3 0.7 collective-permute-start.2
  5.0 1.6 %fetch.1.weight = bf16[512,2048]{1,0:T(8,128)(2,1)S(1)} custom-call(bf16[512,2048]{1,0:T(8,128)(2,1)} %weight.1), custom_call_target="tpu_custom_call" | custom-call | tf_op jit(solution)/shard_map/fetch/pallas_call | solution.py:311
  6.6 0.0 copy-start.3
  6.6 0.0 copy-start.6
  6.6 0.0 copy-start
  6.6 0.0 copy-start.4
  6.6 0.0 copy-start.5
  6.6 2.1 %collective-permute-done.first = bf16[64,512]{1,0:T(8,128)(2,1)S(1)} collective-permute-done((bf16[64,512]{1,0:T(8,128)(2,1)}, bf16[64,512]{1,0:T(8,128)(2,1)S(1)}, u32[]{:S(2)}, u32[]{:S(2)}) %collective-permute-start) | collective-permute-done | bytes 65568 | tf_op jit(solution)/shard_map/ppermute | solution.py:310
  8.7 0.0 collective-permute-done.1.second
  8.7 0.0 collective-permute-done.2.third
  8.7 1.2 %project.1 = bf16[16,80,128]{2,1,0:T(8,128)(2,1)} custom-call(bf16[64,512]{1,0:T(8,128)(2,1)S(1)} %get-tuple-element.9.own, bf16[64,512]{1,0:T(8,128)(2,1)S(1)} %collective-permute-done.first, bf16[64,512]{1,0:T(8,128)(2,1)S(1)} %collective-permute-done.1.second, bf16[64,512]{1,0:T(8,128)(2,1)S(1)} %collective-permute-done.2.third, ...), custom_call_target="tpu_custom_call" | custom-call | tf_op jit(solution)/shard_map/project/pallas_call | solution.py:319
  9.9 15.2 %all-to-all-start = ((bf16[16,80,128]{2,1,0:T(8,128)(2,1)}), bf16[16,80,128]{2,1,0:T(8,128)(2,1)S(1)}, u32[]{:S(2)}, u32[]{:S(2)}) async-start(bf16[16,80,128]{2,1,0:T(8,128)(2,1)} %project.1), calls=%async_computation | async-start | bytes 655360 | tf_op jit(solution)/shard_map/all_to_all | solution.py:272
  25.1 0.0 copy-done.3
  25.1 0.0 copy-done.6
  25.1 0.0 copy-start.1
  25.1 1.0 %copy-done.1 = bf16[32,7680]{1,0:T(8,128)(2,1)S(1)} copy-done((bf16[32,7680]{1,0:T(8,128)(2,1)S(1)}, bf16[32,7680]{1,0:T(8,128)(2,1)}, u32[]{:S(2)}) %copy-start.1) | copy-done | bytes 491544
  26.2 0.0 copy-start.2
  26.2 1.3 %grammar.1 = (bf16[32,7680]{1,0:T(8,128)(2,1)S(1)}, bf16[16,128]{1,0:T(8,128)(2,1)S(1)}) custom-call(bf16[32,7680]{1,0:T(8,128)(2,1)S(1)} %copy-done.1, s32[1,32]{1,0:T(1,128)S(1)} %bitcast.1, s32[24,256]{1,0:T(8,128)S(1)} %copy-done.3), custom_call_target="tpu_custom_call" | custom-call | tf_op jit(solution)/shard_map/grammar/pallas_call | solution.py:326
  27.5 17.4 %all-to-all-done.pieces.received = bf16[16,80,128]{2,1,0:T(8,128)(2,1)S(1)} async-done(((bf16[16,80,128]{2,1,0:T(8,128)(2,1)}), bf16[16,80,128]{2,1,0:T(8,128)(2,1)S(1)}, u32[]{:S(2)}, u32[]{:S(2)}) %all-to-all-start) | async-done | bytes 327712 | tf_op jit(solution)/shard_map/all_to_all | solution.py:272
  44.9 0.0 copy-done
  44.9 0.0 copy-done.4
  44.9 0.0 copy-done.5
  44.9 2.1 %cached.1 = bf16[16,16,128]{2,1,0:T(8,128)(2,1)} custom-call(s32[2]{0:T(128)} %cache_len.1, bf16[16,80,128]{2,1,0:T(8,128)(2,1)S(1)} %all-to-all-done.pieces.received, bf16[2,128,2048]{2,1,0:T(8,128)(2,1)S(1)} %copy-done, bf16[16,128]{1,0:T(8,128)(2,1)S(1)} %get-tuple-element.14.terms, s32[8,16]{1,0:T(8,128)S(1)} %copy-done.4, s32[8,16]{1,0:T(8,128)S(1)} %copy-done.5), custom_call_target="tpu_custom_call" | custom-call | tf_op jit(solution)/shard_map/cached/pallas_call | solution.py:341
  46.9 6.0 %all-to-all-start.1 = ((bf16[16,16,128]{2,1,0:T(8,128)(2,1)}), bf16[16,16,128]{2,1,0:T(8,128)(2,1)S(1)}, u32[]{:S(2)}, u32[]{:S(2)}) async-start(bf16[16,16,128]{2,1,0:T(8,128)(2,1)} %cached.1), calls=%async_computation.1 | async-start | bytes 131072 | tf_op jit(solution)/shard_map/all_to_all | solution.py:272
  53.0 3.8 %collective-permute-start.3 = (bf16[64,128]{1,0:T(8,128)(2,1)S(1)}, bf16[64,128]{1,0:T(8,128)(2,1)S(1)}, u32[]{:S(2)}, u32[]{:S(2)}) collective-permute-start(bf16[64,128]{1,0:T(8,128)(2,1)S(1)} %reduce.1), channel_id=1, source_target_pairs={{0,1},{1,0},{2,3},{3,2},{4,5},{5,4},{6,7},{7,6},{8,9},{9,8},{10,11... | collective-permute-start | bytes 49160 | tf_op jit(solution)/shard_map/ppermute | solution.py:340
  56.9 2.1 %collective-permute-done.3 = bf16[64,128]{1,0:T(8,128)(2,1)S(1)} collective-permute-done((bf16[64,128]{1,0:T(8,128)(2,1)S(1)}, bf16[64,128]{1,0:T(8,128)(2,1)S(1)}, u32[]{:S(2)}, u32[]{:S(2)}) %collective-permute-start.3) | collective-permute-done | bytes 16416 | tf_op jit(solution)/shard_map/ppermute | solution.py:340
  58.9 7.5 %collective-permute-start.4 = (bf16[128,128]{1,0:T(8,128)(2,1)S(1)}, bf16[128,128]{1,0:T(8,128)(2,1)S(1)}, u32[]{:S(2)}, u32[]{:S(2)}) collective-permute-start(bf16[128,128]{1,0:T(8,128)(2,1)S(1)} %pad_maximum_fusion.here), channel_id=1, source_target_pairs={{0,256},{128,384},{384,128},{1,257},{129,385},{385,129},{2,258},{1... | collective-permute-start | bytes 98312 | tf_op jit(solution)/shard_map/ppermute | solution.py:352
  66.4 1.9 %collective-permute-start.5 = (bf16[128,128]{1,0:T(8,128)(2,1)S(1)}, bf16[128,128]{1,0:T(8,128)(2,1)S(1)}, u32[]{:S(2)}, u32[]{:S(2)}) collective-permute-start(bf16[128,128]{1,0:T(8,128)(2,1)S(1)} %pad_maximum_fusion.here), channel_id=1, source_target_pairs={{0,128},{128,256},{256,384},{1,129},{129,257},{257,385},{2,130},{1... | collective-permute-start | bytes 98312 | tf_op jit(solution)/shard_map/ppermute | solution.py:352
  68.3 1.3 %collective-permute-start.6 = (bf16[128,128]{1,0:T(8,128)(2,1)S(1)}, bf16[128,128]{1,0:T(8,128)(2,1)S(1)}, u32[]{:S(2)}, u32[]{:S(2)}) collective-permute-start(bf16[128,128]{1,0:T(8,128)(2,1)S(1)} %pad_maximum_fusion.here), channel_id=1, source_target_pairs={{0,384},{256,128},{384,256},{1,385},{257,129},{385,257},{2,386},{2... | collective-permute-start | bytes 98312 | tf_op jit(solution)/shard_map/ppermute | solution.py:352
  69.6 0.0 all-to-all-done.1.received
  69.7 1.4 %logprob.1 = f32[32,7680]{1,0:T(8,128)} custom-call(bf16[32,7680]{1,0:T(8,128)(2,1)S(1)} %get-tuple-element.15.masked, bf16[16,16,128]{2,1,0:T(8,128)(2,1)S(1)} %all-to-all-done.1.received), custom_call_target="tpu_custom_call" | custom-call | tf_op jit(solution)/shard_map/logprob/pallas_call | solution.py:353
  71.0 0.0 collective-permute-done.4.second
  71.0 1.2 %collective-permute-done.5.first = bf16[128,128]{1,0:T(8,128)(2,1)S(1)} collective-permute-done((bf16[128,128]{1,0:T(8,128)(2,1)S(1)}, bf16[128,128]{1,0:T(8,128)(2,1)S(1)}, u32[]{:S(2)}, u32[]{:S(2)}) %collective-permute-start.5) | collective-permute-done | bytes 32800 | tf_op jit(solution)/shard_map/ppermute | solution.py:352
  72.2 1.9 %collective-permute-done.6.third = bf16[128,128]{1,0:T(8,128)(2,1)S(1)} collective-permute-done((bf16[128,128]{1,0:T(8,128)(2,1)S(1)}, bf16[128,128]{1,0:T(8,128)(2,1)S(1)}, u32[]{:S(2)}, u32[]{:S(2)}) %collective-permute-start.6) | collective-permute-done | bytes 32800 | tf_op jit(solution)/shard_map/ppermute | solution.py:352
  74.2 0.0 copy-done.2
  74.2 1.1 %landed.1 = bf16[32,512]{1,0:T(8,128)(2,1)} custom-call(bf16[128,128]{1,0:T(8,128)(2,1)S(1)} %pad_maximum_fusion.here, bf16[128,128]{1,0:T(8,128)(2,1)S(1)} %collective-permute-done.4.second, bf16[128,128]{1,0:T(8,128)(2,1)S(1)} %collective-permute-done.5.first, bf16[128,128]{1,0:T(8,128)(2,1)S(1)} %collective-permute-done.6.third, ...), custom_call_target="tpu_custom_call" | custom-call | tf_op jit(solution)/shard_map/landed/pallas_call | solution.py:361
  (2 shorter events, 0.0 us)
Async XLA Ops:
  2.3 6.4 %collective-permute-start = (bf16[64,512]{1,0:T(8,128)(2,1)}, bf16[64,512]{1,0:T(8,128)(2,1)S(1)}, u32[]{:S(2)}, u32[]{:S(2)}) collective-permute-start(bf16[64,512]{1,0:T(8,128)(2,1)} %get-tuple-element.10), channel_id=1, source_target_pairs={{0,128},{1,129},{2,130},{3,131},{4,132},{5,133},{6,134},{7,135},{8... | collective-permute-start | bytes 196616 | tf_op jit(solution)/shard_map/ppermute | solution.py:310
  3.6 5.1 %collective-permute-start.1 = (bf16[64,512]{1,0:T(8,128)(2,1)}, bf16[64,512]{1,0:T(8,128)(2,1)S(1)}, u32[]{:S(2)}, u32[]{:S(2)}) collective-permute-start(bf16[64,512]{1,0:T(8,128)(2,1)} %get-tuple-element.11), channel_id=1, source_target_pairs={{0,256},{1,257},{2,258},{3,259},{4,260},{5,261},{6,262},{7,263},{8... | collective-permute-start | bytes 196616 | tf_op jit(solution)/shard_map/ppermute | solution.py:310
  4.3 4.4 %collective-permute-start.2 = (bf16[64,512]{1,0:T(8,128)(2,1)}, bf16[64,512]{1,0:T(8,128)(2,1)S(1)}, u32[]{:S(2)}, u32[]{:S(2)}) collective-permute-start(bf16[64,512]{1,0:T(8,128)(2,1)} %get-tuple-element.12), channel_id=1, source_target_pairs={{0,384},{1,385},{2,386},{3,387},{4,388},{5,389},{6,390},{7,391},{8... | collective-permute-start | bytes 196616 | tf_op jit(solution)/shard_map/ppermute | solution.py:310
  6.6 18.5 %copy-start.3 = (s32[24,256]{1,0:T(8,128)S(1)}, s32[24,256]{1,0:T(8,128)}, u32[]{:S(2)}) copy-start(s32[24,256]{1,0:T(8,128)} %masks.1) | copy-start | bytes 73732
  6.6 18.5 %copy-start.6 = (s32[32]{0:T(128)S(1)}, s32[32]{0:T(128)}, u32[]{:S(2)}) copy-start(s32[32]{0:T(128)} %param.20) | copy-start | bytes 388
  6.6 38.3 %copy-start = (bf16[2,128,2048]{2,1,0:T(8,128)(2,1)S(1)}, bf16[2,128,2048]{2,1,0:T(8,128)(2,1)}, u32[]{:S(2)}) copy-start(bf16[2,128,2048]{2,1,0:T(8,128)(2,1)} %cache.1) | copy-start | bytes 3145732
  6.6 38.3 %copy-start.4 = (s32[8,16]{1,0:T(8,128)S(1)}, s32[8,16]{1,0:T(8,128)}, u32[]{:S(2)}) copy-start(s32[8,16]{1,0:T(8,128)} %lengths.3) | copy-start | bytes 1540
  6.6 38.3 %copy-start.5 = (s32[8,16]{1,0:T(8,128)S(1)}, s32[8,16]{1,0:T(8,128)}, u32[]{:S(2)}) copy-start(s32[8,16]{1,0:T(8,128)} %owners.3) | copy-start | bytes 1540
  9.9 35.0 %all-to-all-start = ((bf16[16,80,128]{2,1,0:T(8,128)(2,1)}), bf16[16,80,128]{2,1,0:T(8,128)(2,1)S(1)}, u32[]{:S(2)}, u32[]{:S(2)}) async-start(bf16[16,80,128]{2,1,0:T(8,128)(2,1)} %project.1), calls=%async_computation | async-start | bytes 655360 | tf_op jit(solution)/shard_map/all_to_all | solution.py:272
  25.1 1.0 %copy-start.1 = (bf16[32,7680]{1,0:T(8,128)(2,1)S(1)}, bf16[32,7680]{1,0:T(8,128)(2,1)}, u32[]{:S(2)}) copy-start(bf16[32,7680]{1,0:T(8,128)(2,1)} %logits.1) | copy-start | bytes 1474564
  26.2 48.0 %copy-start.2 = (bf16[32,512]{1,0:T(8,128)(2,1)S(1)}, bf16[32,512]{1,0:T(8,128)(2,1)}, u32[]{:S(2)}) copy-start(bf16[32,512]{1,0:T(8,128)(2,1)} %queries.3) | copy-start | bytes 98308
  46.9 22.7 %all-to-all-start.1 = ((bf16[16,16,128]{2,1,0:T(8,128)(2,1)}), bf16[16,16,128]{2,1,0:T(8,128)(2,1)S(1)}, u32[]{:S(2)}, u32[]{:S(2)}) async-start(bf16[16,16,128]{2,1,0:T(8,128)(2,1)} %cached.1), calls=%async_computation.1 | async-start | bytes 131072 | tf_op jit(solution)/shard_map/all_to_all | solution.py:272
  53.0 5.9 %collective-permute-start.3 = (bf16[64,128]{1,0:T(8,128)(2,1)S(1)}, bf16[64,128]{1,0:T(8,128)(2,1)S(1)}, u32[]{:S(2)}, u32[]{:S(2)}) collective-permute-start(bf16[64,128]{1,0:T(8,128)(2,1)S(1)} %reduce.1), channel_id=1, source_target_pairs={{0,1},{1,0},{2,3},{3,2},{4,5},{5,4},{6,7},{7,6},{8,9},{9,8},{10,11... | collective-permute-start | bytes 49160 | tf_op jit(solution)/shard_map/ppermute | solution.py:340
  58.9 12.1 %collective-permute-start.4 = (bf16[128,128]{1,0:T(8,128)(2,1)S(1)}, bf16[128,128]{1,0:T(8,128)(2,1)S(1)}, u32[]{:S(2)}, u32[]{:S(2)}) collective-permute-start(bf16[128,128]{1,0:T(8,128)(2,1)S(1)} %pad_maximum_fusion.here), channel_id=1, source_target_pairs={{0,256},{128,384},{384,128},{1,257},{129,385},{385,129},{2,258},{1... | collective-permute-start | bytes 98312 | tf_op jit(solution)/shard_map/ppermute | solution.py:352
  66.4 5.8 %collective-permute-start.5 = (bf16[128,128]{1,0:T(8,128)(2,1)S(1)}, bf16[128,128]{1,0:T(8,128)(2,1)S(1)}, u32[]{:S(2)}, u32[]{:S(2)}) collective-permute-start(bf16[128,128]{1,0:T(8,128)(2,1)S(1)} %pad_maximum_fusion.here), channel_id=1, source_target_pairs={{0,128},{128,256},{256,384},{1,129},{129,257},{257,385},{2,130},{1... | collective-permute-start | bytes 98312 | tf_op jit(solution)/shard_map/ppermute | solution.py:352
  68.3 5.8 %collective-permute-start.6 = (bf16[128,128]{1,0:T(8,128)(2,1)S(1)}, bf16[128,128]{1,0:T(8,128)(2,1)S(1)}, u32[]{:S(2)}, u32[]{:S(2)}) collective-permute-start(bf16[128,128]{1,0:T(8,128)(2,1)S(1)} %pad_maximum_fusion.here), channel_id=1, source_target_pairs={{0,384},{256,128},{384,256},{1,385},{257,129},{385,257},{2,386},{2... | collective-permute-start | bytes 98312 | tf_op jit(solution)/shard_map/ppermute | solution.py:352

commit v5 on v4

--- a/solution.py
+++ b/solution.py
@@ -88,20 +88,19 @@
     copy.wait()
 
 
-def project(own, first, second, third, asked, weight, out):
+def project(own, first, second, third, weight, out):
     turn = lax.axis_index("x")
     tokens = jnp.where(turn == 0, own[...], first[...] + second[...] + third[...])
     full = jnp.dot(tokens, weight[...], preferred_element_type=F32).astype(BF16)
-    out[:, 64:80] = asked[...]
     for c in range(16):
         block = c // 2 + (c % 2) * KVH
-        out[c, 0:64] = full[:, HD * block : HD * (block + 1)]
+        out[c] = full[:, HD * block : HD * (block + 1)]
 
 
 def reduce_blocks(pieces, out):
-    total = pieces[0, 0:64].astype(F32)
+    total = pieces[0].astype(F32)
     for c in range(1, 16):
-        total = total + pieces[c, 0:64].astype(F32)
+        total = total + pieces[c].astype(F32)
     out[...] = total.astype(BF16)
 
 
@@ -180,7 +179,7 @@
         lengths[...], owners[...], lax.axis_index("c8"), lax.axis_index("x")
     )
     landed = landing(jnp.full((1, 1), column, I32), prompts)[0]
-    table = received[:, 64:80, :].reshape(256, HD)
+    table = received[...].reshape(256, HD)
     row = iota((256, 1), 0)
     device, k = row // 16, row % 16
     second = (k >= 4) & (k < 8)
@@ -296,7 +295,7 @@
     tokens, wide = hidden.shape[0] // 4, hidden.shape[1]
     *shares, asked = pl.pallas_call(
         prepare,
-        out_shape=[kept((tokens, wide), BF16)] * 4 + [kept((16, 16, HD), BF16)],
+        out_shape=[kept((tokens, wide), BF16)] * 4 + [sent((16, 16, HD), BF16)],
         in_specs=[hbm] * 3,
         out_specs=[vmem] * 5,
         scratch_shapes=[
@@ -308,6 +307,7 @@
     )(hidden, queries, fresh)
     for k in (2, 1, 3):
         shares[k] = lax.ppermute(shares[k], "x", [(0, k)])
+    asked = exchanged(asked, TP)
     weight = pl.pallas_call(
         fetch,
         out_shape=kept(w_kv.shape, BF16),
@@ -318,10 +318,10 @@
     )(w_kv)
     projected = pl.pallas_call(
         project,
-        out_shape=sent((16, 80, HD), BF16),
-        in_specs=[vmem] * 6,
+        out_shape=sent((16, tokens, HD), BF16),
+        in_specs=[vmem] * 5,
         name="project",
-    )(*held(*shares, asked, weight))
+    )(*held(*shares, weight))
     pieces = exchanged(projected, TP)
     masked, terms = pl.pallas_call(
         grammar,
@@ -343,7 +343,7 @@
         out_shape=sent((16, 16, HD), BF16),
         in_specs=[smem] + [vmem] * 5,
         name="cached",
-    )(cache_len, *held(pieces, cache, terms, prompt_lengths, owner_step))
+    )(cache_len, *held(asked, cache, terms, prompt_lengths, owner_step))
     answers = exchanged(answers, TP)
     both = jnp.concatenate([block, other], axis=0)
     around = [both]

time: 75.8 us -> 82.7 us (1.091)
  the two profiles are of different devices: /device:TPU:26 before, /device:TPU:18 now
where the time goes in v5:
time: 82.7 us; the launch traced here: 82 us
  starting transfers between devices  44.8 us (54%)
  waiting for transfers between devices  24.9 us (30%)
  Pallas kernels  10.4 us (13%)
  local copies, waits for them, and re-layouts  1.06 us (1%)
  between operations  0.85 us (1%)
    all_to_all x3, starting transfers between devices, exchanged(): return lax.all_to_all(slots, axis, 0, 0, tiled=True)  27.7 us
    all_to_all x3, waiting for transfers between devices, exchanged(): return lax.all_to_all(slots, axis, 0, 0, tiled=True)  17.7 us
    ppermute x3, starting transfers between devices, per_device(): around.append(lax.ppermute(both, 'x', route))  10.7 us
    ppermute x1, starting transfers between devices, per_device(): other = lax.ppermute(block, 'zl', [(0, 1), (1, 0)])  3.83 us
    ppermute x3, waiting for transfers between devices, per_device(): around.append(lax.ppermute(both, 'x', route))  3.11 us
    ppermute x3, starting transfers between devices, per_device(): shares[k] = lax.ppermute(shares[k], 'x', [(0, k)])  2.62 us
    ppermute x1, waiting for transfers between devices, per_device(): other = lax.ppermute(block, 'zl', [(0, 1), (1, 0)])  2.08 us
    ppermute x3, waiting for transfers between devices, per_device(): shares[k] = lax.ppermute(shares[k], 'x', [(0, k)])  2.06 us
  transfers between devices with their start and end apart: 10, of which 6 were waited for; matrix products, arithmetic and copies ran while one was open for 0% of the time, Pallas kernels for 9%

profile of v5, /device:TPU:18, one launch (start us, length us, event | category | flops | bytes accessed | tf_op | source)
XLA Modules:
  0.0 82.0 jit_solution(17236331980246708576)
XLA Ops:
  0.6 1.7 %prepare.1 = (bf16[64,512]{1,0:T(8,128)(2,1)S(1)}, bf16[64,512]{1,0:T(8,128)(2,1)}, bf16[64,512]{1,0:T(8,128)(2,1)}, bf16[64,512]{1,0:T(8,128)(2,1)}, bf16[16,16,128]{2,1,0:T(8,128)(2,1)}) custom-call(bf16[256,512]{1,0:T(8,128)(2,1)} %hidden.1, bf16[32,512]{1,0:T(8,128)(2,1)} %queries.3, bf16[32,128]{1,0:T(8,128)(2,1)} %fresh.1), custom_call_target="tpu_custom_call" | custom-call | tf_op jit(solution)/shard_map/prepare/pallas_call | solution.py:296
  2.3 15.2 %all-to-all-start.1 = ((bf16[16,16,128]{2,1,0:T(8,128)(2,1)}), bf16[16,16,128]{2,1,0:T(8,128)(2,1)S(1)}, u32[]{:S(2)}, u32[]{:S(2)}) async-start(bf16[16,16,128]{2,1,0:T(8,128)(2,1)} %get-tuple-element.13), calls=%async_computation.1 | async-start | bytes 131072 | tf_op jit(solution)/shard_map/all_to_all | solution.py:271
  17.6 1.3 %collective-permute-start = (bf16[64,512]{1,0:T(8,128)(2,1)}, bf16[64,512]{1,0:T(8,128)(2,1)S(1)}, u32[]{:S(2)}, u32[]{:S(2)}) collective-permute-start(bf16[64,512]{1,0:T(8,128)(2,1)} %get-tuple-element.10), channel_id=1, source_target_pairs={{0,128},{1,129},{2,130},{3,131},{4,132},{5,133},{6,134},{7,135},{8... | collective-permute-start | bytes 196616 | tf_op jit(solution)/shard_map/ppermute | solution.py:309
  18.9 0.7 collective-permute-start.1
  19.5 0.7 collective-permute-start.2
  20.2 1.6 %fetch.1.weight = bf16[512,2048]{1,0:T(8,128)(2,1)S(1)} custom-call(bf16[512,2048]{1,0:T(8,128)(2,1)} %weight.1), custom_call_target="tpu_custom_call" | custom-call | tf_op jit(solution)/shard_map/fetch/pallas_call | solution.py:311
  21.8 0.0 copy-start.3
  21.8 0.0 copy-start.6
  21.8 0.0 copy-start
  21.8 0.0 copy-start.4
  21.9 0.0 copy-start.5
  21.9 2.1 %collective-permute-done.first = bf16[64,512]{1,0:T(8,128)(2,1)S(1)} collective-permute-done((bf16[64,512]{1,0:T(8,128)(2,1)}, bf16[64,512]{1,0:T(8,128)(2,1)S(1)}, u32[]{:S(2)}, u32[]{:S(2)}) %collective-permute-start) | collective-permute-done | bytes 65568 | tf_op jit(solution)/shard_map/ppermute | solution.py:309
  23.9 0.0 collective-permute-done.1.second
  23.9 0.0 collective-permute-done.2.third
  23.9 1.2 %project.1 = bf16[16,64,128]{2,1,0:T(8,128)(2,1)} custom-call(bf16[64,512]{1,0:T(8,128)(2,1)S(1)} %get-tuple-element.9.own, bf16[64,512]{1,0:T(8,128)(2,1)S(1)} %collective-permute-done.first, bf16[64,512]{1,0:T(8,128)(2,1)S(1)} %collective-permute-done.1.second, bf16[64,512]{1,0:T(8,128)(2,1)S(1)} %collective-permute-done.2.third, ...), custom_call_target="tpu_custom_call" | custom-call | tf_op jit(solution)/shard_map/project/pallas_call | solution.py:319
  25.1 0.0 copy-start.2
  25.1 5.2 %all-to-all-done.1.received = bf16[16,16,128]{2,1,0:T(8,128)(2,1)S(1)} async-done(((bf16[16,16,128]{2,1,0:T(8,128)(2,1)}), bf16[16,16,128]{2,1,0:T(8,128)(2,1)S(1)}, u32[]{:S(2)}, u32[]{:S(2)}) %all-to-all-start.1) | async-done | bytes 65568 | tf_op jit(solution)/shard_map/all_to_all | solution.py:271
  30.3 7.2 %all-to-all-start = ((bf16[16,64,128]{2,1,0:T(8,128)(2,1)}), bf16[16,64,128]{2,1,0:T(8,128)(2,1)S(1)}, u32[]{:S(2)}, u32[]{:S(2)}) async-start(bf16[16,64,128]{2,1,0:T(8,128)(2,1)} %project.1), calls=%async_computation | async-start | bytes 524288 | tf_op jit(solution)/shard_map/all_to_all | solution.py:271
  37.5 0.0 copy-done.3
  37.5 0.0 copy-done.6
  37.5 0.0 copy-start.1
  37.5 1.0 %copy-done.1 = bf16[32,7680]{1,0:T(8,128)(2,1)S(1)} copy-done((bf16[32,7680]{1,0:T(8,128)(2,1)S(1)}, bf16[32,7680]{1,0:T(8,128)(2,1)}, u32[]{:S(2)}) %copy-start.1) | copy-done | bytes 491544
  38.5 1.3 %grammar.1 = (bf16[32,7680]{1,0:T(8,128)(2,1)S(1)}, bf16[16,128]{1,0:T(8,128)(2,1)S(1)}) custom-call(bf16[32,7680]{1,0:T(8,128)(2,1)S(1)} %copy-done.1, s32[1,32]{1,0:T(1,128)S(1)} %bitcast.1, s32[24,256]{1,0:T(8,128)S(1)} %copy-done.3), custom_call_target="tpu_custom_call" | custom-call | tf_op jit(solution)/shard_map/grammar/pallas_call | solution.py:326
  39.8 0.0 copy-done
  39.8 0.0 copy-done.4
  39.8 0.0 copy-done.5
  39.8 2.0 %cached.1 = bf16[16,16,128]{2,1,0:T(8,128)(2,1)} custom-call(s32[2]{0:T(128)} %cache_len.1, bf16[16,16,128]{2,1,0:T(8,128)(2,1)S(1)} %all-to-all-done.1.received, bf16[2,128,2048]{2,1,0:T(8,128)(2,1)S(1)} %copy-done, bf16[16,128]{1,0:T(8,128)(2,1)S(1)} %get-tuple-element.14.terms, s32[8,16]{1,0:T(8,128)S(1)} %copy-done.4, s32[8,16]{1,0:T(8,128)S(1)} %copy-done.5), custom_call_target="tpu_custom_call" | custom-call | tf_op jit(solution)/shard_map/cached/pallas_call | solution.py:341
  41.9 12.5 %all-to-all-done.pieces = bf16[16,64,128]{2,1,0:T(8,128)(2,1)S(1)} async-done(((bf16[16,64,128]{2,1,0:T(8,128)(2,1)}), bf16[16,64,128]{2,1,0:T(8,128)(2,1)S(1)}, u32[]{:S(2)}, u32[]{:S(2)}) %all-to-all-start) | async-done | bytes 262176 | tf_op jit(solution)/shard_map/all_to_all | solution.py:271
  54.4 5.3 %all-to-all-start.2 = ((bf16[16,16,128]{2,1,0:T(8,128)(2,1)}), bf16[16,16,128]{2,1,0:T(8,128)(2,1)S(1)}, u32[]{:S(2)}, u32[]{:S(2)}) async-start(bf16[16,16,128]{2,1,0:T(8,128)(2,1)} %cached.1), calls=%async_computation.2 | async-start | bytes 131072 | tf_op jit(solution)/shard_map/all_to_all | solution.py:271
  59.8 3.8 %collective-permute-start.3 = (bf16[64,128]{1,0:T(8,128)(2,1)S(1)}, bf16[64,128]{1,0:T(8,128)(2,1)S(1)}, u32[]{:S(2)}, u32[]{:S(2)}) collective-permute-start(bf16[64,128]{1,0:T(8,128)(2,1)S(1)} %reduce.1), channel_id=1, source_target_pairs={{0,1},{1,0},{2,3},{3,2},{4,5},{5,4},{6,7},{7,6},{8,9},{9,8},{10,11... | collective-permute-start | bytes 49160 | tf_op jit(solution)/shard_map/ppermute | solution.py:340
  63.6 2.1 %collective-permute-done.3 = bf16[64,128]{1,0:T(8,128)(2,1)S(1)} collective-permute-done((bf16[64,128]{1,0:T(8,128)(2,1)S(1)}, bf16[64,128]{1,0:T(8,128)(2,1)S(1)}, u32[]{:S(2)}, u32[]{:S(2)}) %collective-permute-start.3) | collective-permute-done | bytes 16416 | tf_op jit(solution)/shard_map/ppermute | solution.py:340
  65.7 7.5 %collective-permute-start.4 = (bf16[128,128]{1,0:T(8,128)(2,1)S(1)}, bf16[128,128]{1,0:T(8,128)(2,1)S(1)}, u32[]{:S(2)}, u32[]{:S(2)}) collective-permute-start(bf16[128,128]{1,0:T(8,128)(2,1)S(1)} %pad_maximum_fusion.here), channel_id=1, source_target_pairs={{0,256},{128,384},{384,128},{1,257},{129,385},{385,129},{2,258},{1... | collective-permute-start | bytes 98312 | tf_op jit(solution)/shard_map/ppermute | solution.py:352
  73.2 1.9 %collective-permute-start.5 = (bf16[128,128]{1,0:T(8,128)(2,1)S(1)}, bf16[128,128]{1,0:T(8,128)(2,1)S(1)}, u32[]{:S(2)}, u32[]{:S(2)}) collective-permute-start(bf16[128,128]{1,0:T(8,128)(2,1)S(1)} %pad_maximum_fusion.here), channel_id=1, source_target_pairs={{0,128},{128,256},{256,384},{1,129},{129,257},{257,385},{2,130},{1... | collective-permute-start | bytes 98312 | tf_op jit(solution)/shard_map/ppermute | solution.py:352
  75.1 1.3 %collective-permute-start.6 = (bf16[128,128]{1,0:T(8,128)(2,1)S(1)}, bf16[128,128]{1,0:T(8,128)(2,1)S(1)}, u32[]{:S(2)}, u32[]{:S(2)}) collective-permute-start(bf16[128,128]{1,0:T(8,128)(2,1)S(1)} %pad_maximum_fusion.here), channel_id=1, source_target_pairs={{0,384},{256,128},{384,256},{1,385},{257,129},{385,257},{2,386},{2... | collective-permute-start | bytes 98312 | tf_op jit(solution)/shard_map/ppermute | solution.py:352
  76.4 0.0 all-to-all-done.2.received
  76.4 1.4 %logprob.1 = f32[32,7680]{1,0:T(8,128)} custom-call(bf16[32,7680]{1,0:T(8,128)(2,1)S(1)} %get-tuple-element.15.masked, bf16[16,16,128]{2,1,0:T(8,128)(2,1)S(1)} %all-to-all-done.2.received), custom_call_target="tpu_custom_call" | custom-call | tf_op jit(solution)/shard_map/logprob/pallas_call | solution.py:353
  77.8 0.0 collective-permute-done.4.second
  77.8 1.2 %collective-permute-done.5.first = bf16[128,128]{1,0:T(8,128)(2,1)S(1)} collective-permute-done((bf16[128,128]{1,0:T(8,128)(2,1)S(1)}, bf16[128,128]{1,0:T(8,128)(2,1)S(1)}, u32[]{:S(2)}, u32[]{:S(2)}) %collective-permute-start.5) | collective-permute-done | bytes 32800 | tf_op jit(solution)/shard_map/ppermute | solution.py:352
  79.0 1.9 %collective-permute-done.6.third = bf16[128,128]{1,0:T(8,128)(2,1)S(1)} collective-permute-done((bf16[128,128]{1,0:T(8,128)(2,1)S(1)}, bf16[128,128]{1,0:T(8,128)(2,1)S(1)}, u32[]{:S(2)}, u32[]{:S(2)}) %collective-permute-start.6) | collective-permute-done | bytes 32800 | tf_op jit(solution)/shard_map/ppermute | solution.py:352
  80.9 0.0 copy-done.2
  80.9 1.2 %landed.1 = bf16[32,512]{1,0:T(8,128)(2,1)} custom-call(bf16[128,128]{1,0:T(8,128)(2,1)S(1)} %pad_maximum_fusion.here, bf16[128,128]{1,0:T(8,128)(2,1)S(1)} %collective-permute-done.4.second, bf16[128,128]{1,0:T(8,128)(2,1)S(1)} %collective-permute-done.5.first, bf16[128,128]{1,0:T(8,128)(2,1)S(1)} %collective-permute-done.6.third, ...), custom_call_target="tpu_custom_call" | custom-call | tf_op jit(solution)/shard_map/landed/pallas_call | solution.py:361
  (2 shorter events, 0.0 us)
Async XLA Ops:
  2.3 27.9 %all-to-all-start.1 = ((bf16[16,16,128]{2,1,0:T(8,128)(2,1)}), bf16[16,16,128]{2,1,0:T(8,128)(2,1)S(1)}, u32[]{:S(2)}, u32[]{:S(2)}) async-start(bf16[16,16,128]{2,1,0:T(8,128)(2,1)} %get-tuple-element.13), calls=%async_computation.1 | async-start | bytes 131072 | tf_op jit(solution)/shard_map/all_to_all | solution.py:271
  17.6 6.4 %collective-permute-start = (bf16[64,512]{1,0:T(8,128)(2,1)}, bf16[64,512]{1,0:T(8,128)(2,1)S(1)}, u32[]{:S(2)}, u32[]{:S(2)}) collective-permute-start(bf16[64,512]{1,0:T(8,128)(2,1)} %get-tuple-element.10), channel_id=1, source_target_pairs={{0,128},{1,129},{2,130},{3,131},{4,132},{5,133},{6,134},{7,135},{8... | collective-permute-start | bytes 196616 | tf_op jit(solution)/shard_map/ppermute | solution.py:309
  18.9 5.1 %collective-permute-start.1 = (bf16[64,512]{1,0:T(8,128)(2,1)}, bf16[64,512]{1,0:T(8,128)(2,1)S(1)}, u32[]{:S(2)}, u32[]{:S(2)}) collective-permute-start(bf16[64,512]{1,0:T(8,128)(2,1)} %get-tuple-element.11), channel_id=1, source_target_pairs={{0,256},{1,257},{2,258},{3,259},{4,260},{5,261},{6,262},{7,263},{8... | collective-permute-start | bytes 196616 | tf_op jit(solution)/shard_map/ppermute | solution.py:309
  19.5 4.4 %collective-permute-start.2 = (bf16[64,512]{1,0:T(8,128)(2,1)}, bf16[64,512]{1,0:T(8,128)(2,1)S(1)}, u32[]{:S(2)}, u32[]{:S(2)}) collective-permute-start(bf16[64,512]{1,0:T(8,128)(2,1)} %get-tuple-element.12), channel_id=1, source_target_pairs={{0,384},{1,385},{2,386},{3,387},{4,388},{5,389},{6,390},{7,391},{8... | collective-permute-start | bytes 196616 | tf_op jit(solution)/shard_map/ppermute | solution.py:309
  21.8 15.7 %copy-start.3 = (s32[24,256]{1,0:T(8,128)S(1)}, s32[24,256]{1,0:T(8,128)}, u32[]{:S(2)}) copy-start(s32[24,256]{1,0:T(8,128)} %masks.1) | copy-start | bytes 73732
  21.8 15.7 %copy-start.6 = (s32[32]{0:T(128)S(1)}, s32[32]{0:T(128)}, u32[]{:S(2)}) copy-start(s32[32]{0:T(128)} %param.20) | copy-start | bytes 388
  21.8 18.0 %copy-start = (bf16[2,128,2048]{2,1,0:T(8,128)(2,1)S(1)}, bf16[2,128,2048]{2,1,0:T(8,128)(2,1)}, u32[]{:S(2)}) copy-start(bf16[2,128,2048]{2,1,0:T(8,128)(2,1)} %cache.1) | copy-start | bytes 3145732
  21.8 18.0 %copy-start.4 = (s32[8,16]{1,0:T(8,128)S(1)}, s32[8,16]{1,0:T(8,128)}, u32[]{:S(2)}) copy-start(s32[8,16]{1,0:T(8,128)} %lengths.3) | copy-start | bytes 1540
  21.9 18.0 %copy-start.5 = (s32[8,16]{1,0:T(8,128)S(1)}, s32[8,16]{1,0:T(8,128)}, u32[]{:S(2)}) copy-start(s32[8,16]{1,0:T(8,128)} %owners.3) | copy-start | bytes 1540
  25.1 55.8 %copy-start.2 = (bf16[32,512]{1,0:T(8,128)(2,1)S(1)}, bf16[32,512]{1,0:T(8,128)(2,1)}, u32[]{:S(2)}) copy-start(bf16[32,512]{1,0:T(8,128)(2,1)} %queries.3) | copy-start | bytes 98308
  30.3 24.2 %all-to-all-start = ((bf16[16,64,128]{2,1,0:T(8,128)(2,1)}), bf16[16,64,128]{2,1,0:T(8,128)(2,1)S(1)}, u32[]{:S(2)}, u32[]{:S(2)}) async-start(bf16[16,64,128]{2,1,0:T(8,128)(2,1)} %project.1), calls=%async_computation | async-start | bytes 524288 | tf_op jit(solution)/shard_map/all_to_all | solution.py:271
  37.5 1.0 %copy-start.1 = (bf16[32,7680]{1,0:T(8,128)(2,1)S(1)}, bf16[32,7680]{1,0:T(8,128)(2,1)}, u32[]{:S(2)}) copy-start(bf16[32,7680]{1,0:T(8,128)(2,1)} %logits.1) | copy-start | bytes 1474564
  54.4 21.9 %all-to-all-start.2 = ((bf16[16,16,128]{2,1,0:T(8,128)(2,1)}), bf16[16,16,128]{2,1,0:T(8,128)(2,1)S(1)}, u32[]{:S(2)}, u32[]{:S(2)}) async-start(bf16[16,16,128]{2,1,0:T(8,128)(2,1)} %cached.1), calls=%async_computation.2 | async-start | bytes 131072 | tf_op jit(solution)/shard_map/all_to_all | solution.py:271
  59.8 5.9 %collective-permute-start.3 = (bf16[64,128]{1,0:T(8,128)(2,1)S(1)}, bf16[64,128]{1,0:T(8,128)(2,1)S(1)}, u32[]{:S(2)}, u32[]{:S(2)}) collective-permute-start(bf16[64,128]{1,0:T(8,128)(2,1)S(1)} %reduce.1), channel_id=1, source_target_pairs={{0,1},{1,0},{2,3},{3,2},{4,5},{5,4},{6,7},{7,6},{8,9},{9,8},{10,11... | collective-permute-start | bytes 49160 | tf_op jit(solution)/shard_map/ppermute | solution.py:340
  65.7 12.1 %collective-permute-start.4 = (bf16[128,128]{1,0:T(8,128)(2,1)S(1)}, bf16[128,128]{1,0:T(8,128)(2,1)S(1)}, u32[]{:S(2)}, u32[]{:S(2)}) collective-permute-start(bf16[128,128]{1,0:T(8,128)(2,1)S(1)} %pad_maximum_fusion.here), channel_id=1, source_target_pairs={{0,256},{128,384},{384,128},{1,257},{129,385},{385,129},{2,258},{1... | collective-permute-start | bytes 98312 | tf_op jit(solution)/shard_map/ppermute | solution.py:352
  73.2 5.8 %collective-permute-start.5 = (bf16[128,128]{1,0:T(8,128)(2,1)S(1)}, bf16[128,128]{1,0:T(8,128)(2,1)S(1)}, u32[]{:S(2)}, u32[]{:S(2)}) collective-permute-start(bf16[128,128]{1,0:T(8,128)(2,1)S(1)} %pad_maximum_fusion.here), channel_id=1, source_target_pairs={{0,128},{128,256},{256,384},{1,129},{129,257},{257,385},{2,130},{1... | collective-permute-start | bytes 98312 | tf_op jit(solution)/shard_map/ppermute | solution.py:352
  75.1 5.8 %collective-permute-start.6 = (bf16[128,128]{1,0:T(8,128)(2,1)S(1)}, bf16[128,128]{1,0:T(8,128)(2,1)S(1)}, u32[]{:S(2)}, u32[]{:S(2)}) collective-permute-start(bf16[128,128]{1,0:T(8,128)(2,1)S(1)} %pad_maximum_fusion.here), channel_id=1, source_target_pairs={{0,384},{256,128},{384,256},{1,385},{257,129},{385,257},{2,386},{2... | collective-permute-start | bytes 98312 | tf_op jit(solution)/shard_map/ppermute | solution.py:352

commit v6 on v2

--- a/solution.py
+++ b/solution.py
@@ -89,23 +89,31 @@
     copy.wait()
 
 
-def project(own, first, second, third, weight, asked, out):
+def project(own, first, second, third, asked, weight, out, slots, sems):
     turn = lax.axis_index("x")
     tokens = jnp.where(turn == 0, own[...], first[...] + second[...] + third[...])
-    full = jnp.dot(tokens, weight[...], preferred_element_type=F32).astype(BF16)
-    for c in range(16):
-        block = c // 2 + (c % 2) * KVH
-        out[c, 0:64] = full[:, HD * block : HD * (block + 1)]
-        out[c, 64:80] = asked[c]
+    slots[:, 64:80] = asked[...]
+    copies = []
+    for h in range(4):
+        for part in range(2):
+            at = HD * (KVH * part + 2 * h)
+            full = jnp.dot(
+                tokens, weight[:, at : at + 2 * HD], preferred_element_type=F32
+            ).astype(BF16)
+            slots[4 * h + part, 0:64] = full[:, :HD]
+            slots[4 * h + 2 + part, 0:64] = full[:, HD:]
+        four = pl.ds(4 * h, 4)
+        copies.append(pltpu.make_async_copy(slots.at[four], out.at[four], sems.at[h]))
+        copies[-1].start()
+    for copy in copies:
+        copy.wait()
 
 
 def reduce_blocks(pieces, out):
     total = pieces[0, 0:64].astype(F32)
     for c in range(1, 16):
         total = total + pieces[c, 0:64].astype(F32)
-    total = total.astype(BF16)
-    for d in range(8):
-        out[d] = total
+    out[...] = total.astype(BF16)
 
 
 def grammar(logits, states, masks, masked, terms):
@@ -198,7 +206,7 @@
         both = [transposed(rows, cache[r, :, HD * h : HD * (h + 1)]) for r in range(2)]
         scores.append(jnp.where(second32, both[1], both[0]))
     score = jnp.concatenate(scores, axis=0) * SCALE
-    alive = iota((256, HD), 1) < jnp.where(second, cache_len[1], cache_len[0])
+    alive = iota((256, HD), 1) < jnp.where(second, cache_len[0:1, 1:2], cache_len[0:1, 0:1])
     weight, own_weight = softmax(score, own, alive)
     values = []
     for h in range(KVH):
@@ -217,22 +225,21 @@
     out[...] = result.astype(BF16).reshape(16, 16, HD)
 
 
-def own_prompts(row, lengths, owners):
-    request = row % 32
-    prompts = prompts_of(
-        lengths[...], owners[...], lax.axis_index("c8"), lax.axis_index("x")
-    )
-    return landing((request % 2) * 16 + request // 2, prompts)
-
-
-def attend_prompts(blocks, queries, lengths, owners, result, stats):
-    row = iota((128, 1), 0)
-    landed, start, length = own_prompts(row, lengths, owners)
-    keys = jnp.concatenate([blocks[2 * x] for x in range(4)], axis=0)
-    values = jnp.concatenate([blocks[2 * x + 1] for x in range(4)], axis=0)
+def attend_prompts(here, second, first, third, queries, lengths, owners, result, stats):
+    turn = lax.axis_index("x")
+    prompts = prompts_of(lengths[...], owners[...], lax.axis_index("c8"), turn)
+    request = iota((128, 1), 0) % 32
+    landed, start, length = landing((request % 2) * 16 + request // 2, prompts)
+    even = lax.axis_index("zl") == 0
+    parts = (here, first, second, third)
+    mine = jnp.concatenate([part[0:64] for part in parts], axis=0)
+    other = jnp.concatenate([part[64:128] for part in parts], axis=0)
+    keys = jnp.where(even, mine, other)
+    values = jnp.where(even, other, mine)
     query = jnp.concatenate([queries[:, HD * i : HD * (i + 1)] for i in range(4)], axis=0)
     score = transposed(query, keys) * SCALE
-    position = iota((128, 256), 1).astype(F32)
+    lane = iota((128, 256), 1)
+    position = ((turn + 4 - lane // 64) % 4 * 64 + lane % 64).astype(F32)
     alive = (position >= start) & (position < start + length)
     highest = jnp.max(jnp.where(alive, score, LOWEST), axis=1, keepdims=True)
     exponent = jnp.where(alive, jnp.exp(score - highest), 0.0)
@@ -256,10 +263,9 @@
         at = slice(BLK * b, BLK * (b + 1))
         section = masked[:, at].astype(F32)
         values[:, at] = jnp.where(section == -jnp.inf, 0.0, section - normalizer)
+        piece = pl.ds(BLK * b, BLK)
         copies.append(
-            pltpu.make_async_copy(
-                values.at[:, pl.ds(BLK * b, BLK)], logprob.at[:, pl.ds(BLK * b, BLK)], sems.at[b]
-            )
+            pltpu.make_async_copy(values.at[:, piece], logprob.at[:, piece], sems.at[b])
         )
         copies[-1].start()
     row = iota((128, 1), 0)
@@ -267,9 +273,9 @@
     query = jnp.concatenate([queries[:, HD * i : HD * (i + 1)] for i in range(4)], axis=0)
     table = received[...].reshape(256, HD)
     slot = (request // 2) * 16
-    own_key = pick(slot, table)
-    own_value = pick(slot + 1, table)
-    cached = pick(slot + (request % 2) * 4 + head, table)
+    target = jnp.concatenate([slot, slot + 1, slot + (request % 2) * 4 + head], axis=0)
+    picked = pick(target, table)
+    own_key, own_value, cached = picked[0:128], picked[128:256], picked[256:384]
     own = jnp.sum(query.astype(F32) * own_key, axis=1, keepdims=True) * SCALE
     top, total, landed = stats[:, 0:1], stats[:, 1:2], stats[:, 2:3]
     highest = jnp.maximum(top, own)
@@ -300,7 +306,6 @@
     states,
     masks,
 ):
-    smem = pl.BlockSpec(memory_space=pltpu.SMEM)
     vmem = pl.BlockSpec(memory_space=pltpu.VMEM)
     hbm = pl.BlockSpec(memory_space=pl.ANY)
     sent = jax.ShapeDtypeStruct
@@ -321,7 +326,8 @@
         ],
         name="prepare",
     )(hidden, queries, fresh)
-    shares[1:] = [lax.ppermute(shares[k], "x", [(0, k)]) for k in (1, 2, 3)]
+    for k in (2, 1, 3):
+        shares[k] = lax.ppermute(shares[k], "x", [(0, k)])
     weight = pl.pallas_call(
         fetch,
         out_shape=kept(w_kv.shape, BF16),
@@ -334,8 +340,10 @@
         project,
         out_shape=sent((16, 80, HD), BF16),
         in_specs=[vmem] * 6,
+        out_specs=hbm,
+        scratch_shapes=[pltpu.VMEM((16, 80, HD), BF16), pltpu.SemaphoreType.DMA((4,))],
         name="project",
-    )(*held(*shares, weight, asked))
+    )(*held(*shares, asked, weight))
     pieces = exchanged(projected, TP)
     masked, terms = pl.pallas_call(
         grammar,
@@ -344,27 +352,33 @@
         out_specs=[vmem] * 2,
         name="grammar",
     )(*held(logits, states.reshape(1, -1), masks))
-    blocks = pl.pallas_call(
+    block = pl.pallas_call(
         reduce_blocks,
-        out_shape=sent((8, tokens, HD), BF16),
+        out_shape=kept((tokens, HD), BF16),
         in_specs=[vmem],
+        out_specs=vmem,
         name="reduce",
     )(*held(pieces))
-    blocks = exchanged(blocks, ("x", "zl"))
+    other = lax.ppermute(block, "zl", [(0, 1), (1, 0)])
     answers = pl.pallas_call(
         attend_cached,
         out_shape=sent((16, 16, HD), BF16),
-        in_specs=[smem] + [vmem] * 5,
+        in_specs=[vmem] * 6,
         name="cached",
-    )(cache_len, *held(pieces, cache, terms, prompt_lengths, owner_step))
+    )(*held(cache_len.reshape(1, 2), pieces, cache, terms, prompt_lengths, owner_step))
     answers = exchanged(answers, TP)
+    both = jnp.concatenate([block, other], axis=0)
+    around = [both]
+    for k in (2, 1, 3):
+        route = [(i, (i + k) % 4) for i in range(4) if (i + k) % 4]
+        around.append(lax.ppermute(both, "x", route))
     result, stats = pl.pallas_call(
         attend_prompts,
         out_shape=[kept((128, HD), F32), kept((128, HD), F32)],
-        in_specs=[vmem] * 4,
+        in_specs=[vmem] * 7,
         out_specs=[vmem] * 2,
         name="prompts",
-    )(*held(blocks, queries, prompt_lengths, owner_step))
+    )(*held(*around, queries, prompt_lengths, owner_step))
     logprob, attended = pl.pallas_call(
         finish,
         out_shape=[sent(logits.shape, F32), sent(queries.shape, BF16)],

time: 81.4 us -> 76.5 us (0.940)
  the two profiles are of different devices: /device:TPU:24 before, /device:TPU:18 now
where the time goes in v6:
time: 76.5 us; the launch traced here: 75.9 us
  starting transfers between devices  38.4 us (50%)
  waiting for transfers between devices  26 us (34%)
  Pallas kernels  9.56 us (12%)
  local copies, waits for them, and re-layouts  1.07 us (1%)
  between operations  0.86 us (1%)
    all_to_all x2, starting transfers between devices, exchanged(): return lax.all_to_all(slots, axis, 0, 0, tiled=True)  21.2 us
    all_to_all x2, waiting for transfers between devices, exchanged(): return lax.all_to_all(slots, axis, 0, 0, tiled=True)  17.4 us
    ppermute x3, starting transfers between devices, per_device(): around.append(lax.ppermute(both, 'x', route))  10.7 us
    ppermute x3, waiting for transfers between devices, per_device(): around.append(lax.ppermute(both, 'x', route))  4.5 us
    ppermute x1, starting transfers between devices, per_device(): other = lax.ppermute(block, 'zl', [(0, 1), (1, 0)])  3.83 us
    ppermute x3, starting transfers between devices, per_device(): shares[k] = lax.ppermute(shares[k], 'x', [(0, k)])  2.62 us
    ppermute x1, waiting for transfers between devices, per_device(): other = lax.ppermute(block, 'zl', [(0, 1), (1, 0)])  2.06 us
    ppermute x3, waiting for transfers between devices, per_device(): shares[k] = lax.ppermute(shares[k], 'x', [(0, k)])  2.05 us
  transfers between devices with their start and end apart: 9, of which 5 were waited for; matrix products, arithmetic and copies ran while one was open for 0% of the time, Pallas kernels for 4%

profile of v6, /device:TPU:18, one launch (start us, length us, event | category | flops | bytes accessed | tf_op | source)
XLA Modules:
  0.0 75.9 jit_solution(1226407323657393536)
XLA Ops:
  0.6 1.7 %prepare.1 = (bf16[64,512]{1,0:T(8,128)(2,1)S(1)}, bf16[64,512]{1,0:T(8,128)(2,1)}, bf16[64,512]{1,0:T(8,128)(2,1)}, bf16[64,512]{1,0:T(8,128)(2,1)}, bf16[16,16,128]{2,1,0:T(8,128)(2,1)S(1)}) custom-call(bf16[256,512]{1,0:T(8,128)(2,1)} %hidden.1, bf16[32,512]{1,0:T(8,128)(2,1)} %queries.5, bf16[32,128]{1,0:T(8,128)(2,1)} %fresh.1), custom_call_target="tpu_custom_call" | custom-call | tf_op jit(solution)/shard_map/prepare/pallas_call | solution.py:317
  2.3 1.3 %collective-permute-start = (bf16[64,512]{1,0:T(8,128)(2,1)}, bf16[64,512]{1,0:T(8,128)(2,1)S(1)}, u32[]{:S(2)}, u32[]{:S(2)}) collective-permute-start(bf16[64,512]{1,0:T(8,128)(2,1)} %get-tuple-element.15), channel_id=1, source_target_pairs={{0,128},{1,129},{2,130},{3,131},{4,132},{5,133},{6,134},{7,135},{8... | collective-permute-start | bytes 196616 | tf_op jit(solution)/shard_map/ppermute | solution.py:330
  3.6 0.7 collective-permute-start.1
  4.3 0.7 collective-permute-start.2
  5.0 1.6 %fetch.1.weight = bf16[512,2048]{1,0:T(8,128)(2,1)S(1)} custom-call(bf16[512,2048]{1,0:T(8,128)(2,1)} %weight.1), custom_call_target="tpu_custom_call" | custom-call | tf_op jit(solution)/shard_map/fetch/pallas_call | solution.py:331
  6.6 0.0 copy-start.3
  6.6 0.0 copy-start.6
  6.6 0.0 copy-start
  6.6 0.0 copy-start.4
  6.6 0.0 copy-start.5
  6.6 0.0 copy-start.7
  6.7 2.0 %collective-permute-done.first = bf16[64,512]{1,0:T(8,128)(2,1)S(1)} collective-permute-done((bf16[64,512]{1,0:T(8,128)(2,1)}, bf16[64,512]{1,0:T(8,128)(2,1)S(1)}, u32[]{:S(2)}, u32[]{:S(2)}) %collective-permute-start) | collective-permute-done | bytes 65568 | tf_op jit(solution)/shard_map/ppermute | solution.py:330
  8.7 0.0 collective-permute-done.1.second
  8.7 0.0 collective-permute-done.2.third
  8.7 1.2 %project.1 = bf16[16,80,128]{2,1,0:T(8,128)(2,1)} custom-call(bf16[64,512]{1,0:T(8,128)(2,1)S(1)} %get-tuple-element.14.own, bf16[64,512]{1,0:T(8,128)(2,1)S(1)} %collective-permute-done.first, bf16[64,512]{1,0:T(8,128)(2,1)S(1)} %collective-permute-done.1.second, bf16[64,512]{1,0:T(8,128)(2,1)S(1)} %collective-permute-done.2.third, ...), custom_call_target="tpu_custom_call" | custom-call | tf_op jit(solution)/shard_map/project/pallas_call | solution.py:339
  9.9 0.0 copy-start.2
  9.9 15.2 %all-to-all-start = ((bf16[16,80,128]{2,1,0:T(8,128)(2,1)}), bf16[16,80,128]{2,1,0:T(8,128)(2,1)S(1)}, u32[]{:S(2)}, u32[]{:S(2)}) async-start(bf16[16,80,128]{2,1,0:T(8,128)(2,1)} %project.1), calls=%async_computation | async-start | bytes 655360 | tf_op jit(solution)/shard_map/all_to_all | solution.py:293
  25.1 0.0 copy-done.3
  25.1 0.0 copy-done.6
  25.1 0.0 copy-start.1
  25.1 1.0 %copy-done.1 = bf16[32,7680]{1,0:T(8,128)(2,1)S(1)} copy-done((bf16[32,7680]{1,0:T(8,128)(2,1)S(1)}, bf16[32,7680]{1,0:T(8,128)(2,1)}, u32[]{:S(2)}) %copy-start.1) | copy-done | bytes 491544
  26.2 1.3 %grammar.1 = (bf16[32,7680]{1,0:T(8,128)(2,1)S(1)}, bf16[16,128]{1,0:T(8,128)(2,1)S(1)}) custom-call(bf16[32,7680]{1,0:T(8,128)(2,1)S(1)} %copy-done.1, s32[1,32]{1,0:T(1,128)S(1)} %bitcast.2, s32[24,256]{1,0:T(8,128)S(1)} %copy-done.3), custom_call_target="tpu_custom_call" | custom-call | tf_op jit(solution)/shard_map/grammar/pallas_call | solution.py:348
  27.5 17.4 %all-to-all-done.received.pieces = bf16[16,80,128]{2,1,0:T(8,128)(2,1)S(1)} async-done(((bf16[16,80,128]{2,1,0:T(8,128)(2,1)}), bf16[16,80,128]{2,1,0:T(8,128)(2,1)S(1)}, u32[]{:S(2)}, u32[]{:S(2)}) %all-to-all-start) | async-done | bytes 327712 | tf_op jit(solution)/shard_map/all_to_all | solution.py:293
  44.9 0.0 copy-done
  44.9 0.0 copy-done.4
  44.9 0.0 copy-done.5
  44.9 0.0 copy-done.7
  44.9 1.4 %cached.1 = bf16[16,16,128]{2,1,0:T(8,128)(2,1)} custom-call(s32[1,2]{1,0:T(1,128)S(1)} %bitcast.3, bf16[16,80,128]{2,1,0:T(8,128)(2,1)S(1)} %all-to-all-done.received.pieces, bf16[2,128,2048]{2,1,0:T(8,128)(2,1)S(1)} %copy-done, bf16[16,128]{1,0:T(8,128)(2,1)S(1)} %get-tuple-element.19.terms, s32[8,16]{1,0:T(8,128)S(1)} %copy-done.4, s32[8,16]{1,0:T(8,128)S(1)} %copy-done.5), custom_call_target="tpu_custom_call" | custom-call | tf_op jit(solution)/shard_map/cached/pallas_call | solution.py:363
  46.3 6.0 %all-to-all-start.1 = ((bf16[16,16,128]{2,1,0:T(8,128)(2,1)}), bf16[16,16,128]{2,1,0:T(8,128)(2,1)S(1)}, u32[]{:S(2)}, u32[]{:S(2)}) async-start(bf16[16,16,128]{2,1,0:T(8,128)(2,1)} %cached.1), calls=%async_computation.1 | async-start | bytes 131072 | tf_op jit(solution)/shard_map/all_to_all | solution.py:293
  52.4 3.8 %collective-permute-start.3 = (bf16[64,128]{1,0:T(8,128)(2,1)S(1)}, bf16[64,128]{1,0:T(8,128)(2,1)S(1)}, u32[]{:S(2)}, u32[]{:S(2)}) collective-permute-start(bf16[64,128]{1,0:T(8,128)(2,1)S(1)} %reduce.1), channel_id=1, source_target_pairs={{0,1},{1,0},{2,3},{3,2},{4,5},{5,4},{6,7},{7,6},{8,9},{9,8},{10,11... | collective-permute-start | bytes 49160 | tf_op jit(solution)/shard_map/ppermute | solution.py:362
  56.2 2.1 %collective-permute-done.3 = bf16[64,128]{1,0:T(8,128)(2,1)S(1)} collective-permute-done((bf16[64,128]{1,0:T(8,128)(2,1)S(1)}, bf16[64,128]{1,0:T(8,128)(2,1)S(1)}, u32[]{:S(2)}, u32[]{:S(2)}) %collective-permute-start.3) | collective-permute-done | bytes 16416 | tf_op jit(solution)/shard_map/ppermute | solution.py:362
  58.3 7.5 %collective-permute-start.4 = (bf16[128,128]{1,0:T(8,128)(2,1)S(1)}, bf16[128,128]{1,0:T(8,128)(2,1)S(1)}, u32[]{:S(2)}, u32[]{:S(2)}) collective-permute-start(bf16[128,128]{1,0:T(8,128)(2,1)S(1)} %pad_maximum_fusion.here), channel_id=1, source_target_pairs={{0,256},{128,384},{384,128},{1,257},{129,385},{385,129},{2,258},{1... | collective-permute-start | bytes 98312 | tf_op jit(solution)/shard_map/ppermute | solution.py:374
  65.8 1.9 %collective-permute-start.5 = (bf16[128,128]{1,0:T(8,128)(2,1)S(1)}, bf16[128,128]{1,0:T(8,128)(2,1)S(1)}, u32[]{:S(2)}, u32[]{:S(2)}) collective-permute-start(bf16[128,128]{1,0:T(8,128)(2,1)S(1)} %pad_maximum_fusion.here), channel_id=1, source_target_pairs={{0,128},{128,256},{256,384},{1,129},{129,257},{257,385},{2,130},{1... | collective-permute-start | bytes 98312 | tf_op jit(solution)/shard_map/ppermute | solution.py:374
  67.7 1.3 %collective-permute-start.6 = (bf16[128,128]{1,0:T(8,128)(2,1)S(1)}, bf16[128,128]{1,0:T(8,128)(2,1)S(1)}, u32[]{:S(2)}, u32[]{:S(2)}) collective-permute-start(bf16[128,128]{1,0:T(8,128)(2,1)S(1)} %pad_maximum_fusion.here), channel_id=1, source_target_pairs={{0,384},{256,128},{384,256},{1,385},{257,129},{385,257},{2,386},{2... | collective-permute-start | bytes 98312 | tf_op jit(solution)/shard_map/ppermute | solution.py:374
  69.0 0.0 collective-permute-done.4.second
  69.0 2.6 %collective-permute-done.5.first = bf16[128,128]{1,0:T(8,128)(2,1)S(1)} collective-permute-done((bf16[128,128]{1,0:T(8,128)(2,1)S(1)}, bf16[128,128]{1,0:T(8,128)(2,1)S(1)}, u32[]{:S(2)}, u32[]{:S(2)}) %collective-permute-start.5) | collective-permute-done | bytes 32800 | tf_op jit(solution)/shard_map/ppermute | solution.py:374
  71.6 1.9 %collective-permute-done.6.third = bf16[128,128]{1,0:T(8,128)(2,1)S(1)} collective-permute-done((bf16[128,128]{1,0:T(8,128)(2,1)S(1)}, bf16[128,128]{1,0:T(8,128)(2,1)S(1)}, u32[]{:S(2)}, u32[]{:S(2)}) %collective-permute-start.6) | collective-permute-done | bytes 32800 | tf_op jit(solution)/shard_map/ppermute | solution.py:374
  73.5 0.0 copy-done.2
  73.5 0.4 prompts.1
  73.9 0.0 all-to-all-done.1.received
  73.9 2.0 %finish.1 = (f32[32,7680]{1,0:T(8,128)}, bf16[32,512]{1,0:T(8,128)(2,1)}) custom-call(bf16[32,7680]{1,0:T(8,128)(2,1)S(1)} %get-tuple-element.13.masked, bf16[16,16,128]{2,1,0:T(8,128)(2,1)S(1)} %all-to-all-done.1.received, bf16[32,512]{1,0:T(8,128)(2,1)S(1)} %copy-done.2, f32[128,128]{1,0:T(8,128)S(1)} %get-tuple-element.20.result, ...), custom_call_target="tpu_custom_call" | custom-call | tf_op jit(solution)/shard_map/finish/pallas_call | solution.py:382
  (2 shorter events, 0.0 us)
Async XLA Ops:
  2.3 6.4 %collective-permute-start = (bf16[64,512]{1,0:T(8,128)(2,1)}, bf16[64,512]{1,0:T(8,128)(2,1)S(1)}, u32[]{:S(2)}, u32[]{:S(2)}) collective-permute-start(bf16[64,512]{1,0:T(8,128)(2,1)} %get-tuple-element.15), channel_id=1, source_target_pairs={{0,128},{1,129},{2,130},{3,131},{4,132},{5,133},{6,134},{7,135},{8... | collective-permute-start | bytes 196616 | tf_op jit(solution)/shard_map/ppermute | solution.py:330
  3.6 5.1 %collective-permute-start.1 = (bf16[64,512]{1,0:T(8,128)(2,1)}, bf16[64,512]{1,0:T(8,128)(2,1)S(1)}, u32[]{:S(2)}, u32[]{:S(2)}) collective-permute-start(bf16[64,512]{1,0:T(8,128)(2,1)} %get-tuple-element.16), channel_id=1, source_target_pairs={{0,256},{1,257},{2,258},{3,259},{4,260},{5,261},{6,262},{7,263},{8... | collective-permute-start | bytes 196616 | tf_op jit(solution)/shard_map/ppermute | solution.py:330
  4.3 4.4 %collective-permute-start.2 = (bf16[64,512]{1,0:T(8,128)(2,1)}, bf16[64,512]{1,0:T(8,128)(2,1)S(1)}, u32[]{:S(2)}, u32[]{:S(2)}) collective-permute-start(bf16[64,512]{1,0:T(8,128)(2,1)} %get-tuple-element.17), channel_id=1, source_target_pairs={{0,384},{1,385},{2,386},{3,387},{4,388},{5,389},{6,390},{7,391},{8... | collective-permute-start | bytes 196616 | tf_op jit(solution)/shard_map/ppermute | solution.py:330
  6.6 18.5 %copy-start.3 = (s32[24,256]{1,0:T(8,128)S(1)}, s32[24,256]{1,0:T(8,128)}, u32[]{:S(2)}) copy-start(s32[24,256]{1,0:T(8,128)} %masks.1) | copy-start | bytes 73732
  6.6 18.5 %copy-start.6 = (s32[32]{0:T(128)S(1)}, s32[32]{0:T(128)}, u32[]{:S(2)}) copy-start(s32[32]{0:T(128)} %param.20) | copy-start | bytes 388
  6.6 38.3 %copy-start = (bf16[2,128,2048]{2,1,0:T(8,128)(2,1)S(1)}, bf16[2,128,2048]{2,1,0:T(8,128)(2,1)}, u32[]{:S(2)}) copy-start(bf16[2,128,2048]{2,1,0:T(8,128)(2,1)} %cache.1) | copy-start | bytes 3145732
  6.6 38.3 %copy-start.4 = (s32[8,16]{1,0:T(8,128)S(1)}, s32[8,16]{1,0:T(8,128)}, u32[]{:S(2)}) copy-start(s32[8,16]{1,0:T(8,128)} %lengths.3) | copy-start | bytes 1540
  6.6 38.3 %copy-start.5 = (s32[8,16]{1,0:T(8,128)S(1)}, s32[8,16]{1,0:T(8,128)}, u32[]{:S(2)}) copy-start(s32[8,16]{1,0:T(8,128)} %owners.3) | copy-start | bytes 1540
  6.6 38.2 %copy-start.7 = (s32[2]{0:T(128)S(1)}, s32[2]{0:T(128)}, u32[]{:S(2)}) copy-start(s32[2]{0:T(128)} %param.16) | copy-start | bytes 28
  9.9 63.6 %copy-start.2 = (bf16[32,512]{1,0:T(8,128)(2,1)S(1)}, bf16[32,512]{1,0:T(8,128)(2,1)}, u32[]{:S(2)}) copy-start(bf16[32,512]{1,0:T(8,128)(2,1)} %queries.5) | copy-start | bytes 98308
  9.9 35.0 %all-to-all-start = ((bf16[16,80,128]{2,1,0:T(8,128)(2,1)}), bf16[16,80,128]{2,1,0:T(8,128)(2,1)S(1)}, u32[]{:S(2)}, u32[]{:S(2)}) async-start(bf16[16,80,128]{2,1,0:T(8,128)(2,1)} %project.1), calls=%async_computation | async-start | bytes 655360 | tf_op jit(solution)/shard_map/all_to_all | solution.py:293
  25.1 1.0 %copy-start.1 = (bf16[32,7680]{1,0:T(8,128)(2,1)S(1)}, bf16[32,7680]{1,0:T(8,128)(2,1)}, u32[]{:S(2)}) copy-start(bf16[32,7680]{1,0:T(8,128)(2,1)} %logits.1) | copy-start | bytes 1474564
  46.3 27.6 %all-to-all-start.1 = ((bf16[16,16,128]{2,1,0:T(8,128)(2,1)}), bf16[16,16,128]{2,1,0:T(8,128)(2,1)S(1)}, u32[]{:S(2)}, u32[]{:S(2)}) async-start(bf16[16,16,128]{2,1,0:T(8,128)(2,1)} %cached.1), calls=%async_computation.1 | async-start | bytes 131072 | tf_op jit(solution)/shard_map/all_to_all | solution.py:293
  52.4 5.9 %collective-permute-start.3 = (bf16[64,128]{1,0:T(8,128)(2,1)S(1)}, bf16[64,128]{1,0:T(8,128)(2,1)S(1)}, u32[]{:S(2)}, u32[]{:S(2)}) collective-permute-start(bf16[64,128]{1,0:T(8,128)(2,1)S(1)} %reduce.1), channel_id=1, source_target_pairs={{0,1},{1,0},{2,3},{3,2},{4,5},{5,4},{6,7},{7,6},{8,9},{9,8},{10,11... | collective-permute-start | bytes 49160 | tf_op jit(solution)/shard_map/ppermute | solution.py:362
  58.3 10.7 %collective-permute-start.4 = (bf16[128,128]{1,0:T(8,128)(2,1)S(1)}, bf16[128,128]{1,0:T(8,128)(2,1)S(1)}, u32[]{:S(2)}, u32[]{:S(2)}) collective-permute-start(bf16[128,128]{1,0:T(8,128)(2,1)S(1)} %pad_maximum_fusion.here), channel_id=1, source_target_pairs={{0,256},{128,384},{384,128},{1,257},{129,385},{385,129},{2,258},{1... | collective-permute-start | bytes 98312 | tf_op jit(solution)/shard_map/ppermute | solution.py:374
  65.8 5.8 %collective-permute-start.5 = (bf16[128,128]{1,0:T(8,128)(2,1)S(1)}, bf16[128,128]{1,0:T(8,128)(2,1)S(1)}, u32[]{:S(2)}, u32[]{:S(2)}) collective-permute-start(bf16[128,128]{1,0:T(8,128)(2,1)S(1)} %pad_maximum_fusion.here), channel_id=1, source_target_pairs={{0,128},{128,256},{256,384},{1,129},{129,257},{257,385},{2,130},{1... | collective-permute-start | bytes 98312 | tf_op jit(solution)/shard_map/ppermute | solution.py:374
  67.7 5.8 %collective-permute-start.6 = (bf16[128,128]{1,0:T(8,128)(2,1)S(1)}, bf16[128,128]{1,0:T(8,128)(2,1)S(1)}, u32[]{:S(2)}, u32[]{:S(2)}) collective-permute-start(bf16[128,128]{1,0:T(8,128)(2,1)S(1)} %pad_maximum_fusion.here), channel_id=1, source_target_pairs={{0,384},{256,128},{384,256},{1,385},{257,129},{385,257},{2,386},{2... | collective-permute-start | bytes 98312 | tf_op jit(solution)/shard_map/ppermute | solution.py:374

commit v7 on v6

--- a/solution.py
+++ b/solution.py
@@ -225,21 +225,20 @@
     out[...] = result.astype(BF16).reshape(16, 16, HD)
 
 
-def attend_prompts(here, second, first, third, queries, lengths, owners, result, stats):
-    turn = lax.axis_index("x")
-    prompts = prompts_of(lengths[...], owners[...], lax.axis_index("c8"), turn)
+def attend_prompts(parts, queries, lengths, owners, result, stats):
+    prompts = prompts_of(
+        lengths[...], owners[...], lax.axis_index("c8"), lax.axis_index("x")
+    )
     request = iota((128, 1), 0) % 32
     landed, start, length = landing((request % 2) * 16 + request // 2, prompts)
     even = lax.axis_index("zl") == 0
-    parts = (here, first, second, third)
-    mine = jnp.concatenate([part[0:64] for part in parts], axis=0)
-    other = jnp.concatenate([part[64:128] for part in parts], axis=0)
+    mine = jnp.concatenate([parts[x, 0:64] for x in range(4)], axis=0)
+    other = jnp.concatenate([parts[x, 64:128] for x in range(4)], axis=0)
     keys = jnp.where(even, mine, other)
     values = jnp.where(even, other, mine)
     query = jnp.concatenate([queries[:, HD * i : HD * (i + 1)] for i in range(4)], axis=0)
     score = transposed(query, keys) * SCALE
-    lane = iota((128, 256), 1)
-    position = ((turn + 4 - lane // 64) % 4 * 64 + lane % 64).astype(F32)
+    position = iota((128, 256), 1).astype(F32)
     alive = (position >= start) & (position < start + length)
     highest = jnp.max(jnp.where(alive, score, LOWEST), axis=1, keepdims=True)
     exponent = jnp.where(alive, jnp.exp(score - highest), 0.0)
@@ -326,7 +325,7 @@
         ],
         name="prepare",
     )(hidden, queries, fresh)
-    for k in (2, 1, 3):
+    for k in (1, 3, 2):
         shares[k] = lax.ppermute(shares[k], "x", [(0, k)])
     weight = pl.pallas_call(
         fetch,
@@ -368,17 +367,14 @@
     )(*held(cache_len.reshape(1, 2), pieces, cache, terms, prompt_lengths, owner_step))
     answers = exchanged(answers, TP)
     both = jnp.concatenate([block, other], axis=0)
-    around = [both]
-    for k in (2, 1, 3):
-        route = [(i, (i + k) % 4) for i in range(4) if (i + k) % 4]
-        around.append(lax.ppermute(both, "x", route))
+    around = lax.all_gather(both, "x")
     result, stats = pl.pallas_call(
         attend_prompts,
         out_shape=[kept((128, HD), F32), kept((128, HD), F32)],
-        in_specs=[vmem] * 7,
+        in_specs=[vmem] * 4,
         out_specs=[vmem] * 2,
         name="prompts",
-    )(*held(*around, queries, prompt_lengths, owner_step))
+    )(*held(around, queries, prompt_lengths, owner_step))
     logprob, attended = pl.pallas_call(
         finish,
         out_shape=[sent(logits.shape, F32), sent(queries.shape, BF16)],

time: 76.5 us -> 76.7 us (level)
  the two profiles are of different devices: /device:TPU:18 before, /device:TPU:24 now
where the time goes in v7:
time: 76.7 us; the launch traced here: 75.8 us
  starting transfers between devices  31.8 us (41%)
  waiting for transfers between devices  20.5 us (27%)
  blocking collectives  12 us (16%)
  Pallas kernels  9.55 us (12%)
  local copies, waits for them, and re-layouts  1.07 us (1%)
  between operations  0.84 us (1%)
    all_to_all x2, starting transfers between devices, exchanged(): return lax.all_to_all(slots, axis, 0, 0, tiled=True)  21.1 us
    all_to_all x2, waiting for transfers between devices, exchanged(): return lax.all_to_all(slots, axis, 0, 0, tiled=True)  18 us
    all_gather x1, blocking collectives, per_device(): around = lax.all_gather(both, 'x')  12 us
    ppermute x3, starting transfers between devices, per_device(): shares[k] = lax.ppermute(shares[k], 'x', [(0, k)])  6.89 us
    ppermute x1, starting transfers between devices, per_device(): other = lax.ppermute(block, 'zl', [(0, 1), (1, 0)])  3.83 us
    ppermute x1, waiting for transfers between devices, per_device(): other = lax.ppermute(block, 'zl', [(0, 1), (1, 0)])  2.03 us
    pallas_call x1, Pallas kernels, per_device(): pl.pallas_call(finish, out_shape=[sent(logits.shape, F32), sent(queries.s...  1.97 us
    pallas_call x1, Pallas kernels, per_device(): pl.pallas_call(prepare, out_shape=[kept((tokens, wide), BF16)] * 4 + [kep...  1.68 us
  transfers between devices with their start and end apart: 6, of which 3 were waited for; matrix products, arithmetic and copies ran while one was open for 0% of the time, Pallas kernels for 4%

profile of v7, /device:TPU:24, one launch (start us, length us, event | category | flops | bytes accessed | tf_op | source)
XLA Modules:
  0.0 75.8 jit_solution(677294121859968430)
XLA Ops:
  0.6 1.7 %prepare.1 = (bf16[64,512]{1,0:T(8,128)(2,1)S(1)}, bf16[64,512]{1,0:T(8,128)(2,1)}, bf16[64,512]{1,0:T(8,128)(2,1)}, bf16[64,512]{1,0:T(8,128)(2,1)}, bf16[16,16,128]{2,1,0:T(8,128)(2,1)S(1)}) custom-call(bf16[256,512]{1,0:T(8,128)(2,1)} %hidden.1, bf16[32,512]{1,0:T(8,128)(2,1)} %queries.5, bf16[32,128]{1,0:T(8,128)(2,1)} %fresh.1), custom_call_target="tpu_custom_call" | custom-call | tf_op jit(solution)/shard_map/prepare/pallas_call | solution.py:316
  2.3 3.4 %collective-permute-start = (bf16[64,512]{1,0:T(8,128)(2,1)}, bf16[64,512]{1,0:T(8,128)(2,1)S(1)}, u32[]{:S(2)}, u32[]{:S(2)}) collective-permute-start(bf16[64,512]{1,0:T(8,128)(2,1)} %get-tuple-element.15), channel_id=1, source_target_pairs={{0,128},{1,129},{2,130},{3,131},{4,132},{5,133},{6,134},{7,135},{8... | collective-permute-start | bytes 196616 | tf_op jit(solution)/shard_map/ppermute | solution.py:329
  5.7 2.2 %collective-permute-start.1 = (bf16[64,512]{1,0:T(8,128)(2,1)}, bf16[64,512]{1,0:T(8,128)(2,1)S(1)}, u32[]{:S(2)}, u32[]{:S(2)}) collective-permute-start(bf16[64,512]{1,0:T(8,128)(2,1)} %get-tuple-element.16), channel_id=1, source_target_pairs={{0,256},{1,257},{2,258},{3,259},{4,260},{5,261},{6,262},{7,263},{8... | collective-permute-start | bytes 196616 | tf_op jit(solution)/shard_map/ppermute | solution.py:329
  7.9 1.3 %collective-permute-start.2 = (bf16[64,512]{1,0:T(8,128)(2,1)}, bf16[64,512]{1,0:T(8,128)(2,1)S(1)}, u32[]{:S(2)}, u32[]{:S(2)}) collective-permute-start(bf16[64,512]{1,0:T(8,128)(2,1)} %get-tuple-element.17), channel_id=1, source_target_pairs={{0,384},{1,385},{2,386},{3,387},{4,388},{5,389},{6,390},{7,391},{8... | collective-permute-start | bytes 196616 | tf_op jit(solution)/shard_map/ppermute | solution.py:329
  9.2 1.6 %fetch.1.weight = bf16[512,2048]{1,0:T(8,128)(2,1)S(1)} custom-call(bf16[512,2048]{1,0:T(8,128)(2,1)} %weight.1), custom_call_target="tpu_custom_call" | custom-call | tf_op jit(solution)/shard_map/fetch/pallas_call | solution.py:330
  10.8 0.0 copy-start.3
  10.9 0.0 copy-start.6
  10.9 0.0 copy-start
  10.9 0.0 copy-start.4
  10.9 0.0 copy-start.5
  10.9 0.0 copy-start.7
  10.9 0.0 collective-permute-done.first
  10.9 0.0 collective-permute-done.1.second
  10.9 0.5 collective-permute-done.2.third
  11.4 1.2 %project.1 = bf16[16,80,128]{2,1,0:T(8,128)(2,1)} custom-call(bf16[64,512]{1,0:T(8,128)(2,1)S(1)} %get-tuple-element.14.own, bf16[64,512]{1,0:T(8,128)(2,1)S(1)} %collective-permute-done.first, bf16[64,512]{1,0:T(8,128)(2,1)S(1)} %collective-permute-done.1.second, bf16[64,512]{1,0:T(8,128)(2,1)S(1)} %collective-permute-done.2.third, ...), custom_call_target="tpu_custom_call" | custom-call | tf_op jit(solution)/shard_map/project/pallas_call | solution.py:338
  12.6 0.0 copy-start.2
  12.6 15.2 %all-to-all-start = ((bf16[16,80,128]{2,1,0:T(8,128)(2,1)}), bf16[16,80,128]{2,1,0:T(8,128)(2,1)S(1)}, u32[]{:S(2)}, u32[]{:S(2)}) async-start(bf16[16,80,128]{2,1,0:T(8,128)(2,1)} %project.1), calls=%async_computation | async-start | bytes 655360 | tf_op jit(solution)/shard_map/all_to_all | solution.py:292
  27.8 0.0 copy-done.3
  27.8 0.0 copy-done.6
  27.9 0.0 copy-start.1
  27.9 1.0 %copy-done.1 = bf16[32,7680]{1,0:T(8,128)(2,1)S(1)} copy-done((bf16[32,7680]{1,0:T(8,128)(2,1)S(1)}, bf16[32,7680]{1,0:T(8,128)(2,1)}, u32[]{:S(2)}) %copy-start.1) | copy-done | bytes 491544
  28.9 1.3 %grammar.1 = (bf16[32,7680]{1,0:T(8,128)(2,1)S(1)}, bf16[16,128]{1,0:T(8,128)(2,1)S(1)}) custom-call(bf16[32,7680]{1,0:T(8,128)(2,1)S(1)} %copy-done.1, s32[1,32]{1,0:T(1,128)S(1)} %bitcast.4, s32[24,256]{1,0:T(8,128)S(1)} %copy-done.3), custom_call_target="tpu_custom_call" | custom-call | tf_op jit(solution)/shard_map/grammar/pallas_call | solution.py:347
  30.2 18.0 %all-to-all-done.received.pieces = bf16[16,80,128]{2,1,0:T(8,128)(2,1)S(1)} async-done(((bf16[16,80,128]{2,1,0:T(8,128)(2,1)}), bf16[16,80,128]{2,1,0:T(8,128)(2,1)S(1)}, u32[]{:S(2)}, u32[]{:S(2)}) %all-to-all-start) | async-done | bytes 327712 | tf_op jit(solution)/shard_map/all_to_all | solution.py:292
  48.1 0.0 copy-done
  48.2 0.0 copy-done.4
  48.2 0.0 copy-done.5
  48.2 0.0 copy-done.7
  48.2 1.4 %cached.1 = bf16[16,16,128]{2,1,0:T(8,128)(2,1)} custom-call(s32[1,2]{1,0:T(1,128)S(1)} %bitcast.5, bf16[16,80,128]{2,1,0:T(8,128)(2,1)S(1)} %all-to-all-done.received.pieces, bf16[2,128,2048]{2,1,0:T(8,128)(2,1)S(1)} %copy-done, bf16[16,128]{1,0:T(8,128)(2,1)S(1)} %get-tuple-element.19.terms, s32[8,16]{1,0:T(8,128)S(1)} %copy-done.4, s32[8,16]{1,0:T(8,128)S(1)} %copy-done.5), custom_call_target="tpu_custom_call" | custom-call | tf_op jit(solution)/shard_map/cached/pallas_call | solution.py:362
  49.6 5.9 %all-to-all-start.1 = ((bf16[16,16,128]{2,1,0:T(8,128)(2,1)}), bf16[16,16,128]{2,1,0:T(8,128)(2,1)S(1)}, u32[]{:S(2)}, u32[]{:S(2)}) async-start(bf16[16,16,128]{2,1,0:T(8,128)(2,1)} %cached.1), calls=%async_computation.1 | async-start | bytes 131072 | tf_op jit(solution)/shard_map/all_to_all | solution.py:292
  55.5 3.8 %collective-permute-start.3 = (bf16[64,128]{1,0:T(8,128)(2,1)S(1)}, bf16[64,128]{1,0:T(8,128)(2,1)S(1)}, u32[]{:S(2)}, u32[]{:S(2)}) collective-permute-start(bf16[64,128]{1,0:T(8,128)(2,1)S(1)} %reduce.1), channel_id=1, source_target_pairs={{0,1},{1,0},{2,3},{3,2},{4,5},{5,4},{6,7},{7,6},{8,9},{9,8},{10,11... | collective-permute-start | bytes 49160 | tf_op jit(solution)/shard_map/ppermute | solution.py:361
  59.3 2.0 %collective-permute-done.3 = bf16[64,128]{1,0:T(8,128)(2,1)S(1)} collective-permute-done((bf16[64,128]{1,0:T(8,128)(2,1)S(1)}, bf16[64,128]{1,0:T(8,128)(2,1)S(1)}, u32[]{:S(2)}, u32[]{:S(2)}) %collective-permute-start.3) | collective-permute-done | bytes 16416 | tf_op jit(solution)/shard_map/ppermute | solution.py:361
  61.4 12.0 %all-gather = bf16[512,128]{1,0:T(8,128)(2,1)S(1)} all-gather(bf16[128,128]{1,0:T(8,128)(2,1)S(1)} %pad_maximum_fusion), channel_id=2, replica_groups=mesh['x'=4,'c8'=8,'zh'=8,'zl'=2] {'x'}, dimensions={0}, use_global_device_ids=true | all-gather | bytes 163840 | tf_op jit(solution)/shard_map/all_gather | solution.py:370
  73.3 0.0 copy-done.2
  73.3 0.4 prompts.1
  73.8 0.0 all-to-all-done.1.received
  73.8 2.0 %finish.1 = (f32[32,7680]{1,0:T(8,128)}, bf16[32,512]{1,0:T(8,128)(2,1)}) custom-call(bf16[32,7680]{1,0:T(8,128)(2,1)S(1)} %get-tuple-element.13.masked, bf16[16,16,128]{2,1,0:T(8,128)(2,1)S(1)} %all-to-all-done.1.received, bf16[32,512]{1,0:T(8,128)(2,1)S(1)} %copy-done.2, f32[128,128]{1,0:T(8,128)S(1)} %get-tuple-element.20.result, ...), custom_call_target="tpu_custom_call" | custom-call | tf_op jit(solution)/shard_map/finish/pallas_call | solution.py:378
  (2 shorter events, 0.0 us)
Async XLA Ops:
  2.3 8.6 %collective-permute-start = (bf16[64,512]{1,0:T(8,128)(2,1)}, bf16[64,512]{1,0:T(8,128)(2,1)S(1)}, u32[]{:S(2)}, u32[]{:S(2)}) collective-permute-start(bf16[64,512]{1,0:T(8,128)(2,1)} %get-tuple-element.15), channel_id=1, source_target_pairs={{0,128},{1,129},{2,130},{3,131},{4,132},{5,133},{6,134},{7,135},{8... | collective-permute-start | bytes 196616 | tf_op jit(solution)/shard_map/ppermute | solution.py:329
  5.7 5.2 %collective-permute-start.1 = (bf16[64,512]{1,0:T(8,128)(2,1)}, bf16[64,512]{1,0:T(8,128)(2,1)S(1)}, u32[]{:S(2)}, u32[]{:S(2)}) collective-permute-start(bf16[64,512]{1,0:T(8,128)(2,1)} %get-tuple-element.16), channel_id=1, source_target_pairs={{0,256},{1,257},{2,258},{3,259},{4,260},{5,261},{6,262},{7,263},{8... | collective-permute-start | bytes 196616 | tf_op jit(solution)/shard_map/ppermute | solution.py:329
  7.9 3.5 %collective-permute-start.2 = (bf16[64,512]{1,0:T(8,128)(2,1)}, bf16[64,512]{1,0:T(8,128)(2,1)S(1)}, u32[]{:S(2)}, u32[]{:S(2)}) collective-permute-start(bf16[64,512]{1,0:T(8,128)(2,1)} %get-tuple-element.17), channel_id=1, source_target_pairs={{0,384},{1,385},{2,386},{3,387},{4,388},{5,389},{6,390},{7,391},{8... | collective-permute-start | bytes 196616 | tf_op jit(solution)/shard_map/ppermute | solution.py:329
  10.8 17.0 %copy-start.3 = (s32[24,256]{1,0:T(8,128)S(1)}, s32[24,256]{1,0:T(8,128)}, u32[]{:S(2)}) copy-start(s32[24,256]{1,0:T(8,128)} %masks.1) | copy-start | bytes 73732
  10.9 17.0 %copy-start.6 = (s32[32]{0:T(128)S(1)}, s32[32]{0:T(128)}, u32[]{:S(2)}) copy-start(s32[32]{0:T(128)} %param.20) | copy-start | bytes 388
  10.9 37.3 %copy-start = (bf16[2,128,2048]{2,1,0:T(8,128)(2,1)S(1)}, bf16[2,128,2048]{2,1,0:T(8,128)(2,1)}, u32[]{:S(2)}) copy-start(bf16[2,128,2048]{2,1,0:T(8,128)(2,1)} %cache.1) | copy-start | bytes 3145732
  10.9 37.3 %copy-start.4 = (s32[8,16]{1,0:T(8,128)S(1)}, s32[8,16]{1,0:T(8,128)}, u32[]{:S(2)}) copy-start(s32[8,16]{1,0:T(8,128)} %lengths.3) | copy-start | bytes 1540
  10.9 37.3 %copy-start.5 = (s32[8,16]{1,0:T(8,128)S(1)}, s32[8,16]{1,0:T(8,128)}, u32[]{:S(2)}) copy-start(s32[8,16]{1,0:T(8,128)} %owners.3) | copy-start | bytes 1540
  10.9 37.3 %copy-start.7 = (s32[2]{0:T(128)S(1)}, s32[2]{0:T(128)}, u32[]{:S(2)}) copy-start(s32[2]{0:T(128)} %param.16) | copy-start | bytes 28
  12.6 60.7 %copy-start.2 = (bf16[32,512]{1,0:T(8,128)(2,1)S(1)}, bf16[32,512]{1,0:T(8,128)(2,1)}, u32[]{:S(2)}) copy-start(bf16[32,512]{1,0:T(8,128)(2,1)} %queries.5) | copy-start | bytes 98308
  12.6 35.5 %all-to-all-start = ((bf16[16,80,128]{2,1,0:T(8,128)(2,1)}), bf16[16,80,128]{2,1,0:T(8,128)(2,1)S(1)}, u32[]{:S(2)}, u32[]{:S(2)}) async-start(bf16[16,80,128]{2,1,0:T(8,128)(2,1)} %project.1), calls=%async_computation | async-start | bytes 655360 | tf_op jit(solution)/shard_map/all_to_all | solution.py:292
  27.9 1.0 %copy-start.1 = (bf16[32,7680]{1,0:T(8,128)(2,1)S(1)}, bf16[32,7680]{1,0:T(8,128)(2,1)}, u32[]{:S(2)}) copy-start(bf16[32,7680]{1,0:T(8,128)(2,1)} %logits.1) | copy-start | bytes 1474564
  49.6 24.2 %all-to-all-start.1 = ((bf16[16,16,128]{2,1,0:T(8,128)(2,1)}), bf16[16,16,128]{2,1,0:T(8,128)(2,1)S(1)}, u32[]{:S(2)}, u32[]{:S(2)}) async-start(bf16[16,16,128]{2,1,0:T(8,128)(2,1)} %cached.1), calls=%async_computation.1 | async-start | bytes 131072 | tf_op jit(solution)/shard_map/all_to_all | solution.py:292
  55.5 5.9 %collective-permute-start.3 = (bf16[64,128]{1,0:T(8,128)(2,1)S(1)}, bf16[64,128]{1,0:T(8,128)(2,1)S(1)}, u32[]{:S(2)}, u32[]{:S(2)}) collective-permute-start(bf16[64,128]{1,0:T(8,128)(2,1)S(1)} %reduce.1), channel_id=1, source_target_pairs={{0,1},{1,0},{2,3},{3,2},{4,5},{5,4},{6,7},{7,6},{8,9},{9,8},{10,11... | collective-permute-start | bytes 49160 | tf_op jit(solution)/shard_map/ppermute | solution.py:361

commit v8 on v7

--- a/solution.py
+++ b/solution.py
@@ -29,6 +29,11 @@
     return (iota((rows, width), 1) == target).astype(F32).astype(BF16)
 
 
+def kernel(body, **options):
+    limit = pltpu.CompilerParams(vmem_limit_bytes=16 << 20)
+    return pl.pallas_call(body, compiler_params=limit, **options)
+
+
 def pick(target, table):
     return jnp.dot(one_hot(target, table.shape[0]), table, preferred_element_type=F32)
 
@@ -55,21 +60,20 @@
     return jnp.sum(matched, axis=1, keepdims=True), total(start), total(length)
 
 
-def prepare(hidden, queries, fresh, own, first, second, third, asked, query, new, sems):
-    shares = [
+def cut(hidden, own, first, second, third, sems):
+    copies = [
         pltpu.make_async_copy(hidden.at[pl.ds(64 * k, 64)], out, sems.at[k])
         for k, out in enumerate((own, first, second, third))
     ]
-    loads = [
-        pltpu.make_async_copy(queries, query, sems.at[4]),
-        pltpu.make_async_copy(fresh, new, sems.at[5]),
-    ]
-    for copy in loads + shares:
+    for copy in copies:
         copy.start()
-    for copy in loads:
+    for copy in copies:
         copy.wait()
+
+
+def pack(queries, fresh, out):
     table = jnp.concatenate(
-        [query[:, HD * i : HD * (i + 1)] for i in range(4)] + [new[...]], axis=0
+        [queries[:, HD * i : HD * (i + 1)] for i in range(4)] + [fresh[...]], axis=0
     )
     row = iota((256, 1), 0)
     dest, k = row // 16, row % 16
@@ -78,15 +82,7 @@
         (k % 4) * 32 + 2 * dest + k // 4,
         jnp.where(k < 10, 128 + 2 * dest + k - 8, 160),
     )
-    asked[...] = pick(target, table).astype(BF16).reshape(16, 16, HD)
-    for copy in shares:
-        copy.wait()
-
-
-def fetch(weight, out, sem):
-    copy = pltpu.make_async_copy(weight, out, sem)
-    copy.start()
-    copy.wait()
+    out[...] = pick(target, table).astype(BF16).reshape(16, 16, HD)
 
 
 def project(own, first, second, third, asked, weight, out, slots, sems):
@@ -257,16 +253,6 @@
     normalizer = highest + jnp.log(total)
     row, lane = iota((32, 32), 0), iota((32, 32), 1)
     normalizer = jnp.sum(jnp.where(row == lane, normalizer, 0.0), axis=1, keepdims=True)
-    copies = []
-    for b in range(4):
-        at = slice(BLK * b, BLK * (b + 1))
-        section = masked[:, at].astype(F32)
-        values[:, at] = jnp.where(section == -jnp.inf, 0.0, section - normalizer)
-        piece = pl.ds(BLK * b, BLK)
-        copies.append(
-            pltpu.make_async_copy(values.at[:, piece], logprob.at[:, piece], sems.at[b])
-        )
-        copies[-1].start()
     row = iota((128, 1), 0)
     head, request = row // 32, row % 32
     query = jnp.concatenate([queries[:, HD * i : HD * (i + 1)] for i in range(4)], axis=0)
@@ -282,6 +268,16 @@
     scale = 1.0 / (total * share + own_share)
     merged = (result[...] * share + own_value * own_share) * scale
     merged = jnp.where(landed > 0.5, merged, cached).astype(BF16)
+    copies = []
+    for b in range(4):
+        at = slice(BLK * b, BLK * (b + 1))
+        section = masked[:, at].astype(F32)
+        values[:, at] = jnp.where(section == -jnp.inf, 0.0, section - normalizer)
+        piece = pl.ds(BLK * b, BLK)
+        copies.append(
+            pltpu.make_async_copy(values.at[:, piece], logprob.at[:, piece], sems.at[b])
+        )
+        copies[-1].start()
     for i in range(4):
         attended[:, HD * i : HD * (i + 1)] = merged[32 * i : 32 * (i + 1)]
     for copy in copies:
@@ -306,52 +302,48 @@
     masks,
 ):
     vmem = pl.BlockSpec(memory_space=pltpu.VMEM)
-    hbm = pl.BlockSpec(memory_space=pl.ANY)
+    hbm = pl.BlockSpec(memory_space=pltpu.HBM)
     sent = jax.ShapeDtypeStruct
     kept = pltpu.VMEM
     held = lambda *values: [
         pltpu.with_memory_space_constraint(value, pltpu.VMEM) for value in values
     ]
     tokens, wide = hidden.shape[0] // 4, hidden.shape[1]
-    *shares, asked = pl.pallas_call(
-        prepare,
-        out_shape=[kept((tokens, wide), BF16)] * 4 + [kept((16, 16, HD), BF16)],
-        in_specs=[hbm] * 3,
-        out_specs=[vmem] * 5,
-        scratch_shapes=[
-            pltpu.VMEM(queries.shape, BF16),
-            pltpu.VMEM(fresh.shape, BF16),
-            pltpu.SemaphoreType.DMA((6,)),
-        ],
-        name="prepare",
-    )(hidden, queries, fresh)
+    shares = list(kernel(
+        cut,
+        out_shape=[kept((tokens, wide), BF16)] * 4,
+        in_specs=[hbm],
+        out_specs=[vmem] * 4,
+        scratch_shapes=[pltpu.SemaphoreType.DMA((4,))],
+        name="cut",
+        cost_estimate=pl.CostEstimate(flops=2000000000, bytes_accessed=1000, transcendentals=0),
+    )(pltpu.with_memory_space_constraint(hidden, pltpu.HBM)))
     for k in (1, 3, 2):
         shares[k] = lax.ppermute(shares[k], "x", [(0, k)])
-    weight = pl.pallas_call(
-        fetch,
-        out_shape=kept(w_kv.shape, BF16),
-        in_specs=[hbm],
+    asked = kernel(
+        pack,
+        out_shape=kept((16, 16, HD), BF16),
+        in_specs=[vmem] * 2,
         out_specs=vmem,
-        scratch_shapes=[pltpu.SemaphoreType.DMA],
-        name="fetch",
-    )(w_kv)
-    projected = pl.pallas_call(
+        name="pack",
+    )(*held(queries, fresh))
+    projected = kernel(
         project,
-        out_shape=sent((16, 80, HD), BF16),
+        out_shape=pltpu.HBM((16, 80, HD), BF16),
         in_specs=[vmem] * 6,
         out_specs=hbm,
         scratch_shapes=[pltpu.VMEM((16, 80, HD), BF16), pltpu.SemaphoreType.DMA((4,))],
         name="project",
-    )(*held(*shares, asked, weight))
+    )(*held(*shares, asked, w_kv))
     pieces = exchanged(projected, TP)
-    masked, terms = pl.pallas_call(
+    masked, terms = kernel(
         grammar,
         out_shape=[kept(logits.shape, BF16), kept((16, HD), BF16)],
         in_specs=[vmem] * 3,
         out_specs=[vmem] * 2,
         name="grammar",
     )(*held(logits, states.reshape(1, -1), masks))
-    block = pl.pallas_call(
+    block = kernel(
         reduce_blocks,
         out_shape=kept((tokens, HD), BF16),
         in_specs=[vmem],
@@ -359,7 +351,7 @@
         name="reduce",
     )(*held(pieces))
     other = lax.ppermute(block, "zl", [(0, 1), (1, 0)])
-    answers = pl.pallas_call(
+    answers = kernel(
         attend_cached,
         out_shape=sent((16, 16, HD), BF16),
         in_specs=[vmem] * 6,
@@ -368,16 +360,16 @@
     answers = exchanged(answers, TP)
     both = jnp.concatenate([block, other], axis=0)
     around = lax.all_gather(both, "x")
-    result, stats = pl.pallas_call(
+    result, stats = kernel(
         attend_prompts,
         out_shape=[kept((128, HD), F32), kept((128, HD), F32)],
         in_specs=[vmem] * 4,
         out_specs=[vmem] * 2,
         name="prompts",
     )(*held(around, queries, prompt_lengths, owner_step))
-    logprob, attended = pl.pallas_call(
+    logprob, attended = kernel(
         finish,
-        out_shape=[sent(logits.shape, F32), sent(queries.shape, BF16)],
+        out_shape=[pltpu.HBM(logits.shape, F32), sent(queries.shape, BF16)],
         in_specs=[vmem] * 5,
         out_specs=[hbm, vmem],
         scratch_shapes=[pltpu.VMEM(logits.shape, F32), pltpu.SemaphoreType.DMA((4,))],

time: 76.7 us -> 76 us (level)
  waiting for transfers between devices: 20.5 us -> 22.6 us
  Pallas kernels: 9.55 us -> 7.59 us
  local copies, waits for them, and re-layouts: 1.07 us -> 0.06 us
    pallas_call x8, Pallas kernels: 9.55 us -> 7.59 us  [the longest x1 1.97 us: per_device(): kernel(finish, out_shape=[pltpu.HBM(logits.shape, F32), sent(queries.shap...]
    ppermute x3, waiting for transfers between devices: 0.5 us -> 1.66 us  [per_device(): shares[k] = lax.ppermute(shares[k], 'x', [(0, k)])]
    unnamed x16 -> x20, local copies, waits for them, and re-layouts: 1.07 us -> 0.06 us
    all_to_all x2, waiting for transfers between devices: 18 us -> 18.9 us  [exchanged(): return lax.all_to_all(slots, axis, 0, 0, tiled=True)]
  transfers between devices with their start and end apart: 6 -> 6, of which waited for: 3 -> 4; matrix products, arithmetic and copies ran while one was open for 0% -> 0% of each run, Pallas kernels for 4% -> 3%
where the time goes in v8:
time: 76 us; the launch traced here: 75.1 us
  starting transfers between devices  31.9 us (42%)
  waiting for transfers between devices  22.6 us (30%)
  blocking collectives  12.1 us (16%)
  Pallas kernels  7.59 us (10%)
  between operations  0.87 us (1%)
    all_to_all x2, starting transfers between devices, exchanged(): return lax.all_to_all(slots, axis, 0, 0, tiled=True)  21.1 us
    all_to_all x2, waiting for transfers between devices, exchanged(): return lax.all_to_all(slots, axis, 0, 0, tiled=True)  18.9 us
    all_gather x1, blocking collectives, per_device(): around = lax.all_gather(both, 'x')  12.1 us
    ppermute x3, starting transfers between devices, per_device(): shares[k] = lax.ppermute(shares[k], 'x', [(0, k)])  7.02 us
    ppermute x1, starting transfers between devices, per_device(): other = lax.ppermute(block, 'zl', [(0, 1), (1, 0)])  3.83 us
    ppermute x1, waiting for transfers between devices, per_device(): other = lax.ppermute(block, 'zl', [(0, 1), (1, 0)])  2.03 us
    pallas_call x1, Pallas kernels, per_device(): kernel(finish, out_shape=[pltpu.HBM(logits.shape, F32), sent(queries.shap...  1.97 us
    ppermute x3, waiting for transfers between devices, per_device(): shares[k] = lax.ppermute(shares[k], 'x', [(0, k)])  1.66 us
  transfers between devices with their start and end apart: 6, of which 4 were waited for; matrix products, arithmetic and copies ran while one was open for 0% of the time, Pallas kernels for 3%

profile of v8, /device:TPU:24, one launch (start us, length us, event | category | flops | bytes accessed | tf_op | source)
XLA Modules:
  0.0 75.1 jit_solution(16759681623336808873)
XLA Ops:
  0.6 0.0 copy-start.3
  0.6 0.0 copy-start.7
  0.7 0.0 copy-start
  0.7 1.1 %cut.1 = (bf16[64,512]{1,0:T(8,128)(2,1)S(1)}, bf16[64,512]{1,0:T(8,128)(2,1)S(1)}, bf16[64,512]{1,0:T(8,128)(2,1)S(1)}, bf16[64,512]{1,0:T(8,128)(2,1)S(1)}) custom-call(bf16[256,512]{1,0:T(8,128)(2,1)} %hidden.1), custom_call_target="tpu_custom_call" | custom-call | flops 2000000000 | bytes 1000 | tf_op jit(solution)/shard_map/cut/pallas_call | solution.py:312
  1.8 0.0 copy-start.2
  1.8 0.0 copy-start.4
  1.8 0.0 copy-start.8
  1.8 0.0 copy-start.1
  1.8 0.0 copy-start.5
  1.8 0.0 copy-start.6
  1.9 0.0 copy-start.9
  1.9 3.5 %collective-permute-start = (bf16[64,512]{1,0:T(8,128)(2,1)S(1)}, bf16[64,512]{1,0:T(8,128)(2,1)S(1)}, u32[]{:S(2)}, u32[]{:S(2)}) collective-permute-start(bf16[64,512]{1,0:T(8,128)(2,1)S(1)} %get-tuple-element.14), channel_id=1, source_target_pairs={{0,128},{1,129},{2,130},{3,131},{4,132},{5,133},{6,134},{7,135},{8... | collective-permute-start | bytes 196616 | tf_op jit(solution)/shard_map/ppermute | solution.py:322
  5.4 2.2 %collective-permute-start.1 = (bf16[64,512]{1,0:T(8,128)(2,1)S(1)}, bf16[64,512]{1,0:T(8,128)(2,1)S(1)}, u32[]{:S(2)}, u32[]{:S(2)}) collective-permute-start(bf16[64,512]{1,0:T(8,128)(2,1)S(1)} %get-tuple-element.15), channel_id=1, source_target_pairs={{0,256},{1,257},{2,258},{3,259},{4,260},{5,261},{6,262},{7,263},{8... | collective-permute-start | bytes 196616 | tf_op jit(solution)/shard_map/ppermute | solution.py:322
  7.6 1.3 %collective-permute-start.2 = (bf16[64,512]{1,0:T(8,128)(2,1)S(1)}, bf16[64,512]{1,0:T(8,128)(2,1)S(1)}, u32[]{:S(2)}, u32[]{:S(2)}) collective-permute-start(bf16[64,512]{1,0:T(8,128)(2,1)S(1)} %get-tuple-element.16), channel_id=1, source_target_pairs={{0,384},{1,385},{2,386},{3,387},{4,388},{5,389},{6,390},{7,391},{8... | collective-permute-start | bytes 196616 | tf_op jit(solution)/shard_map/ppermute | solution.py:322
  8.9 0.0 copy-done.3
  8.9 0.0 copy-done.7
  8.9 0.2 pack.1.asked
  9.1 0.0 collective-permute-done.first
  9.1 0.4 collective-permute-done.1.second
  9.5 1.3 %collective-permute-done.2.third = bf16[64,512]{1,0:T(8,128)(2,1)S(1)} collective-permute-done((bf16[64,512]{1,0:T(8,128)(2,1)S(1)}, bf16[64,512]{1,0:T(8,128)(2,1)S(1)}, u32[]{:S(2)}, u32[]{:S(2)}) %collective-permute-start.2) | collective-permute-done | bytes 65568 | tf_op jit(solution)/shard_map/ppermute | solution.py:322
  10.8 0.0 copy-done
  10.8 1.2 %project.1 = bf16[16,80,128]{2,1,0:T(8,128)(2,1)} custom-call(bf16[64,512]{1,0:T(8,128)(2,1)S(1)} %get-tuple-element.13.own, bf16[64,512]{1,0:T(8,128)(2,1)S(1)} %collective-permute-done.first, bf16[64,512]{1,0:T(8,128)(2,1)S(1)} %collective-permute-done.1.second, bf16[64,512]{1,0:T(8,128)(2,1)S(1)} %collective-permute-done.2.third, ...), custom_call_target="tpu_custom_call" | custom-call | tf_op jit(solution)/shard_map/project/pallas_call | solution.py:330
  12.0 15.2 %all-to-all-start = ((bf16[16,80,128]{2,1,0:T(8,128)(2,1)}), bf16[16,80,128]{2,1,0:T(8,128)(2,1)S(1)}, u32[]{:S(2)}, u32[]{:S(2)}) async-start(bf16[16,80,128]{2,1,0:T(8,128)(2,1)} %project.1), calls=%async_computation | async-start | bytes 655360 | tf_op jit(solution)/shard_map/all_to_all | solution.py:288
  27.2 0.0 copy-done.2
  27.2 0.0 copy-done.4
  27.2 0.0 copy-done.8
  27.2 1.3 %grammar.1 = (bf16[32,7680]{1,0:T(8,128)(2,1)S(1)}, bf16[16,128]{1,0:T(8,128)(2,1)S(1)}) custom-call(bf16[32,7680]{1,0:T(8,128)(2,1)S(1)} %copy-done.2, s32[1,32]{1,0:T(1,128)S(1)} %bitcast.4, s32[24,256]{1,0:T(8,128)S(1)} %copy-done.4), custom_call_target="tpu_custom_call" | custom-call | tf_op jit(solution)/shard_map/grammar/pallas_call | solution.py:339
  28.5 18.9 %all-to-all-done.received.pieces = bf16[16,80,128]{2,1,0:T(8,128)(2,1)S(1)} async-done(((bf16[16,80,128]{2,1,0:T(8,128)(2,1)}), bf16[16,80,128]{2,1,0:T(8,128)(2,1)S(1)}, u32[]{:S(2)}, u32[]{:S(2)}) %all-to-all-start) | async-done | bytes 327712 | tf_op jit(solution)/shard_map/all_to_all | solution.py:288
  47.4 0.0 copy-done.1
  47.4 0.0 copy-done.5
  47.4 0.0 copy-done.6
  47.5 0.0 copy-done.9
  47.5 1.4 %cached.1 = bf16[16,16,128]{2,1,0:T(8,128)(2,1)} custom-call(s32[1,2]{1,0:T(1,128)S(1)} %bitcast.5, bf16[16,80,128]{2,1,0:T(8,128)(2,1)S(1)} %all-to-all-done.received.pieces, bf16[2,128,2048]{2,1,0:T(8,128)(2,1)S(1)} %copy-done.1, bf16[16,128]{1,0:T(8,128)(2,1)S(1)} %get-tuple-element.17.terms, s32[8,16]{1,0:T(8,128)S(1)} %copy-done.5, s32[8,16]{1,0:T(8,128)S(1)} %copy-done.6), custom_call_target="tpu_custom_call" | custom-call | tf_op jit(solution)/shard_map/cached/pallas_call | solution.py:354
  48.9 5.9 %all-to-all-start.1 = ((bf16[16,16,128]{2,1,0:T(8,128)(2,1)}), bf16[16,16,128]{2,1,0:T(8,128)(2,1)S(1)}, u32[]{:S(2)}, u32[]{:S(2)}) async-start(bf16[16,16,128]{2,1,0:T(8,128)(2,1)} %cached.1), calls=%async_computation.1 | async-start | bytes 131072 | tf_op jit(solution)/shard_map/all_to_all | solution.py:288
  54.8 3.8 %collective-permute-start.3 = (bf16[64,128]{1,0:T(8,128)(2,1)S(1)}, bf16[64,128]{1,0:T(8,128)(2,1)S(1)}, u32[]{:S(2)}, u32[]{:S(2)}) collective-permute-start(bf16[64,128]{1,0:T(8,128)(2,1)S(1)} %reduce.1), channel_id=1, source_target_pairs={{0,1},{1,0},{2,3},{3,2},{4,5},{5,4},{6,7},{7,6},{8,9},{9,8},{10,11... | collective-permute-start | bytes 49160 | tf_op jit(solution)/shard_map/ppermute | solution.py:353
  58.6 2.0 %collective-permute-done.3 = bf16[64,128]{1,0:T(8,128)(2,1)S(1)} collective-permute-done((bf16[64,128]{1,0:T(8,128)(2,1)S(1)}, bf16[64,128]{1,0:T(8,128)(2,1)S(1)}, u32[]{:S(2)}, u32[]{:S(2)}) %collective-permute-start.3) | collective-permute-done | bytes 16416 | tf_op jit(solution)/shard_map/ppermute | solution.py:353
  60.6 12.1 %all-gather = bf16[512,128]{1,0:T(8,128)(2,1)S(1)} all-gather(bf16[128,128]{1,0:T(8,128)(2,1)S(1)} %pad_maximum_fusion), channel_id=2, replica_groups=mesh['x'=4,'c8'=8,'zh'=8,'zl'=2] {'x'}, dimensions={0}, use_global_device_ids=true | all-gather | bytes 163840 | tf_op jit(solution)/shard_map/all_gather | solution.py:362
  72.7 0.4 prompts.1
  73.1 0.0 all-to-all-done.1.received
  73.1 2.0 %finish.1 = (f32[32,7680]{1,0:T(8,128)}, bf16[32,512]{1,0:T(8,128)(2,1)}) custom-call(bf16[32,7680]{1,0:T(8,128)(2,1)S(1)} %get-tuple-element.12.masked, bf16[16,16,128]{2,1,0:T(8,128)(2,1)S(1)} %all-to-all-done.1.received, bf16[32,512]{1,0:T(8,128)(2,1)S(1)} %copy-done.3, f32[128,128]{1,0:T(8,128)S(1)} %get-tuple-element.18.result, ...), custom_call_target="tpu_custom_call" | custom-call | tf_op jit(solution)/shard_map/finish/pallas_call | solution.py:370
  (2 shorter events, 0.0 us)
Async XLA Ops:
  0.6 8.3 %copy-start.3 = (bf16[32,512]{1,0:T(8,128)(2,1)S(1)}, bf16[32,512]{1,0:T(8,128)(2,1)}, u32[]{:S(2)}) copy-start(bf16[32,512]{1,0:T(8,128)(2,1)} %queries.5) | copy-start | bytes 98308
  0.6 8.3 %copy-start.7 = (bf16[32,128]{1,0:T(8,128)(2,1)S(1)}, bf16[32,128]{1,0:T(8,128)(2,1)}, u32[]{:S(2)}) copy-start(bf16[32,128]{1,0:T(8,128)(2,1)} %fresh.1) | copy-start | bytes 24580
  0.7 10.2 %copy-start = (bf16[512,2048]{1,0:T(8,128)(2,1)S(1)}, bf16[512,2048]{1,0:T(8,128)(2,1)}, u32[]{:S(2)}) copy-start(bf16[512,2048]{1,0:T(8,128)(2,1)} %weight.1) | copy-start | bytes 6291460
  1.8 25.4 %copy-start.2 = (bf16[32,7680]{1,0:T(8,128)(2,1)S(1)}, bf16[32,7680]{1,0:T(8,128)(2,1)}, u32[]{:S(2)}) copy-start(bf16[32,7680]{1,0:T(8,128)(2,1)} %logits.1) | copy-start | bytes 1474564
  1.8 25.4 %copy-start.4 = (s32[24,256]{1,0:T(8,128)S(1)}, s32[24,256]{1,0:T(8,128)}, u32[]{:S(2)}) copy-start(s32[24,256]{1,0:T(8,128)} %masks.1) | copy-start | bytes 73732
  1.8 25.4 %copy-start.8 = (s32[32]{0:T(128)S(1)}, s32[32]{0:T(128)}, u32[]{:S(2)}) copy-start(s32[32]{0:T(128)} %param.20) | copy-start | bytes 388
  1.8 45.6 %copy-start.1 = (bf16[2,128,2048]{2,1,0:T(8,128)(2,1)S(1)}, bf16[2,128,2048]{2,1,0:T(8,128)(2,1)}, u32[]{:S(2)}) copy-start(bf16[2,128,2048]{2,1,0:T(8,128)(2,1)} %cache.1) | copy-start | bytes 3145732
  1.8 45.6 %copy-start.5 = (s32[8,16]{1,0:T(8,128)S(1)}, s32[8,16]{1,0:T(8,128)}, u32[]{:S(2)}) copy-start(s32[8,16]{1,0:T(8,128)} %lengths.3) | copy-start | bytes 1540
  1.8 45.6 %copy-start.6 = (s32[8,16]{1,0:T(8,128)S(1)}, s32[8,16]{1,0:T(8,128)}, u32[]{:S(2)}) copy-start(s32[8,16]{1,0:T(8,128)} %owners.3) | copy-start | bytes 1540
  1.9 45.6 %copy-start.9 = (s32[2]{0:T(128)S(1)}, s32[2]{0:T(128)}, u32[]{:S(2)}) copy-start(s32[2]{0:T(128)} %param.16) | copy-start | bytes 28
  1.9 7.3 %collective-permute-start = (bf16[64,512]{1,0:T(8,128)(2,1)S(1)}, bf16[64,512]{1,0:T(8,128)(2,1)S(1)}, u32[]{:S(2)}, u32[]{:S(2)}) collective-permute-start(bf16[64,512]{1,0:T(8,128)(2,1)S(1)} %get-tuple-element.14), channel_id=1, source_target_pairs={{0,128},{1,129},{2,130},{3,131},{4,132},{5,133},{6,134},{7,135},{8... | collective-permute-start | bytes 196616 | tf_op jit(solution)/shard_map/ppermute | solution.py:322
  5.4 4.1 %collective-permute-start.1 = (bf16[64,512]{1,0:T(8,128)(2,1)S(1)}, bf16[64,512]{1,0:T(8,128)(2,1)S(1)}, u32[]{:S(2)}, u32[]{:S(2)}) collective-permute-start(bf16[64,512]{1,0:T(8,128)(2,1)S(1)} %get-tuple-element.15), channel_id=1, source_target_pairs={{0,256},{1,257},{2,258},{3,259},{4,260},{5,261},{6,262},{7,263},{8... | collective-permute-start | bytes 196616 | tf_op jit(solution)/shard_map/ppermute | solution.py:322
  7.6 3.2 %collective-permute-start.2 = (bf16[64,512]{1,0:T(8,128)(2,1)S(1)}, bf16[64,512]{1,0:T(8,128)(2,1)S(1)}, u32[]{:S(2)}, u32[]{:S(2)}) collective-permute-start(bf16[64,512]{1,0:T(8,128)(2,1)S(1)} %get-tuple-element.16), channel_id=1, source_target_pairs={{0,384},{1,385},{2,386},{3,387},{4,388},{5,389},{6,390},{7,391},{8... | collective-permute-start | bytes 196616 | tf_op jit(solution)/shard_map/ppermute | solution.py:322
  12.0 35.5 %all-to-all-start = ((bf16[16,80,128]{2,1,0:T(8,128)(2,1)}), bf16[16,80,128]{2,1,0:T(8,128)(2,1)S(1)}, u32[]{:S(2)}, u32[]{:S(2)}) async-start(bf16[16,80,128]{2,1,0:T(8,128)(2,1)} %project.1), calls=%async_computation | async-start | bytes 655360 | tf_op jit(solution)/shard_map/all_to_all | solution.py:288
  48.9 24.3 %all-to-all-start.1 = ((bf16[16,16,128]{2,1,0:T(8,128)(2,1)}), bf16[16,16,128]{2,1,0:T(8,128)(2,1)S(1)}, u32[]{:S(2)}, u32[]{:S(2)}) async-start(bf16[16,16,128]{2,1,0:T(8,128)(2,1)} %cached.1), calls=%async_computation.1 | async-start | bytes 131072 | tf_op jit(solution)/shard_map/all_to_all | solution.py:288
  54.8 5.9 %collective-permute-start.3 = (bf16[64,128]{1,0:T(8,128)(2,1)S(1)}, bf16[64,128]{1,0:T(8,128)(2,1)S(1)}, u32[]{:S(2)}, u32[]{:S(2)}) collective-permute-start(bf16[64,128]{1,0:T(8,128)(2,1)S(1)} %reduce.1), channel_id=1, source_target_pairs={{0,1},{1,0},{2,3},{3,2},{4,5},{5,4},{6,7},{7,6},{8,9},{9,8},{10,11... | collective-permute-start | bytes 49160 | tf_op jit(solution)/shard_map/ppermute | solution.py:353

commit v9 on v8

--- a/solution.py
+++ b/solution.py
@@ -71,24 +71,17 @@
         copy.wait()
 
 
-def pack(queries, fresh, out):
-    table = jnp.concatenate(
-        [queries[:, HD * i : HD * (i + 1)] for i in range(4)] + [fresh[...]], axis=0
-    )
-    row = iota((256, 1), 0)
-    dest, k = row // 16, row % 16
-    target = jnp.where(
-        k < 8,
-        (k % 4) * 32 + 2 * dest + k // 4,
-        jnp.where(k < 10, 128 + 2 * dest + k - 8, 160),
-    )
-    out[...] = pick(target, table).astype(BF16).reshape(16, 16, HD)
+def pack(queries, out):
+    table = jnp.concatenate([queries[:, HD * i : HD * (i + 1)] for i in range(4)], axis=0)
+    row = iota((128, 1), 0)
+    dest, k = row // 8, row % 8
+    out[...] = pick((k % 4) * 32 + 2 * dest + k // 4, table).astype(BF16).reshape(16, 8, HD)
 
 
 def project(own, first, second, third, asked, weight, out, slots, sems):
     turn = lax.axis_index("x")
     tokens = jnp.where(turn == 0, own[...], first[...] + second[...] + third[...])
-    slots[:, 64:80] = asked[...]
+    slots[:, 64:72] = asked[...]
     copies = []
     for h in range(4):
         for part in range(2):
@@ -154,9 +147,7 @@
         top = jnp.max(section, axis=1, keepdims=True)
         peak = top if peak is None else jnp.maximum(peak, top)
     total = sum(jnp.sum(jnp.exp(section - peak), axis=1, keepdims=True) for section in kept)
-    high = total.astype(BF16).astype(F32)
-    middle = (total - high).astype(BF16).astype(F32)
-    low = total - high - middle
+    high, middle, low = thirds(total)
     row, lane = iota((32, HD), 0), iota((32, HD), 1)
     spot = lane - row
     line = jnp.where(
@@ -166,59 +157,52 @@
     terms[...] = jnp.broadcast_to(jnp.sum(line, axis=0, keepdims=True), (16, HD)).astype(BF16)
 
 
-def softmax(score, own, alive):
-    highest = jnp.maximum(
-        jnp.max(jnp.where(alive, score, -jnp.inf), axis=1, keepdims=True), own
-    )
-    exponent = jnp.where(alive, jnp.exp(score - highest), 0.0)
-    own_exponent = jnp.exp(own - highest)
-    total = jnp.sum(exponent, axis=1, keepdims=True) + own_exponent
-    own_weight = (own_exponent / total).astype(BF16).astype(F32)
-    return (exponent / total).astype(BF16), own_weight
-
-
 def transposed(a, b):
     return lax.dot_general(a, b, (((1,), (1,)), ((), ())), preferred_element_type=F32)
 
 
-def attend_cached(cache_len, received, cache, terms, lengths, owners, out):
-    column = lax.axis_index("zh") * 2 + lax.axis_index("zl")
-    prompts = prompts_of(
-        lengths[...], owners[...], lax.axis_index("c8"), lax.axis_index("x")
-    )
-    landed = landing(jnp.full((1, 1), column, I32), prompts)[0]
-    table = received[:, 64:80, :].reshape(256, HD)
-    row = iota((256, 1), 0)
-    device, k = row // 16, row % 16
-    second = (k >= 4) & (k < 8)
-    fresh_row = (device // 2) * 16 + jnp.where(second, 9, 8)
-    own_key = pick(fresh_row, table)
-    own_value = pick(fresh_row + KVH * 16, table)
-    own = jnp.sum(table.astype(F32) * own_key, axis=1, keepdims=True) * SCALE
-    second32 = second[0:32]
+def thirds(value):
+    high = value.astype(BF16).astype(F32)
+    middle = (value - high).astype(BF16).astype(F32)
+    return high, middle, value - high - middle
+
+
+def attend_cached(cache_len, received, cache, terms, out):
+    table = received[:, 64:72, :].reshape(128, HD)
+    k = iota((128, 1), 0) % 8
+    second = k >= 4
+    second16 = second[0:16]
     scores = []
     for h in range(KVH):
-        rows = table[32 * h : 32 * (h + 1)]
+        rows = table[16 * h : 16 * (h + 1)]
         both = [transposed(rows, cache[r, :, HD * h : HD * (h + 1)]) for r in range(2)]
-        scores.append(jnp.where(second32, both[1], both[0]))
+        scores.append(jnp.where(second16, both[1], both[0]))
     score = jnp.concatenate(scores, axis=0) * SCALE
-    alive = iota((256, HD), 1) < jnp.where(second, cache_len[0:1, 1:2], cache_len[0:1, 0:1])
-    weight, own_weight = softmax(score, own, alive)
+    count = jnp.where(second, cache_len[0:1, 1:2], cache_len[0:1, 0:1])
+    alive = iota((128, HD), 1) < count
+    highest = jnp.max(jnp.where(alive, score, LOWEST), axis=1, keepdims=True)
+    exponent = jnp.where(alive, jnp.exp(score - highest), 0.0)
+    total = jnp.sum(exponent, axis=1, keepdims=True)
+    weight = (exponent / total).astype(BF16)
     values = []
     for h in range(KVH):
-        rows = weight[32 * h : 32 * (h + 1)]
+        rows = weight[16 * h : 16 * (h + 1)]
         at = HD * (KVH + h)
         both = [
             jnp.dot(rows, cache[r, :, at : at + HD], preferred_element_type=F32)
             for r in range(2)
         ]
-        values.append(jnp.where(second32, both[1], both[0]))
-    result = jnp.concatenate(values, axis=0) + own_weight * own_value
-    arrived = jnp.broadcast_to(landed > 0.5, (256, 1))
-    result = jnp.where(arrived & (k == 0), own_key, result)
-    result = jnp.where(arrived & (k == 1), own_value, result)
-    result = jnp.where(k == 8, terms[0:1, :].astype(F32), result)
-    out[...] = result.astype(BF16).reshape(16, 16, HD)
+        values.append(jnp.where(second16, both[1], both[0]))
+    high, middle, low = thirds(highest + jnp.log(total))
+    spot = iota((128, HD), 1) - k
+    line = jnp.where(
+        spot == 0, high, jnp.where(spot == 8, middle, jnp.where(spot == 16, low, 0.0))
+    )
+    line = jnp.sum(line.reshape(16, 8, HD), axis=1, keepdims=True)
+    slot = iota((16, 8, HD), 1)
+    rest = jnp.where(slot == 0, terms[0:1, :].astype(F32).reshape(1, 1, HD), line)
+    result = jnp.concatenate(values, axis=0).reshape(16, 8, HD)
+    out[...] = jnp.concatenate([result, rest], axis=1).astype(BF16)
 
 
 def attend_prompts(parts, queries, lengths, owners, result, stats):
@@ -244,7 +228,7 @@
     stats[...] = jnp.where(lane == 0, highest, jnp.where(lane == 1, total, landed))
 
 
-def finish(masked, received, queries, result, stats, logprob, attended, values, sems):
+def finish(masked, received, queries, first, second, result, stats, logprob, attended, values, sems):
     lines = received[:, 8, :].astype(F32)
     take = lambda k: lines[:, 32 * k : 32 * (k + 1)]
     peak, total = take(0), take(1) + take(2) + take(3)
@@ -257,17 +241,26 @@
     head, request = row // 32, row % 32
     query = jnp.concatenate([queries[:, HD * i : HD * (i + 1)] for i in range(4)], axis=0)
     table = received[...].reshape(256, HD)
+    place = (request % 2) * 4 + head
     slot = (request // 2) * 16
-    target = jnp.concatenate([slot, slot + 1, slot + (request % 2) * 4 + head], axis=0)
-    picked = pick(target, table)
-    own_key, own_value, cached = picked[0:128], picked[128:256], picked[256:384]
+    picked = pick(jnp.concatenate([slot + place, slot + 9], axis=0), table)
+    spot = iota((128, HD), 1) - place
+    cached_top = jnp.where((spot == 0) | (spot == 8) | (spot == 16), picked[128:256], 0.0)
+    cached_top = jnp.sum(cached_top, axis=1, keepdims=True)
+    even = lax.axis_index("zl") == 0
+    own_key = jnp.where(even, first[...], second[...]).astype(F32)
+    own_value = jnp.where(even, second[...], first[...]).astype(F32)
+    own_key = jnp.concatenate([own_key] * 4, axis=0)
+    own_value = jnp.concatenate([own_value] * 4, axis=0)
     own = jnp.sum(query.astype(F32) * own_key, axis=1, keepdims=True) * SCALE
-    top, total, landed = stats[:, 0:1], stats[:, 1:2], stats[:, 2:3]
+    landed = stats[:, 2:3] > 0.5
+    top = jnp.where(landed, stats[:, 0:1], cached_top)
+    total = jnp.where(landed, stats[:, 1:2], 1.0)
+    live = jnp.where(landed, result[...], picked[0:128])
     highest = jnp.maximum(top, own)
     share, own_share = jnp.exp(top - highest), jnp.exp(own - highest)
     scale = 1.0 / (total * share + own_share)
-    merged = (result[...] * share + own_value * own_share) * scale
-    merged = jnp.where(landed > 0.5, merged, cached).astype(BF16)
+    merged = ((live * share + own_value * own_share) * scale).astype(BF16)
     copies = []
     for b in range(4):
         at = slice(BLK * b, BLK * (b + 1))
@@ -322,20 +315,23 @@
         shares[k] = lax.ppermute(shares[k], "x", [(0, k)])
     asked = kernel(
         pack,
-        out_shape=kept((16, 16, HD), BF16),
-        in_specs=[vmem] * 2,
+        out_shape=kept((16, 8, HD), BF16),
+        in_specs=[vmem],
         out_specs=vmem,
         name="pack",
-    )(*held(queries, fresh))
+    )(*held(queries))
     projected = kernel(
         project,
-        out_shape=pltpu.HBM((16, 80, HD), BF16),
+        out_shape=pltpu.HBM((16, 72, HD), BF16),
         in_specs=[vmem] * 6,
         out_specs=hbm,
-        scratch_shapes=[pltpu.VMEM((16, 80, HD), BF16), pltpu.SemaphoreType.DMA((4,))],
+        scratch_shapes=[pltpu.VMEM((16, 72, HD), BF16), pltpu.SemaphoreType.DMA((4,))],
         name="project",
     )(*held(*shares, asked, w_kv))
     pieces = exchanged(projected, TP)
+    keys_first = [(b, 2 * b) if b < KVH else (b, 2 * (b - KVH) + 1) for b in range(16)]
+    values_first = [(b, d + 1 - 2 * (d % 2)) for b, d in keys_first]
+    renewed = [lax.ppermute(fresh, TP, route) for route in (keys_first, values_first)]
     masked, terms = kernel(
         grammar,
         out_shape=[kept(logits.shape, BF16), kept((16, HD), BF16)],
@@ -354,9 +350,9 @@
     answers = kernel(
         attend_cached,
         out_shape=sent((16, 16, HD), BF16),
-        in_specs=[vmem] * 6,
+        in_specs=[vmem] * 4,
         name="cached",
-    )(*held(cache_len.reshape(1, 2), pieces, cache, terms, prompt_lengths, owner_step))
+    )(*held(cache_len.reshape(1, 2), pieces, cache, terms))
     answers = exchanged(answers, TP)
     both = jnp.concatenate([block, other], axis=0)
     around = lax.all_gather(both, "x")
@@ -370,11 +366,11 @@
     logprob, attended = kernel(
         finish,
         out_shape=[pltpu.HBM(logits.shape, F32), sent(queries.shape, BF16)],
-        in_specs=[vmem] * 5,
+        in_specs=[vmem] * 7,
         out_specs=[hbm, vmem],
         scratch_shapes=[pltpu.VMEM(logits.shape, F32), pltpu.SemaphoreType.DMA((4,))],
         name="finish",
-    )(*held(masked, answers, queries, result, stats))
+    )(*held(masked, answers, queries, *renewed, result, stats))
     return attended, logprob
 
 

time: 76 us -> 84.6 us (1.11)
  the two profiles are of different devices: /device:TPU:24 before, /device:TPU:90 now
where the time goes in v9:
time: 84.6 us; the launch traced here: 84.2 us
  starting transfers between devices  39.5 us (47%)
  waiting for transfers between devices  20.7 us (24%)
  blocking collectives  15.5 us (18%)
  Pallas kernels  7.53 us (9%)
  between operations  0.87 us (1%)
    all_to_all x2, starting transfers between devices, exchanged(): return lax.all_to_all(slots, axis, 0, 0, tiled=True)  20.6 us
    all_to_all x2, waiting for transfers between devices, exchanged(): return lax.all_to_all(slots, axis, 0, 0, tiled=True)  17.4 us
    all_gather x1, blocking collectives, per_device(): around = lax.all_gather(both, 'x')  15.5 us
    ppermute x2, starting transfers between devices, per_device(): lax.ppermute(fresh, TP, route)  12.8 us
    ppermute x1, starting transfers between devices, per_device(): other = lax.ppermute(block, 'zl', [(0, 1), (1, 0)])  3.37 us
    ppermute x3, waiting for transfers between devices, per_device(): shares[k] = lax.ppermute(shares[k], 'x', [(0, k)])  3.36 us
    ppermute x3, starting transfers between devices, per_device(): shares[k] = lax.ppermute(shares[k], 'x', [(0, k)])  2.75 us
    pallas_call x1, Pallas kernels, per_device(): kernel(finish, out_shape=[pltpu.HBM(logits.shape, F32), sent(queries.shap...  2.03 us
  transfers between devices with their start and end apart: 8, of which 2 were waited for; matrix products, arithmetic and copies ran while one was open for 0% of the time, Pallas kernels for 2%

profile of v9, /device:TPU:90, one launch (start us, length us, event | category | flops | bytes accessed | tf_op | source)
XLA Modules:
  0.0 84.2 jit_solution(749848545329945595)
XLA Ops:
  0.6 0.0 copy-start.3
  0.6 0.0 copy-start
  0.6 1.1 %cut.1 = (bf16[64,512]{1,0:T(8,128)(2,1)S(1)}, bf16[64,512]{1,0:T(8,128)(2,1)S(1)}, bf16[64,512]{1,0:T(8,128)(2,1)S(1)}, bf16[64,512]{1,0:T(8,128)(2,1)S(1)}) custom-call(bf16[256,512]{1,0:T(8,128)(2,1)} %hidden.1), custom_call_target="tpu_custom_call" | custom-call | flops 2000000000 | bytes 1000 | tf_op jit(solution)/shard_map/cut/pallas_call | solution.py:305
  1.8 0.0 copy-start.2
  1.8 0.0 copy-start.4
  1.8 0.0 copy-start.8
  1.8 0.0 copy-start.1
  1.8 0.0 copy-start.7
  1.8 1.4 %collective-permute-start = (bf16[64,512]{1,0:T(8,128)(2,1)S(1)}, bf16[64,512]{1,0:T(8,128)(2,1)S(1)}, u32[]{:S(2)}, u32[]{:S(2)}) collective-permute-start(bf16[64,512]{1,0:T(8,128)(2,1)S(1)} %get-tuple-element.14), channel_id=1, source_target_pairs={{0,128},{1,129},{2,130},{3,131},{4,132},{5,133},{6,134},{7,135},{8... | collective-permute-start | bytes 196616 | tf_op jit(solution)/shard_map/ppermute | solution.py:315
  3.3 0.7 collective-permute-start.1
  3.9 0.7 collective-permute-start.2
  4.6 0.0 copy-done.3
  4.6 0.2 pack.1.asked
  4.8 3.4 %collective-permute-done.first = bf16[64,512]{1,0:T(8,128)(2,1)S(1)} collective-permute-done((bf16[64,512]{1,0:T(8,128)(2,1)S(1)}, bf16[64,512]{1,0:T(8,128)(2,1)S(1)}, u32[]{:S(2)}, u32[]{:S(2)}) %collective-permute-start) | collective-permute-done | bytes 65568 | tf_op jit(solution)/shard_map/ppermute | solution.py:315
  8.1 0.0 collective-permute-done.1.second
  8.1 0.0 collective-permute-done.2.third
  8.1 0.0 copy-done
  8.1 1.2 %project.1 = bf16[16,72,128]{2,1,0:T(8,128)(2,1)} custom-call(bf16[64,512]{1,0:T(8,128)(2,1)S(1)} %get-tuple-element.13.own, bf16[64,512]{1,0:T(8,128)(2,1)S(1)} %collective-permute-done.first, bf16[64,512]{1,0:T(8,128)(2,1)S(1)} %collective-permute-done.1.second, bf16[64,512]{1,0:T(8,128)(2,1)S(1)} %collective-permute-done.2.third, ...), custom_call_target="tpu_custom_call" | custom-call | tf_op jit(solution)/shard_map/project/pallas_call | solution.py:323
  9.3 0.0 copy-start.9
  9.3 0.0 copy-start.5
  9.3 0.0 copy-start.6
  9.3 14.9 %all-to-all-start = ((bf16[16,72,128]{2,1,0:T(8,128)(2,1)}), bf16[16,72,128]{2,1,0:T(8,128)(2,1)S(1)}, u32[]{:S(2)}, u32[]{:S(2)}) async-start(bf16[16,72,128]{2,1,0:T(8,128)(2,1)} %project.1), calls=%async_computation | async-start | bytes 589824 | tf_op jit(solution)/shard_map/all_to_all | solution.py:281
  24.2 0.0 copy-done.2
  24.3 0.0 copy-done.4
  24.3 0.0 copy-done.8
  24.3 1.3 %grammar.1 = (bf16[32,7680]{1,0:T(8,128)(2,1)S(1)}, bf16[16,128]{1,0:T(8,128)(2,1)S(1)}) custom-call(bf16[32,7680]{1,0:T(8,128)(2,1)S(1)} %copy-done.2, s32[1,32]{1,0:T(1,128)S(1)} %bitcast.5, s32[24,256]{1,0:T(8,128)S(1)} %copy-done.4), custom_call_target="tpu_custom_call" | custom-call | tf_op jit(solution)/shard_map/grammar/pallas_call | solution.py:335
  25.6 17.3 %all-to-all-done.received.pieces = bf16[16,72,128]{2,1,0:T(8,128)(2,1)S(1)} async-done(((bf16[16,72,128]{2,1,0:T(8,128)(2,1)}), bf16[16,72,128]{2,1,0:T(8,128)(2,1)S(1)}, u32[]{:S(2)}, u32[]{:S(2)}) %all-to-all-start) | async-done | bytes 294944 | tf_op jit(solution)/shard_map/all_to_all | solution.py:281
  42.9 0.0 copy-done.1
  42.9 0.0 copy-done.7
  42.9 1.3 %cached.1 = bf16[16,16,128]{2,1,0:T(8,128)(2,1)} custom-call(s32[1,2]{1,0:T(1,128)S(1)} %bitcast.4, bf16[16,72,128]{2,1,0:T(8,128)(2,1)S(1)} %all-to-all-done.received.pieces, bf16[2,128,2048]{2,1,0:T(8,128)(2,1)S(1)} %copy-done.1, bf16[16,128]{1,0:T(8,128)(2,1)S(1)} %get-tuple-element.17.terms), custom_call_target="tpu_custom_call" | custom-call | tf_op jit(solution)/shard_map/cached/pallas_call | solution.py:350
  44.2 5.7 %all-to-all-start.1 = ((bf16[16,16,128]{2,1,0:T(8,128)(2,1)}), bf16[16,16,128]{2,1,0:T(8,128)(2,1)S(1)}, u32[]{:S(2)}, u32[]{:S(2)}) async-start(bf16[16,16,128]{2,1,0:T(8,128)(2,1)} %cached.1), calls=%async_computation.1 | async-start | bytes 131072 | tf_op jit(solution)/shard_map/all_to_all | solution.py:281
  50.0 3.4 %collective-permute-start.5 = (bf16[64,128]{1,0:T(8,128)(2,1)S(1)}, bf16[64,128]{1,0:T(8,128)(2,1)S(1)}, u32[]{:S(2)}, u32[]{:S(2)}) collective-permute-start(bf16[64,128]{1,0:T(8,128)(2,1)S(1)} %reduce.1), channel_id=1, source_target_pairs={{0,1},{1,0},{2,3},{3,2},{4,5},{5,4},{6,7},{7,6},{8,9},{9,8},{10,11... | collective-permute-start | bytes 49160 | tf_op jit(solution)/shard_map/ppermute | solution.py:349
  53.4 0.0 copy-done.9
  53.4 5.5 %collective-permute-start.4 = (bf16[32,128]{1,0:T(8,128)(2,1)S(1)}, bf16[32,128]{1,0:T(8,128)(2,1)S(1)}, u32[]{:S(2)}, u32[]{:S(2)}) collective-permute-start(bf16[32,128]{1,0:T(8,128)(2,1)S(1)} %copy-done.9), channel_id=1, source_target_pairs={{0,1},{1,3},{2,5},{3,7},{4,9},{5,11},{6,13},{7,15},{8,0},{9,2},{10... | collective-permute-start | bytes 24584 | tf_op jit(solution)/shard_map/ppermute | solution.py:334
  58.9 7.3 %collective-permute-start.3 = (bf16[32,128]{1,0:T(8,128)(2,1)S(1)}, bf16[32,128]{1,0:T(8,128)(2,1)S(1)}, u32[]{:S(2)}, u32[]{:S(2)}) collective-permute-start(bf16[32,128]{1,0:T(8,128)(2,1)S(1)} %copy-done.9), channel_id=1, source_target_pairs={{0,0},{1,2},{2,4},{3,6},{4,8},{5,10},{6,12},{7,14},{8,1},{9,3},{10... | collective-permute-start | bytes 24584 | tf_op jit(solution)/shard_map/ppermute | solution.py:334
  66.2 0.0 collective-permute-done.5
  66.2 15.5 %all-gather = bf16[512,128]{1,0:T(8,128)(2,1)S(1)} all-gather(bf16[128,128]{1,0:T(8,128)(2,1)S(1)} %pad_maximum_fusion), channel_id=2, replica_groups=mesh['x'=4,'c8'=8,'zh'=8,'zl'=2] {'x'}, dimensions={0}, use_global_device_ids=true | all-gather | bytes 163840 | tf_op jit(solution)/shard_map/all_gather | solution.py:358
  81.7 0.0 copy-done.5
  81.7 0.0 copy-done.6
  81.7 0.4 prompts.1
  82.1 0.0 collective-permute-done.4.second
  82.1 0.0 collective-permute-done.3.first
  82.1 0.0 all-to-all-done.1.received
  82.2 2.0 %finish.1 = (f32[32,7680]{1,0:T(8,128)}, bf16[32,512]{1,0:T(8,128)(2,1)}) custom-call(bf16[32,7680]{1,0:T(8,128)(2,1)S(1)} %get-tuple-element.12.masked, bf16[16,16,128]{2,1,0:T(8,128)(2,1)S(1)} %all-to-all-done.1.received, bf16[32,512]{1,0:T(8,128)(2,1)S(1)} %copy-done.3, bf16[32,128]{1,0:T(8,128)(2,1)S(1)} %collective-permute-done.3.first, ...), custom_call_target="tpu_custom_call" | custom-call | tf_op jit(solution)/shard_map/finish/pallas_call | solution.py:366
  (2 shorter events, 0.0 us)
Async XLA Ops:
  0.6 4.0 %copy-start.3 = (bf16[32,512]{1,0:T(8,128)(2,1)S(1)}, bf16[32,512]{1,0:T(8,128)(2,1)}, u32[]{:S(2)}) copy-start(bf16[32,512]{1,0:T(8,128)(2,1)} %queries.5) | copy-start | bytes 98308
  0.6 7.5 %copy-start = (bf16[512,2048]{1,0:T(8,128)(2,1)S(1)}, bf16[512,2048]{1,0:T(8,128)(2,1)}, u32[]{:S(2)}) copy-start(bf16[512,2048]{1,0:T(8,128)(2,1)} %weight.1) | copy-start | bytes 6291460
  1.8 22.5 %copy-start.2 = (bf16[32,7680]{1,0:T(8,128)(2,1)S(1)}, bf16[32,7680]{1,0:T(8,128)(2,1)}, u32[]{:S(2)}) copy-start(bf16[32,7680]{1,0:T(8,128)(2,1)} %logits.1) | copy-start | bytes 1474564
  1.8 22.5 %copy-start.4 = (s32[24,256]{1,0:T(8,128)S(1)}, s32[24,256]{1,0:T(8,128)}, u32[]{:S(2)}) copy-start(s32[24,256]{1,0:T(8,128)} %masks.1) | copy-start | bytes 73732
  1.8 22.5 %copy-start.8 = (s32[32]{0:T(128)S(1)}, s32[32]{0:T(128)}, u32[]{:S(2)}) copy-start(s32[32]{0:T(128)} %param.20) | copy-start | bytes 388
  1.8 41.1 %copy-start.1 = (bf16[2,128,2048]{2,1,0:T(8,128)(2,1)S(1)}, bf16[2,128,2048]{2,1,0:T(8,128)(2,1)}, u32[]{:S(2)}) copy-start(bf16[2,128,2048]{2,1,0:T(8,128)(2,1)} %cache.1) | copy-start | bytes 3145732
  1.8 41.1 %copy-start.7 = (s32[2]{0:T(128)S(1)}, s32[2]{0:T(128)}, u32[]{:S(2)}) copy-start(s32[2]{0:T(128)} %param.16) | copy-start | bytes 28
  1.8 6.3 %collective-permute-start = (bf16[64,512]{1,0:T(8,128)(2,1)S(1)}, bf16[64,512]{1,0:T(8,128)(2,1)S(1)}, u32[]{:S(2)}, u32[]{:S(2)}) collective-permute-start(bf16[64,512]{1,0:T(8,128)(2,1)S(1)} %get-tuple-element.14), channel_id=1, source_target_pairs={{0,128},{1,129},{2,130},{3,131},{4,132},{5,133},{6,134},{7,135},{8... | collective-permute-start | bytes 196616 | tf_op jit(solution)/shard_map/ppermute | solution.py:315
  3.3 4.9 %collective-permute-start.1 = (bf16[64,512]{1,0:T(8,128)(2,1)S(1)}, bf16[64,512]{1,0:T(8,128)(2,1)S(1)}, u32[]{:S(2)}, u32[]{:S(2)}) collective-permute-start(bf16[64,512]{1,0:T(8,128)(2,1)S(1)} %get-tuple-element.15), channel_id=1, source_target_pairs={{0,256},{1,257},{2,258},{3,259},{4,260},{5,261},{6,262},{7,263},{8... | collective-permute-start | bytes 196616 | tf_op jit(solution)/shard_map/ppermute | solution.py:315
  3.9 4.2 %collective-permute-start.2 = (bf16[64,512]{1,0:T(8,128)(2,1)S(1)}, bf16[64,512]{1,0:T(8,128)(2,1)S(1)}, u32[]{:S(2)}, u32[]{:S(2)}) collective-permute-start(bf16[64,512]{1,0:T(8,128)(2,1)S(1)} %get-tuple-element.16), channel_id=1, source_target_pairs={{0,384},{1,385},{2,386},{3,387},{4,388},{5,389},{6,390},{7,391},{8... | collective-permute-start | bytes 196616 | tf_op jit(solution)/shard_map/ppermute | solution.py:315
  9.3 44.1 %copy-start.9 = (bf16[32,128]{1,0:T(8,128)(2,1)S(1)}, bf16[32,128]{1,0:T(8,128)(2,1)}, u32[]{:S(2)}) copy-start(bf16[32,128]{1,0:T(8,128)(2,1)} %param.18) | copy-start | bytes 24580
  9.3 72.4 %copy-start.5 = (s32[8,16]{1,0:T(8,128)S(1)}, s32[8,16]{1,0:T(8,128)}, u32[]{:S(2)}) copy-start(s32[8,16]{1,0:T(8,128)} %lengths.1) | copy-start | bytes 1540
  9.3 72.4 %copy-start.6 = (s32[8,16]{1,0:T(8,128)S(1)}, s32[8,16]{1,0:T(8,128)}, u32[]{:S(2)}) copy-start(s32[8,16]{1,0:T(8,128)} %owners.1) | copy-start | bytes 1540
  9.3 33.6 %all-to-all-start = ((bf16[16,72,128]{2,1,0:T(8,128)(2,1)}), bf16[16,72,128]{2,1,0:T(8,128)(2,1)S(1)}, u32[]{:S(2)}, u32[]{:S(2)}) async-start(bf16[16,72,128]{2,1,0:T(8,128)(2,1)} %project.1), calls=%async_computation | async-start | bytes 589824 | tf_op jit(solution)/shard_map/all_to_all | solution.py:281
  44.2 37.9 %all-to-all-start.1 = ((bf16[16,16,128]{2,1,0:T(8,128)(2,1)}), bf16[16,16,128]{2,1,0:T(8,128)(2,1)S(1)}, u32[]{:S(2)}, u32[]{:S(2)}) async-start(bf16[16,16,128]{2,1,0:T(8,128)(2,1)} %cached.1), calls=%async_computation.1 | async-start | bytes 131072 | tf_op jit(solution)/shard_map/all_to_all | solution.py:281
  50.0 16.2 %collective-permute-start.5 = (bf16[64,128]{1,0:T(8,128)(2,1)S(1)}, bf16[64,128]{1,0:T(8,128)(2,1)S(1)}, u32[]{:S(2)}, u32[]{:S(2)}) collective-permute-start(bf16[64,128]{1,0:T(8,128)(2,1)S(1)} %reduce.1), channel_id=1, source_target_pairs={{0,1},{1,0},{2,3},{3,2},{4,5},{5,4},{6,7},{7,6},{8,9},{9,8},{10,11... | collective-permute-start | bytes 49160 | tf_op jit(solution)/shard_map/ppermute | solution.py:349
  53.4 28.7 %collective-permute-start.4 = (bf16[32,128]{1,0:T(8,128)(2,1)S(1)}, bf16[32,128]{1,0:T(8,128)(2,1)S(1)}, u32[]{:S(2)}, u32[]{:S(2)}) collective-permute-start(bf16[32,128]{1,0:T(8,128)(2,1)S(1)} %copy-done.9), channel_id=1, source_target_pairs={{0,1},{1,3},{2,5},{3,7},{4,9},{5,11},{6,13},{7,15},{8,0},{9,2},{10... | collective-permute-start | bytes 24584 | tf_op jit(solution)/shard_map/ppermute | solution.py:334
  58.9 23.2 %collective-permute-start.3 = (bf16[32,128]{1,0:T(8,128)(2,1)S(1)}, bf16[32,128]{1,0:T(8,128)(2,1)S(1)}, u32[]{:S(2)}, u32[]{:S(2)}) collective-permute-start(bf16[32,128]{1,0:T(8,128)(2,1)S(1)} %copy-done.9), channel_id=1, source_target_pairs={{0,0},{1,2},{2,4},{3,6},{4,8},{5,10},{6,12},{7,14},{8,1},{9,3},{10... | collective-permute-start | bytes 24584 | tf_op jit(solution)/shard_map/ppermute | solution.py:334

commit v10 on v9

--- a/solution.py
+++ b/solution.py
@@ -228,7 +228,7 @@
     stats[...] = jnp.where(lane == 0, highest, jnp.where(lane == 1, total, landed))
 
 
-def finish(masked, received, queries, first, second, result, stats, logprob, attended, values, sems):
+def finish(masked, received, queries, first, second, result, stats, logprob, attended, values, rows, sems):
     lines = received[:, 8, :].astype(F32)
     take = lambda k: lines[:, 32 * k : 32 * (k + 1)]
     peak, total = take(0), take(1) + take(2) + take(3)
@@ -261,7 +261,10 @@
     share, own_share = jnp.exp(top - highest), jnp.exp(own - highest)
     scale = 1.0 / (total * share + own_share)
     merged = ((live * share + own_value * own_share) * scale).astype(BF16)
-    copies = []
+    for i in range(4):
+        rows[:, HD * i : HD * (i + 1)] = merged[32 * i : 32 * (i + 1)]
+    copies = [pltpu.make_async_copy(rows, attended, sems.at[4])]
+    copies[0].start()
     for b in range(4):
         at = slice(BLK * b, BLK * (b + 1))
         section = masked[:, at].astype(F32)
@@ -271,8 +274,6 @@
             pltpu.make_async_copy(values.at[:, piece], logprob.at[:, piece], sems.at[b])
         )
         copies[-1].start()
-    for i in range(4):
-        attended[:, HD * i : HD * (i + 1)] = merged[32 * i : 32 * (i + 1)]
     for copy in copies:
         copy.wait()
 
@@ -309,7 +310,6 @@
         out_specs=[vmem] * 4,
         scratch_shapes=[pltpu.SemaphoreType.DMA((4,))],
         name="cut",
-        cost_estimate=pl.CostEstimate(flops=2000000000, bytes_accessed=1000, transcendentals=0),
     )(pltpu.with_memory_space_constraint(hidden, pltpu.HBM)))
     for k in (1, 3, 2):
         shares[k] = lax.ppermute(shares[k], "x", [(0, k)])
@@ -319,6 +319,9 @@
         in_specs=[vmem],
         out_specs=vmem,
         name="pack",
+        cost_estimate=pl.CostEstimate(
+            flops=2000000000, bytes_accessed=1000, transcendentals=0
+        ),
     )(*held(queries))
     projected = kernel(
         project,
@@ -365,10 +368,14 @@
     )(*held(around, queries, prompt_lengths, owner_step))
     logprob, attended = kernel(
         finish,
-        out_shape=[pltpu.HBM(logits.shape, F32), sent(queries.shape, BF16)],
+        out_shape=[pltpu.HBM(logits.shape, F32), pltpu.HBM(queries.shape, BF16)],
         in_specs=[vmem] * 7,
-        out_specs=[hbm, vmem],
-        scratch_shapes=[pltpu.VMEM(logits.shape, F32), pltpu.SemaphoreType.DMA((4,))],
+        out_specs=[hbm, hbm],
+        scratch_shapes=[
+            pltpu.VMEM(logits.shape, F32),
+            pltpu.VMEM(queries.shape, BF16),
+            pltpu.SemaphoreType.DMA((5,)),
+        ],
         name="finish",
     )(*held(masked, answers, queries, *renewed, result, stats))
     return attended, logprob

time: 84.6 us -> 84 us (level)
  waiting for transfers between devices: 20.7 us -> 19.8 us
    ppermute x3, waiting for transfers between devices: 3.36 us -> 2.41 us  [per_device(): shares[k] = lax.ppermute(shares[k], 'x', [(0, k)])]
where the time goes in v10:
time: 84 us; the launch traced here: 83.5 us
  starting transfers between devices  39.5 us (47%)
  waiting for transfers between devices  19.8 us (24%)
  blocking collectives  15.6 us (19%)
  Pallas kernels  6.87 us (8%)
  between operations  0.87 us (1%)
    all_to_all x2, starting transfers between devices, exchanged(): return lax.all_to_all(slots, axis, 0, 0, tiled=True)  20.6 us
    all_to_all x2, waiting for transfers between devices, exchanged(): return lax.all_to_all(slots, axis, 0, 0, tiled=True)  17.3 us
    all_gather x1, blocking collectives, per_device(): around = lax.all_gather(both, 'x')  15.6 us
    ppermute x2, starting transfers between devices, per_device(): lax.ppermute(fresh, TP, route)  12.8 us
    ppermute x1, starting transfers between devices, per_device(): other = lax.ppermute(block, 'zl', [(0, 1), (1, 0)])  3.37 us
    ppermute x3, starting transfers between devices, per_device(): shares[k] = lax.ppermute(shares[k], 'x', [(0, k)])  2.75 us
    ppermute x3, waiting for transfers between devices, per_device(): shares[k] = lax.ppermute(shares[k], 'x', [(0, k)])  2.41 us
  transfers between devices with their start and end apart: 8, of which 2 were waited for; matrix products, arithmetic and copies ran while one was open for 0% of the time, Pallas kernels for 2%

profile of v10, /device:TPU:90, one launch (start us, length us, event | category | flops | bytes accessed | tf_op | source)
XLA Modules:
  0.0 83.5 jit_solution(1754500788712623445)
XLA Ops:
  0.6 1.0 %cut.1 = (bf16[64,512]{1,0:T(8,128)(2,1)S(1)}, bf16[64,512]{1,0:T(8,128)(2,1)S(1)}, bf16[64,512]{1,0:T(8,128)(2,1)S(1)}, bf16[64,512]{1,0:T(8,128)(2,1)S(1)}) custom-call(bf16[256,512]{1,0:T(8,128)(2,1)} %hidden.1), custom_call_target="tpu_custom_call" | custom-call | tf_op jit(solution)/shard_map/cut/pallas_call | solution.py:306
  1.6 1.3 %collective-permute-start = (bf16[64,512]{1,0:T(8,128)(2,1)S(1)}, bf16[64,512]{1,0:T(8,128)(2,1)S(1)}, u32[]{:S(2)}, u32[]{:S(2)}) collective-permute-start(bf16[64,512]{1,0:T(8,128)(2,1)S(1)} %get-tuple-element.14), channel_id=1, source_target_pairs={{0,128},{1,129},{2,130},{3,131},{4,132},{5,133},{6,134},{7,135},{8... | collective-permute-start | bytes 196616 | tf_op jit(solution)/shard_map/ppermute | solution.py:315
  2.9 0.7 collective-permute-start.1
  3.6 0.0 copy-start
  3.6 0.8 collective-permute-start.2
  4.4 0.0 copy-start.3
  4.4 0.7 copy-done.3
  5.2 0.1 pack.1.asked
  5.3 0.0 copy-start.2
  5.3 0.0 copy-start.5
  5.3 0.0 copy-start.9
  5.3 0.0 copy-start.1
  5.4 0.0 copy-start.8
  5.4 2.4 %collective-permute-done.first = bf16[64,512]{1,0:T(8,128)(2,1)S(1)} collective-permute-done((bf16[64,512]{1,0:T(8,128)(2,1)S(1)}, bf16[64,512]{1,0:T(8,128)(2,1)S(1)}, u32[]{:S(2)}, u32[]{:S(2)}) %collective-permute-start) | collective-permute-done | bytes 65568 | tf_op jit(solution)/shard_map/ppermute | solution.py:315
  7.8 0.0 collective-permute-done.1.second
  7.8 0.0 collective-permute-done.2.third
  7.8 0.0 copy-done
  7.8 1.2 %project.1 = bf16[16,72,128]{2,1,0:T(8,128)(2,1)} custom-call(bf16[64,512]{1,0:T(8,128)(2,1)S(1)} %get-tuple-element.13.own, bf16[64,512]{1,0:T(8,128)(2,1)S(1)} %collective-permute-done.first, bf16[64,512]{1,0:T(8,128)(2,1)S(1)} %collective-permute-done.1.second, bf16[64,512]{1,0:T(8,128)(2,1)S(1)} %collective-permute-done.2.third, ...), custom_call_target="tpu_custom_call" | custom-call | tf_op jit(solution)/shard_map/project/pallas_call | solution.py:326
  9.0 0.0 copy-start.10
  9.0 0.0 copy-start.4
  9.0 0.0 copy-start.6
  9.0 0.0 copy-start.7
  9.0 14.9 %all-to-all-start = ((bf16[16,72,128]{2,1,0:T(8,128)(2,1)}), bf16[16,72,128]{2,1,0:T(8,128)(2,1)S(1)}, u32[]{:S(2)}, u32[]{:S(2)}) async-start(bf16[16,72,128]{2,1,0:T(8,128)(2,1)} %project.1), calls=%async_computation | async-start | bytes 589824 | tf_op jit(solution)/shard_map/all_to_all | solution.py:282
  23.9 0.0 copy-done.2
  23.9 0.0 copy-done.5
  23.9 0.0 copy-done.9
  23.9 1.3 %grammar.1 = (bf16[32,7680]{1,0:T(8,128)(2,1)S(1)}, bf16[16,128]{1,0:T(8,128)(2,1)S(1)}) custom-call(bf16[32,7680]{1,0:T(8,128)(2,1)S(1)} %copy-done.2, s32[1,32]{1,0:T(1,128)S(1)} %bitcast.5, s32[24,256]{1,0:T(8,128)S(1)} %copy-done.5), custom_call_target="tpu_custom_call" | custom-call | tf_op jit(solution)/shard_map/grammar/pallas_call | solution.py:338
  25.2 17.3 %all-to-all-done.received.pieces = bf16[16,72,128]{2,1,0:T(8,128)(2,1)S(1)} async-done(((bf16[16,72,128]{2,1,0:T(8,128)(2,1)}), bf16[16,72,128]{2,1,0:T(8,128)(2,1)S(1)}, u32[]{:S(2)}, u32[]{:S(2)}) %all-to-all-start) | async-done | bytes 294944 | tf_op jit(solution)/shard_map/all_to_all | solution.py:282
  42.6 0.0 copy-done.1
  42.6 0.0 copy-done.8
  42.6 1.3 %cached.1 = bf16[16,16,128]{2,1,0:T(8,128)(2,1)} custom-call(s32[1,2]{1,0:T(1,128)S(1)} %bitcast.4, bf16[16,72,128]{2,1,0:T(8,128)(2,1)S(1)} %all-to-all-done.received.pieces, bf16[2,128,2048]{2,1,0:T(8,128)(2,1)S(1)} %copy-done.1, bf16[16,128]{1,0:T(8,128)(2,1)S(1)} %get-tuple-element.17.terms), custom_call_target="tpu_custom_call" | custom-call | tf_op jit(solution)/shard_map/cached/pallas_call | solution.py:353
  43.9 5.7 %all-to-all-start.1 = ((bf16[16,16,128]{2,1,0:T(8,128)(2,1)}), bf16[16,16,128]{2,1,0:T(8,128)(2,1)S(1)}, u32[]{:S(2)}, u32[]{:S(2)}) async-start(bf16[16,16,128]{2,1,0:T(8,128)(2,1)} %cached.1), calls=%async_computation.1 | async-start | bytes 131072 | tf_op jit(solution)/shard_map/all_to_all | solution.py:282
  49.7 3.4 %collective-permute-start.5 = (bf16[64,128]{1,0:T(8,128)(2,1)S(1)}, bf16[64,128]{1,0:T(8,128)(2,1)S(1)}, u32[]{:S(2)}, u32[]{:S(2)}) collective-permute-start(bf16[64,128]{1,0:T(8,128)(2,1)S(1)} %reduce.1), channel_id=1, source_target_pairs={{0,1},{1,0},{2,3},{3,2},{4,5},{5,4},{6,7},{7,6},{8,9},{9,8},{10,11... | collective-permute-start | bytes 49160 | tf_op jit(solution)/shard_map/ppermute | solution.py:352
  53.0 0.0 copy-done.10
  53.1 5.5 %collective-permute-start.4 = (bf16[32,128]{1,0:T(8,128)(2,1)S(1)}, bf16[32,128]{1,0:T(8,128)(2,1)S(1)}, u32[]{:S(2)}, u32[]{:S(2)}) collective-permute-start(bf16[32,128]{1,0:T(8,128)(2,1)S(1)} %copy-done.10), channel_id=1, source_target_pairs={{0,1},{1,3},{2,5},{3,7},{4,9},{5,11},{6,13},{7,15},{8,0},{9,2},{10... | collective-permute-start | bytes 24584 | tf_op jit(solution)/shard_map/ppermute | solution.py:337
  58.5 7.3 %collective-permute-start.3 = (bf16[32,128]{1,0:T(8,128)(2,1)S(1)}, bf16[32,128]{1,0:T(8,128)(2,1)S(1)}, u32[]{:S(2)}, u32[]{:S(2)}) collective-permute-start(bf16[32,128]{1,0:T(8,128)(2,1)S(1)} %copy-done.10), channel_id=1, source_target_pairs={{0,0},{1,2},{2,4},{3,6},{4,8},{5,10},{6,12},{7,14},{8,1},{9,3},{10... | collective-permute-start | bytes 24584 | tf_op jit(solution)/shard_map/ppermute | solution.py:337
  65.8 0.0 collective-permute-done.5
  65.9 15.6 %all-gather = bf16[512,128]{1,0:T(8,128)(2,1)S(1)} all-gather(bf16[128,128]{1,0:T(8,128)(2,1)S(1)} %pad_maximum_fusion), channel_id=2, replica_groups=mesh['x'=4,'c8'=8,'zh'=8,'zl'=2] {'x'}, dimensions={0}, use_global_device_ids=true | all-gather | bytes 163840 | tf_op jit(solution)/shard_map/all_gather | solution.py:361
  81.5 0.0 copy-done.4
  81.5 0.0 copy-done.6
  81.5 0.0 copy-done.7
  81.5 0.4 prompts.1
  81.9 0.0 collective-permute-done.4.second
  81.9 0.0 collective-permute-done.3.first
  82.0 0.0 all-to-all-done.1.received
  82.0 1.5 %finish.1 = (f32[32,7680]{1,0:T(8,128)}, bf16[32,512]{1,0:T(8,128)(2,1)}) custom-call(bf16[32,7680]{1,0:T(8,128)(2,1)S(1)} %get-tuple-element.12.masked, bf16[16,16,128]{2,1,0:T(8,128)(2,1)S(1)} %all-to-all-done.1.received, bf16[32,512]{1,0:T(8,128)(2,1)S(1)} %copy-done.4, bf16[32,128]{1,0:T(8,128)(2,1)S(1)} %collective-permute-done.3.first, ...), custom_call_target="tpu_custom_call" | custom-call | tf_op jit(solution)/shard_map/finish/pallas_call | solution.py:369
  (2 shorter events, 0.0 us)
Async XLA Ops:
  1.6 6.2 %collective-permute-start = (bf16[64,512]{1,0:T(8,128)(2,1)S(1)}, bf16[64,512]{1,0:T(8,128)(2,1)S(1)}, u32[]{:S(2)}, u32[]{:S(2)}) collective-permute-start(bf16[64,512]{1,0:T(8,128)(2,1)S(1)} %get-tuple-element.14), channel_id=1, source_target_pairs={{0,128},{1,129},{2,130},{3,131},{4,132},{5,133},{6,134},{7,135},{8... | collective-permute-start | bytes 196616 | tf_op jit(solution)/shard_map/ppermute | solution.py:315
  2.9 4.9 %collective-permute-start.1 = (bf16[64,512]{1,0:T(8,128)(2,1)S(1)}, bf16[64,512]{1,0:T(8,128)(2,1)S(1)}, u32[]{:S(2)}, u32[]{:S(2)}) collective-permute-start(bf16[64,512]{1,0:T(8,128)(2,1)S(1)} %get-tuple-element.15), channel_id=1, source_target_pairs={{0,256},{1,257},{2,258},{3,259},{4,260},{5,261},{6,262},{7,263},{8... | collective-permute-start | bytes 196616 | tf_op jit(solution)/shard_map/ppermute | solution.py:315
  3.6 4.2 %copy-start = (bf16[512,2048]{1,0:T(8,128)(2,1)S(1)}, bf16[512,2048]{1,0:T(8,128)(2,1)}, u32[]{:S(2)}) copy-start(bf16[512,2048]{1,0:T(8,128)(2,1)} %weight.1) | copy-start | bytes 6291460
  3.6 4.2 %collective-permute-start.2 = (bf16[64,512]{1,0:T(8,128)(2,1)S(1)}, bf16[64,512]{1,0:T(8,128)(2,1)S(1)}, u32[]{:S(2)}, u32[]{:S(2)}) collective-permute-start(bf16[64,512]{1,0:T(8,128)(2,1)S(1)} %get-tuple-element.16), channel_id=1, source_target_pairs={{0,384},{1,385},{2,386},{3,387},{4,388},{5,389},{6,390},{7,391},{8... | collective-permute-start | bytes 196616 | tf_op jit(solution)/shard_map/ppermute | solution.py:315
  4.4 0.8 copy-start.3
  5.3 18.6 %copy-start.2 = (bf16[32,7680]{1,0:T(8,128)(2,1)S(1)}, bf16[32,7680]{1,0:T(8,128)(2,1)}, u32[]{:S(2)}) copy-start(bf16[32,7680]{1,0:T(8,128)(2,1)} %logits.1) | copy-start | bytes 1474564
  5.3 18.6 %copy-start.5 = (s32[24,256]{1,0:T(8,128)S(1)}, s32[24,256]{1,0:T(8,128)}, u32[]{:S(2)}) copy-start(s32[24,256]{1,0:T(8,128)} %masks.1) | copy-start | bytes 73732
  5.3 18.6 %copy-start.9 = (s32[32]{0:T(128)S(1)}, s32[32]{0:T(128)}, u32[]{:S(2)}) copy-start(s32[32]{0:T(128)} %param.20) | copy-start | bytes 388
  5.3 37.2 %copy-start.1 = (bf16[2,128,2048]{2,1,0:T(8,128)(2,1)S(1)}, bf16[2,128,2048]{2,1,0:T(8,128)(2,1)}, u32[]{:S(2)}) copy-start(bf16[2,128,2048]{2,1,0:T(8,128)(2,1)} %cache.1) | copy-start | bytes 3145732
  5.4 37.2 %copy-start.8 = (s32[2]{0:T(128)S(1)}, s32[2]{0:T(128)}, u32[]{:S(2)}) copy-start(s32[2]{0:T(128)} %param.16) | copy-start | bytes 28
  9.0 44.1 %copy-start.10 = (bf16[32,128]{1,0:T(8,128)(2,1)S(1)}, bf16[32,128]{1,0:T(8,128)(2,1)}, u32[]{:S(2)}) copy-start(bf16[32,128]{1,0:T(8,128)(2,1)} %param.18) | copy-start | bytes 24580
  9.0 72.5 %copy-start.4 = (bf16[32,512]{1,0:T(8,128)(2,1)S(1)}, bf16[32,512]{1,0:T(8,128)(2,1)}, u32[]{:S(2)}) copy-start(bf16[32,512]{1,0:T(8,128)(2,1)} %queries.5) | copy-start | bytes 98308
  9.0 72.5 %copy-start.6 = (s32[8,16]{1,0:T(8,128)S(1)}, s32[8,16]{1,0:T(8,128)}, u32[]{:S(2)}) copy-start(s32[8,16]{1,0:T(8,128)} %lengths.1) | copy-start | bytes 1540
  9.0 72.5 %copy-start.7 = (s32[8,16]{1,0:T(8,128)S(1)}, s32[8,16]{1,0:T(8,128)}, u32[]{:S(2)}) copy-start(s32[8,16]{1,0:T(8,128)} %owners.1) | copy-start | bytes 1540
  9.0 33.6 %all-to-all-start = ((bf16[16,72,128]{2,1,0:T(8,128)(2,1)}), bf16[16,72,128]{2,1,0:T(8,128)(2,1)S(1)}, u32[]{:S(2)}, u32[]{:S(2)}) async-start(bf16[16,72,128]{2,1,0:T(8,128)(2,1)} %project.1), calls=%async_computation | async-start | bytes 589824 | tf_op jit(solution)/shard_map/all_to_all | solution.py:282
  43.9 38.1 %all-to-all-start.1 = ((bf16[16,16,128]{2,1,0:T(8,128)(2,1)}), bf16[16,16,128]{2,1,0:T(8,128)(2,1)S(1)}, u32[]{:S(2)}, u32[]{:S(2)}) async-start(bf16[16,16,128]{2,1,0:T(8,128)(2,1)} %cached.1), calls=%async_computation.1 | async-start | bytes 131072 | tf_op jit(solution)/shard_map/all_to_all | solution.py:282
  49.7 16.2 %collective-permute-start.5 = (bf16[64,128]{1,0:T(8,128)(2,1)S(1)}, bf16[64,128]{1,0:T(8,128)(2,1)S(1)}, u32[]{:S(2)}, u32[]{:S(2)}) collective-permute-start(bf16[64,128]{1,0:T(8,128)(2,1)S(1)} %reduce.1), channel_id=1, source_target_pairs={{0,1},{1,0},{2,3},{3,2},{4,5},{5,4},{6,7},{7,6},{8,9},{9,8},{10,11... | collective-permute-start | bytes 49160 | tf_op jit(solution)/shard_map/ppermute | solution.py:352
  53.1 28.9 %collective-permute-start.4 = (bf16[32,128]{1,0:T(8,128)(2,1)S(1)}, bf16[32,128]{1,0:T(8,128)(2,1)S(1)}, u32[]{:S(2)}, u32[]{:S(2)}) collective-permute-start(bf16[32,128]{1,0:T(8,128)(2,1)S(1)} %copy-done.10), channel_id=1, source_target_pairs={{0,1},{1,3},{2,5},{3,7},{4,9},{5,11},{6,13},{7,15},{8,0},{9,2},{10... | collective-permute-start | bytes 24584 | tf_op jit(solution)/shard_map/ppermute | solution.py:337
  58.5 23.4 %collective-permute-start.3 = (bf16[32,128]{1,0:T(8,128)(2,1)S(1)}, bf16[32,128]{1,0:T(8,128)(2,1)S(1)}, u32[]{:S(2)}, u32[]{:S(2)}) collective-permute-start(bf16[32,128]{1,0:T(8,128)(2,1)S(1)} %copy-done.10), channel_id=1, source_target_pairs={{0,0},{1,2},{2,4},{3,6},{4,8},{5,10},{6,12},{7,14},{8,1},{9,3},{10... | collective-permute-start | bytes 24584 | tf_op jit(solution)/shard_map/ppermute | solution.py:337
